TPU v7x, 256 devices: a whole 4x4x8 slice. The times are simulated.
256 devices in a mesh: gx: 16 (over x, y), gy: 8 (over z), gz: 2 (over core).
Axes of the slice: x: 4, y: 4, z: 8, core: 2. Of those that a mesh axis runs over, the one named last changes fastest.
Arguments:
- membrane: float32 [256, 128, 512], P('gx', 'gy', 'gz'), may hold values from 0 to 0.95
- recovery: float32 [256, 128, 512], P('gx', 'gy', 'gz'), may hold values from 0 to 2
- extracellular: float32 [256, 128, 512], P('gx', 'gy', 'gz'), may hold values from -6 to 6
- fiber_scale: float32 [256, 128, 512], P('gx', 'gy', 'gz'), may hold values from 0.5 to 2
- labels: int32 [32, 16, 64], P('gx', 'gy', 'gz'), may hold values from 0 to 2
Outputs:
- membrane_next: float32 [256, 128, 512], P('gx', 'gy', 'gz')
- recovery_next: float32 [256, 128, 512], P('gx', 'gy', 'gz')
- extracellular_next: float32 [256, 128, 512], P('gx', 'gy', 'gz')
All inputs are finite; a program needn't handle non-finite values.
Results may differ from a plain program's by a relative error of at most 0.0003.
Values sent between devices are 32-bit elements; how exact they have to be, the bound alone decides.
No kernel may reach another device: no remote copies, remote signals or barrier semaphores. Data moves between devices by JAX's collectives and lax.ppermute only.
A program may use at most 128 MiB of HBM per device.

v0:
```python
import jax
import jax.numpy as jnp
from jax import lax
from jax.sharding import PartitionSpec as P

LEVELS = 4
SMOOTH_SWEEPS = 1
COARSE_SWEEPS = 8


TIME_STEP = 0.05
ionic_gain = 8.0
ionic_onset = 0.15
recovery_rate = 0.01
DIRECTIONS = ((0, -1), (0, 1), (1, -1), (1, 1), (2, -1), (2, 1))


def extended(shard, sides, width):
    edges = {}
    for axis, dim in sides:
        peers, length = (lax.axis_size(axis), shard.shape[dim])
        up = [(i, (i + 1) % peers) for i in range(peers - 1)]
        last = lax.slice_in_dim(shard, length - width, length, axis=dim)
        first = lax.slice_in_dim(shard, 0, width, axis=dim)
        edges[dim] = (
            lax.ppermute(last, axis, up),
            lax.ppermute(first, axis, [(b, a) for a, b in up]),
        )
    done = []
    for _, dim in sides:
        low, high = edges[dim]
        around = [(width, width) if d in done else (0, 0) for d in range(shard.ndim)]
        shard = jnp.concatenate([jnp.pad(low, around), shard, jnp.pad(high, around)], axis=dim)
        done.append(dim)
    return shard


def lookup(labels):
    inner = jnp.where(labels == 1, 1.0, jnp.where(labels == 2, 0.3, 0.0)).astype(jnp.float32)
    outer = jnp.where(labels == 0, 3.0, 1.0).astype(jnp.float32)
    return (inner, outer)


def expand(blocks, factor):
    sa, sb, sc = blocks.shape
    big = jnp.broadcast_to(blocks[:, None, :, None, :, None], (sa, factor, sb, factor, sc, factor))
    return big.reshape(sa * factor, sb * factor, sc * factor)


def restrict(values):
    shape = values.shape
    lead = shape[:-3]
    folded = values.reshape(lead + (shape[-3] // 2, 2, shape[-2] // 2, 2, shape[-1] // 2, 2))
    return jnp.mean(folded, axis=(-5, -3, -1))


def neighbour(padded, axis_index, side):
    pieces = [
        slice(1, padded.shape[0] - 1),
        slice(1, padded.shape[1] - 1),
        slice(1, padded.shape[2] - 1),
    ]
    pieces[axis_index] = slice(1 + side, padded.shape[axis_index] - 1 + side)
    return padded[tuple(pieces)]


def widen(field):
    return jnp.pad(field, 1)


def rims(field):
    return extended(field, (("gx", 0), ("gy", 1), ("gz", 2)), 1)


def coef_rims(coef):
    return extended(coef, (("gx", 1), ("gy", 2), ("gz", 3)), 1)


def couplings(pcoef):
    centre_in = neighbour(pcoef[0], 0, 0)
    centre_out = neighbour(pcoef[1], 0, 0)
    result = []
    for axis_index, side in DIRECTIONS:
        result.append(
            jnp.minimum(centre_in, neighbour(pcoef[0], axis_index, side))
            + 0.5 * (centre_out + neighbour(pcoef[1], axis_index, side))
        )
    return result


def offdiag(padded_field, coupling):
    total = jnp.zeros(coupling[0].shape, jnp.float32)
    for index, (axis_index, side) in enumerate(DIRECTIONS):
        total = total + coupling[index] * neighbour(padded_field, axis_index, side)
    return total


def intra(padded_field, pcoef):
    centre_in = neighbour(pcoef[0], 0, 0)
    centre_val = neighbour(padded_field, 0, 0)
    total = jnp.zeros(centre_val.shape, jnp.float32)
    for axis_index, side in DIRECTIONS:
        weight = jnp.minimum(centre_in, neighbour(pcoef[0], axis_index, side))
        total = total + weight * (neighbour(padded_field, axis_index, side) - centre_val)
    return total


def parity_of(shape):
    total = lax.broadcasted_iota(jnp.int32, shape, 0) + lax.broadcasted_iota(jnp.int32, shape, 1)
    total = total + lax.broadcasted_iota(jnp.int32, shape, 2)
    return total % 2


def sweeps(field, rhs, coupling, diagonal, parity, count, extend):
    for sweep_index in range(count):
        for colour in (0, 1):
            updated = (rhs + offdiag(extend(field), coupling)) / diagonal
            field = jnp.where(parity == colour, updated, field)
    return field


def coarse_solve(rhs, coef):
    stacked = jnp.concatenate([rhs[None], coef], axis=0)[None]
    whole = lax.all_gather(stacked, ("gx", "gy", "gz"), axis=0, tiled=True)
    count_x, count_y, count_z = (lax.axis_size("gx"), lax.axis_size("gy"), lax.axis_size("gz"))
    depth, rows_x, rows_y, rows_z = stacked.shape[1:]
    grid = whole.reshape(count_x, count_y, count_z, depth, rows_x, rows_y, rows_z)
    grid = grid.transpose(3, 0, 4, 1, 5, 2, 6).reshape(
        depth, count_x * rows_x, count_y * rows_y, count_z * rows_z
    )
    grid_rhs = grid[0]
    grid_coef = jnp.pad(grid[1:], ((0, 0), (1, 1), (1, 1), (1, 1)))
    coupling = couplings(grid_coef)
    diagonal = sum(coupling)
    solved = sweeps(
        jnp.zeros_like(grid_rhs),
        grid_rhs,
        coupling,
        diagonal,
        parity_of(grid_rhs.shape),
        COARSE_SWEEPS,
        widen,
    )
    start = (
        lax.axis_index("gx") * rows_x,
        lax.axis_index("gy") * rows_y,
        lax.axis_index("gz") * rows_z,
    )
    return lax.dynamic_slice(solved, start, rhs.shape)


def cycle(level_index, field, rhs, padded_coefs, coarse_coef):
    if level_index == LEVELS - 1:
        return coarse_solve(rhs, coarse_coef)
    coupling = couplings(padded_coefs[level_index])
    diagonal = sum(coupling)
    parity = parity_of(rhs.shape)
    field = sweeps(field, rhs, coupling, diagonal, parity, SMOOTH_SWEEPS, rims)
    remainder = rhs - (diagonal * field - offdiag(rims(field), coupling))
    coarse_rhs = 4.0 * restrict(remainder)
    correction = cycle(
        level_index + 1, jnp.zeros_like(coarse_rhs), coarse_rhs, padded_coefs, coarse_coef
    )
    field = field + expand(correction, 2)
    return sweeps(field, rhs, coupling, diagonal, parity, SMOOTH_SWEEPS, rims)


def on_device(membrane, recovery, extracellular, fiber_scale, labels):
    lab_in, lab_out = lookup(labels)
    tissue = (expand(labels, 8) != 0).astype(jnp.float32)
    inner = expand(lab_in, 8) * fiber_scale
    outer = expand(lab_out, 8)
    plain_coefs = [jnp.stack([inner, outer])]
    for level_index in range(1, LEVELS):
        plain_coefs.append(restrict(plain_coefs[-1]))
    padded_coefs = []
    for level_index in range(LEVELS - 1):
        padded_coefs.append(coef_rims(plain_coefs[level_index]))
    drive = intra(rims(membrane + extracellular), padded_coefs[0])
    ionic = (
        ionic_gain * membrane * (membrane - ionic_onset) * (membrane - 1.0) + membrane * recovery
    )
    membrane_next = membrane + TIME_STEP * (drive - tissue * ionic)
    recovery_next = recovery + TIME_STEP * recovery_rate * (
        -recovery - ionic_gain * membrane * (membrane - ionic_onset - 1.0)
    )
    rhs = intra(rims(membrane_next), padded_coefs[0])
    extracellular_next = cycle(0, extracellular, rhs, padded_coefs, plain_coefs[LEVELS - 1])
    return (membrane_next, recovery_next, extracellular_next)


def solution(mesh):
    placed = (
        P("gx", "gy", "gz"),
        P("gx", "gy", "gz"),
        P("gx", "gy", "gz"),
        P("gx", "gy", "gz"),
        P("gx", "gy", "gz"),
    )
    return jax.shard_map(
        on_device,
        mesh=mesh,
        in_specs=placed,
        out_specs=(P("gx", "gy", "gz"), P("gx", "gy", "gz"), P("gx", "gy", "gz")),
        check_vma=False,
    )
```

profile of v0, /device:TPU:131, one launch (start us, length us, event | category | flops | bytes accessed | tf_op | source)
XLA Modules:
  0.0 596.0 jit_solution(10458067483653969350)
XLA Ops:
  8.0 18.1 %stack.12 = f32[1,8,2,8,2,128,2]{6,5,4,3,2,1,0:T(8,128)} reshape(f32[16,16,256]{2,1,0:T(8,128)S(1)} %mul.746) | data formatting | bytes 524288 | tf_op jit(solution)/shard_map/stack | solution.py:173
  26.2 10.0 %copy.10 = f32[1,8,2,8,2,128,2]{5,3,6,4,2,1,0:T(8,128)S(1)} copy(f32[1,8,2,8,2,128,2]{6,5,4,3,2,1,0:T(8,128)} %stack.12) | data formatting | bytes 524288 | tf_op jit(solution)/shard_map/stack | solution.py:173
  37.1 5.6 div.118
  84.2 5.6 collective-permute-start.65
  132.8 5.6 collective-permute-start.7
  180.2 5.5 collective-permute-start.39
  204.7 5.5 collective-permute-start.25
  224.4 6.0 %collective-permute-start.31 = (f32[1,16,256]{2,1,0:T(8,128)S(1)}, f32[1,16,256]{2,1,0:T(8,128)S(1)}, u32[]{:S(2)}, u32[]{:S(2)}) collective-permute-start(f32[1,16,256]{2,1,0:T(8,128)S(1)} %get-tuple-element.63), channel_id=1, source_target_pairs={{16,0},{32,16},{48,32},{64,48},{80,64},{96,80},{112,96},{128,112},... | collective-permute-start | bytes 49160 | tf_op jit(solution)/shard_map/ppermute | solution.py:27
  236.8 5.5 collective-permute-start.43
  242.7 18.1 %reshape.67 = f32[8,2,8,2,128,2]{5,4,3,2,1,0:T(8,128)} reshape(f32[16,16,256]{2,1,0:T(8,128)S(1)} %fusion.278) | data formatting | bytes 524288 | tf_op jit(solution)/shard_map/reshape | solution.py:53
  260.8 7.0 %reduce_sum.54 = f32[8,8,128]{2,1,0:T(8,128)S(1)} reduce(f32[8,2,8,2,128,2]{5,4,3,2,1,0:T(8,128)} %reshape.67, f32[]{:T(128)} %constant.47.clone.1), dimensions={1,3,5}, to_apply=%region_0.1 | reduce | flops 57344 | bytes 294916 | tf_op jit(solution)/shard_map/reduce_sum | solution.py:54
  281.0 5.5 collective-permute-start.49
  295.8 5.7 collective-permute-start.55
  315.4 5.5 collective-permute-start.67
  334.9 5.5 collective-permute-start.73
  354.2 5.5 collective-permute-start.79
  365.8 72.7 %all-gather = f32[768,2,2,32]{3,2,1,0:T(2,128)S(1)} all-gather(f32[3,2,2,32]{3,2,1,0:T(2,128)S(1)} %pad_maximum_fusion.261), channel_id=2, replica_groups=mesh['gx'=16,'gy'=8,'gz'=2] {'gx','gy','gz'}, dimensions={0}, use_global_device_ids=true | all-gather | bytes 394752 | tf_op jit(solution)/shard_map/all_gather | solution.py:124
  460.8 5.5 collective-permute-start.85
  480.2 5.5 collective-permute-start.91
  502.7 5.5 collective-permute-start.97
  535.2 6.5 %broadcast_in_dim.87 = f32[8,2,8,2,128,2]{5,4,3,2,1,0:T(8,128)} broadcast(f32[8,8,128]{2,1,0:T(8,128)S(1)} %fusion.403), dimensions={0,2,4} | broadcast | bytes 294912 | tf_op jit(solution)/shard_map/broadcast_in_dim | solution.py:46
  541.8 12.7 %reshape.73 = f32[16,16,256]{2,1,0:T(8,128)S(1)} reshape(f32[8,2,8,2,128,2]{5,4,3,2,1,0:T(8,128)} %broadcast_in_dim.87) | data formatting | bytes 524288 | tf_op jit(solution)/shard_map/reshape | solution.py:47
  563.2 5.5 collective-permute-start.109
  583.3 5.5 collective-permute-start.115
  (456 shorter events, 352.9 us)
Async XLA Ops:
  45.3 30.7 %collective-permute-start.60 = (f32[2,4,4,1]{3,2,1,0:T(4,128)S(1)}, f32[2,4,4,1]{3,2,1,0:T(4,128)S(1)}, u32[]{:S(2)}, u32[]{:S(2)}) collective-permute-start(f32[2,4,4,1]{3,2,1,0:T(4,128)S(1)} %get-tuple-element.127), channel_id=1, source_target_pairs={{0,1},{2,3},{4,5},{6,7},{8,9},{10,11},{12,13},{14,15},{16,17},{18,... | collective-permute-start | bytes 392 | tf_op jit(solution)/shard_map/ppermute | solution.py:26
  46.6 46.3 %collective-permute-start.61 = (f32[2,4,1,64]{3,2,1,0:T(1,128)S(1)}, f32[2,4,1,64]{3,2,1,0:T(1,128)S(1)}, u32[]{:S(2)}, u32[]{:S(2)}) collective-permute-start(f32[2,4,1,64]{3,2,1,0:T(1,128)S(1)} %get-tuple-element.129), channel_id=1, source_target_pairs={{0,2},{2,4},{4,6},{6,8},{8,10},{10,12},{12,14},{1,3},{3,5},{5,7},{... | collective-permute-start | bytes 6152 | tf_op jit(solution)/shard_map/ppermute | solution.py:26
  49.3 48.2 %collective-permute-start.62 = (f32[2,1,4,64]{3,2,1,0:T(4,128)S(1)}, f32[2,1,4,64]{3,2,1,0:T(4,128)S(1)}, u32[]{:S(2)}, u32[]{:S(2)}) collective-permute-start(f32[2,1,4,64]{3,2,1,0:T(4,128)S(1)} %get-tuple-element.125), channel_id=1, source_target_pairs={{0,16},{16,32},{32,48},{48,64},{64,80},{80,96},{96,112},{112,128},... | collective-permute-start | bytes 6152 | tf_op jit(solution)/shard_map/ppermute | solution.py:26
  52.5 46.3 %collective-permute-start.63 = (f32[2,1,4,64]{3,2,1,0:T(4,128)S(1)}, f32[2,1,4,64]{3,2,1,0:T(4,128)S(1)}, u32[]{:S(2)}, u32[]{:S(2)}) collective-permute-start(f32[2,1,4,64]{3,2,1,0:T(4,128)S(1)} %get-tuple-element.126), channel_id=1, source_target_pairs={{16,0},{32,16},{48,32},{64,48},{80,64},{96,80},{112,96},{128,112},... | collective-permute-start | bytes 6152 | tf_op jit(solution)/shard_map/ppermute | solution.py:27
  56.7 23.2 %collective-permute-start.68 = (f32[4,1,64]{2,1,0:T(1,128)S(1)}, f32[4,1,64]{2,1,0:T(1,128)S(1)}, u32[]{:S(2)}, u32[]{:S(2)}) collective-permute-start(f32[4,1,64]{2,1,0:T(1,128)S(1)} %broadcast.324), channel_id=1, source_target_pairs={{0,2},{2,4},{4,6},{6,8},{8,10},{10,12},{12,14},{1,3},{3,5},{5,7},{... | collective-permute-start | bytes 3080 | tf_op jit(solution)/shard_map/ppermute | solution.py:26
  76.0 25.8 %collective-permute-start.64 = (f32[2,4,1,64]{3,2,1,0:T(1,128)S(1)}, f32[2,4,1,64]{3,2,1,0:T(1,128)S(1)}, u32[]{:S(2)}, u32[]{:S(2)}) collective-permute-start(f32[2,4,1,64]{3,2,1,0:T(1,128)S(1)} %get-tuple-element.130), channel_id=1, source_target_pairs={{2,0},{4,2},{6,4},{8,6},{10,8},{12,10},{14,12},{3,1},{5,3},{7,5},{... | collective-permute-start | bytes 6152 | tf_op jit(solution)/shard_map/ppermute | solution.py:27
  98.8 20.1 %collective-permute-start.5 = (f32[2,16,16,1]{3,2,1,0:T(8,128)S(1)}, f32[2,16,16,1]{3,2,1,0:T(8,128)S(1)}, u32[]{:S(2)}, u32[]{:S(2)}) collective-permute-start(f32[2,16,16,1]{3,2,1,0:T(8,128)S(1)} %get-tuple-element.39), channel_id=1, source_target_pairs={{1,0},{3,2},{5,4},{7,6},{9,8},{11,10},{13,12},{15,14},{17,16},{19,... | collective-permute-start | bytes 6152 | tf_op jit(solution)/shard_map/ppermute | solution.py:27
  118.8 21.6 %collective-permute-start.10 = (f32[16,16,1]{2,1,0:T(8,128)S(1)}, f32[16,16,1]{2,1,0:T(8,128)S(1)}, u32[]{:S(2)}, u32[]{:S(2)}) collective-permute-start(f32[16,16,1]{2,1,0:T(8,128)S(1)} %get-tuple-element.87), channel_id=1, source_target_pairs={{0,1},{2,3},{4,5},{6,7},{8,9},{10,11},{12,13},{14,15},{16,17},{18,... | collective-permute-start | bytes 3080 | tf_op jit(solution)/shard_map/ppermute | solution.py:26
  120.2 21.6 %collective-permute-start.11 = (f32[16,16,1]{2,1,0:T(8,128)S(1)}, f32[16,16,1]{2,1,0:T(8,128)S(1)}, u32[]{:S(2)}, u32[]{:S(2)}) collective-permute-start(f32[16,16,1]{2,1,0:T(8,128)S(1)} %get-tuple-element.88), channel_id=1, source_target_pairs={{1,0},{3,2},{5,4},{7,6},{9,8},{11,10},{13,12},{15,14},{17,16},{19,... | collective-permute-start | bytes 3080 | tf_op jit(solution)/shard_map/ppermute | solution.py:27
  141.8 18.2 %collective-permute-start.20 = (f32[16,1,256]{2,1,0:T(1,128)S(1)}, f32[16,1,256]{2,1,0:T(1,128)S(1)}, u32[]{:S(2)}, u32[]{:S(2)}) collective-permute-start(f32[16,1,256]{2,1,0:T(1,128)S(1)} %copy-done.18), channel_id=1, source_target_pairs={{0,2},{2,4},{4,6},{6,8},{8,10},{10,12},{12,14},{1,3},{3,5},{5,7},{... | collective-permute-start | bytes 49160 | tf_op jit(solution)/shard_map/ppermute | solution.py:26
  143.7 17.5 %collective-permute-start.21 = (f32[16,1,256]{2,1,0:T(1,128)S(1)}, f32[16,1,256]{2,1,0:T(1,128)S(1)}, u32[]{:S(2)}, u32[]{:S(2)}) collective-permute-start(f32[16,1,256]{2,1,0:T(1,128)S(1)} %copy-done.17), channel_id=1, source_target_pairs={{2,0},{4,2},{6,4},{8,6},{10,8},{12,10},{14,12},{3,1},{5,3},{7,5},{... | collective-permute-start | bytes 49160 | tf_op jit(solution)/shard_map/ppermute | solution.py:27
  173.2 18.6 %collective-permute-start.41 = (f32[2,8,8,1]{3,2,1,0:T(8,128)S(1)}, f32[2,8,8,1]{3,2,1,0:T(8,128)S(1)}, u32[]{:S(2)}, u32[]{:S(2)}) collective-permute-start(f32[2,8,8,1]{3,2,1,0:T(8,128)S(1)} %get-tuple-element.96), channel_id=1, source_target_pairs={{1,0},{3,2},{5,4},{7,6},{9,8},{11,10},{13,12},{15,14},{17,16},{19,... | collective-permute-start | bytes 1544 | tf_op jit(solution)/shard_map/ppermute | solution.py:27
  176.3 17.5 %collective-permute-start.37 = (f32[2,8,1,128]{3,2,1,0:T(1,128)S(1)}, f32[2,8,1,128]{3,2,1,0:T(1,128)S(1)}, u32[]{:S(2)}, u32[]{:S(2)}) collective-permute-start(f32[2,8,1,128]{3,2,1,0:T(1,128)S(1)} %copy-done.25), channel_id=1, source_target_pairs={{0,2},{2,4},{4,6},{6,8},{8,10},{10,12},{12,14},{1,3},{3,5},{5,7},{... | collective-permute-start | bytes 24584 | tf_op jit(solution)/shard_map/ppermute | solution.py:26
  180.2 18.0 %collective-permute-start.39 = (f32[2,1,8,128]{3,2,1,0:T(8,128)S(1)}, f32[2,1,8,128]{3,2,1,0:T(8,128)S(1)}, u32[]{:S(2)}, u32[]{:S(2)}) collective-permute-start(f32[2,1,8,128]{3,2,1,0:T(8,128)S(1)} %copy-done.23), channel_id=1, source_target_pairs={{16,0},{32,16},{48,32},{64,48},{80,64},{96,80},{112,96},{128,112},... | collective-permute-start | bytes 24584 | tf_op jit(solution)/shard_map/ppermute | solution.py:27
  213.5 18.3 %collective-permute-start.34 = (f32[16,16,1]{2,1,0:T(8,128)S(1)}, f32[16,16,1]{2,1,0:T(8,128)S(1)}, u32[]{:S(2)}, u32[]{:S(2)}) collective-permute-start(f32[16,16,1]{2,1,0:T(8,128)S(1)} %get-tuple-element.60), channel_id=1, source_target_pairs={{0,1},{2,3},{4,5},{6,7},{8,9},{10,11},{12,13},{14,15},{16,17},{18,... | collective-permute-start | bytes 3080 | tf_op jit(solution)/shard_map/ppermute | solution.py:26
  214.8 20.0 %collective-permute-start.35 = (f32[16,16,1]{2,1,0:T(8,128)S(1)}, f32[16,16,1]{2,1,0:T(8,128)S(1)}, u32[]{:S(2)}, u32[]{:S(2)}) collective-permute-start(f32[16,16,1]{2,1,0:T(8,128)S(1)} %get-tuple-element.61), channel_id=1, source_target_pairs={{1,0},{3,2},{5,4},{7,6},{9,8},{11,10},{13,12},{15,14},{17,16},{19,... | collective-permute-start | bytes 3080 | tf_op jit(solution)/shard_map/ppermute | solution.py:27
  224.4 17.9 %collective-permute-start.31 = (f32[1,16,256]{2,1,0:T(8,128)S(1)}, f32[1,16,256]{2,1,0:T(8,128)S(1)}, u32[]{:S(2)}, u32[]{:S(2)}) collective-permute-start(f32[1,16,256]{2,1,0:T(8,128)S(1)} %get-tuple-element.63), channel_id=1, source_target_pairs={{16,0},{32,16},{48,32},{64,48},{80,64},{96,80},{112,96},{128,112},... | collective-permute-start | bytes 49160 | tf_op jit(solution)/shard_map/ppermute | solution.py:27
  230.5 37.3 %collective-permute-start.46 = (f32[8,8,1]{2,1,0:T(8,128)S(1)}, f32[8,8,1]{2,1,0:T(8,128)S(1)}, u32[]{:S(2)}, u32[]{:S(2)}) collective-permute-start(f32[8,8,1]{2,1,0:T(8,128)S(1)} %broadcast.321), channel_id=1, source_target_pairs={{0,1},{2,3},{4,5},{6,7},{8,9},{10,11},{12,13},{14,15},{16,17},{18,... | collective-permute-start | bytes 776 | tf_op jit(solution)/shard_map/ppermute | solution.py:26
  231.8 36.0 %collective-permute-start.47 = (f32[8,8,1]{2,1,0:T(8,128)S(1)}, f32[8,8,1]{2,1,0:T(8,128)S(1)}, u32[]{:S(2)}, u32[]{:S(2)}) collective-permute-start(f32[8,8,1]{2,1,0:T(8,128)S(1)} %broadcast.321), channel_id=1, source_target_pairs={{1,0},{3,2},{5,4},{7,6},{9,8},{11,10},{13,12},{15,14},{17,16},{19,... | collective-permute-start | bytes 776 | tf_op jit(solution)/shard_map/ppermute | solution.py:27
  234.8 33.0 %collective-permute-start.42 = (f32[1,8,128]{2,1,0:T(8,128)S(1)}, f32[1,8,128]{2,1,0:T(8,128)S(1)}, u32[]{:S(2)}, u32[]{:S(2)}) collective-permute-start(f32[1,8,128]{2,1,0:T(8,128)S(1)} %broadcast.319), channel_id=1, source_target_pairs={{0,16},{16,32},{32,48},{48,64},{64,80},{80,96},{96,112},{112,128},... | collective-permute-start | bytes 12296 | tf_op jit(solution)/shard_map/ppermute | solution.py:26
  236.8 31.0 %collective-permute-start.43 = (f32[1,8,128]{2,1,0:T(8,128)S(1)}, f32[1,8,128]{2,1,0:T(8,128)S(1)}, u32[]{:S(2)}, u32[]{:S(2)}) collective-permute-start(f32[1,8,128]{2,1,0:T(8,128)S(1)} %broadcast.319), channel_id=1, source_target_pairs={{16,0},{32,16},{48,32},{64,48},{80,64},{96,80},{112,96},{128,112},... | collective-permute-start | bytes 12296 | tf_op jit(solution)/shard_map/ppermute | solution.py:27
  289.3 17.5 %collective-permute-start.57 = (f32[8,1,128]{2,1,0:T(1,128)S(1)}, f32[8,1,128]{2,1,0:T(1,128)S(1)}, u32[]{:S(2)}, u32[]{:S(2)}) collective-permute-start(f32[8,1,128]{2,1,0:T(1,128)S(1)} %get-tuple-element.118), channel_id=1, source_target_pairs={{2,0},{4,2},{6,4},{8,6},{10,8},{12,10},{14,12},{3,1},{5,3},{7,5},{... | collective-permute-start | bytes 12296 | tf_op jit(solution)/shard_map/ppermute | solution.py:27
  293.9 21.5 %collective-permute-start.54 = (f32[1,8,128]{2,1,0:T(8,128)S(1)}, f32[1,8,128]{2,1,0:T(8,128)S(1)}, u32[]{:S(2)}, u32[]{:S(2)}) collective-permute-start(f32[1,8,128]{2,1,0:T(8,128)S(1)} %get-tuple-element.115), channel_id=1, source_target_pairs={{0,16},{16,32},{32,48},{48,64},{64,80},{80,96},{96,112},{112,128},... | collective-permute-start | bytes 12296 | tf_op jit(solution)/shard_map/ppermute | solution.py:26
  295.8 25.1 %collective-permute-start.55 = (f32[1,8,128]{2,1,0:T(8,128)S(1)}, f32[1,8,128]{2,1,0:T(8,128)S(1)}, u32[]{:S(2)}, u32[]{:S(2)}) collective-permute-start(f32[1,8,128]{2,1,0:T(8,128)S(1)} %get-tuple-element.116), channel_id=1, source_target_pairs={{16,0},{32,16},{48,32},{64,48},{80,64},{96,80},{112,96},{128,112},... | collective-permute-start | bytes 12296 | tf_op jit(solution)/shard_map/ppermute | solution.py:27
  (122 other events, 1862.2 us)
where the time goes:
time: 604 us; the launch traced here: 596 us
  starting transfers between devices  368 us (61%)
  local copies, waits for them, and re-layouts  109 us (18%)
  blocking collectives  72.7 us (12%)
  other arithmetic  32.4 us (5%)
  waiting for transfers between devices  9.26 us (2%)
    ppermute x60, starting transfers between devices, extended(): lax.ppermute(first, axis, [(b, a) for a, b in up])  261 us
    ppermute x60, starting transfers between devices, extended(): lax.ppermute(last, axis, up)  108 us
    all_gather x1, blocking collectives, coarse_solve(): whole = lax.all_gather(stacked, ('gx', 'gy', 'gz'), axis=0, tiled=True)  72.7 us
    another operation x3, local copies, waits for them, and re-layouts, on_device(): plain_coefs = [jnp.stack([inner, outer])]  32.1 us
    reshape x3, local copies, waits for them, and re-layouts, restrict(): values.reshape(lead + (shape[-3] // 2, 2, shape[-2] // 2, 2, shape[-1] //...  21.2 us
    reshape x4, local copies, waits for them, and re-layouts, expand(): return big.reshape(sa * factor, sb * factor, sc * factor)  18.8 us
    broadcast_in_dim x9, local copies, waits for them, and re-layouts, expand(): jnp.broadcast_to(blocks[:, None, :, None, :, None], (sa, factor, sb, fact...  13.3 us
    select_n x28, other arithmetic, sweeps(): field = jnp.where(parity == colour, updated, field)  13 us
  transfers between devices with their start and end apart: 120, of which 12 were waited for; matrix products, arithmetic and copies ran while one was open for 9% of the time, Pallas kernels for 0%

commit v1 on v0

v1 whole, which is shorter than its diff:
```python
import jax
import jax.numpy as jnp
from jax import lax
from jax.experimental import pallas as pl
from jax.experimental.pallas import tpu as pltpu
from jax.sharding import PartitionSpec as P

TIME_STEP = 0.05
IONIC_GAIN = 8.0
IONIC_ONSET = 0.15
RECOVERY_RATE = 0.01
COARSE_SWEEPS = 8

F32 = jnp.float32
BX, BY, BZ = 16, 16, 256
H = 5
X0, Y0, Z0 = BX + 2 * H, 32, 2 * BZ
X1, Y1, Z1 = BX // 2 + 2 * H, 24, BZ
Z2 = BZ // 2
PAD = 4
VMEM = pl.BlockSpec(memory_space=pltpu.VMEM)
SMEM = pl.BlockSpec(memory_space=pltpu.SMEM)
PARAMS = pltpu.CompilerParams(vmem_limit_bytes=60 * 1024 * 1024)


def iota(shape, dim):
    return lax.broadcasted_iota(jnp.int32, shape, dim)


def up(x, axis):
    return pltpu.roll(x, x.shape[axis] - 1, axis)


def down(x, axis):
    return pltpu.roll(x, 1, axis)


def pair_matrix(rows, cols, value):
    return jnp.where(iota((rows, cols), 0) // 2 == iota((rows, cols), 1), value, 0.0).astype(F32)


def copy_matrix(rows, cols):
    return jnp.where(iota((rows, cols), 1) // 2 == iota((rows, cols), 0), 1.0, 0.0).astype(F32)


def dot(a, b):
    return jnp.dot(a, b, precision=lax.Precision.HIGHEST, preferred_element_type=F32)


def sum_rows(buf, x):
    rows, cols = x.shape
    sums = []
    for c in range(cols // 128):
        buf[c, 0:rows, :] = x[:, 128 * c : 128 * c + 128]
        sums.append(buf[c, pl.ds(0, rows // 2, 2), :] + buf[c, pl.ds(1, rows // 2, 2), :])
    return sums[0] if len(sums) == 1 else jnp.concatenate(sums, axis=1)


def twice_rows(buf, x):
    rows, cols = x.shape
    for c in range(cols // 128):
        for k in (0, 1):
            buf[c, pl.ds(k, rows, 2), :] = x[:, 128 * c : 128 * c + 128]


def columns(buf, start, rows, cols):
    parts = [buf[c, pl.ds(start, rows), :] for c in range(cols // 128)]
    return parts[0] if len(parts) == 1 else jnp.concatenate(parts, axis=1)


def loop(start, stop, step, body):
    def run(index, carry):
        body(start + index * step)
        return carry

    lax.fori_loop(0, (stop - start) // step, run, 0)


def faces(inner, outer, ax, ay, az, diag, inv, mx, my, mz, step):
    n, ys, zs = inner.shape
    shape = (step, ys, zs)
    row, lane = iota(shape, 1), iota(shape, 2)

    def x_face(i):
        here, there = pl.ds(i, step), pl.ds(i + 1, step)
        low = jnp.minimum(inner[here], inner[there])
        if mx is not None:
            mx[here] = low
        ax[here] = low + 0.5 * (outer[here] + outer[there])

    def first():
        low = jnp.minimum(inner[0:1], inner[1:2])
        if mx is not None:
            mx[0:1] = low
        ax[0:1] = low + 0.5 * (outer[0:1] + outer[1:2])

    first()

    def body(i):
        x_face(i)
        here = pl.ds(i, step)
        c_in, c_out = inner[here], outer[here]
        half = 0.5 * c_out
        low = jnp.where(row < ys - 1, jnp.minimum(c_in, up(c_in, 1)), 0.0)
        full = low + half + jnp.where(row < ys - 1, up(half, 1), 0.0)
        if my is not None:
            my[here] = low
        ay[here] = jnp.where(row < ys - 1, full, 0.0)
        total = full + jnp.where(row > 0, down(full, 1), half)
        low = jnp.where(lane < zs - 1, jnp.minimum(c_in, up(c_in, 2)), 0.0)
        full = low + half + jnp.where(lane < zs - 1, up(half, 2), 0.0)
        if mz is not None:
            mz[here] = low
        az[here] = jnp.where(lane < zs - 1, full, 0.0)
        total = total + full + jnp.where(lane > 0, down(full, 2), half)
        total = total + ax[here] + ax[pl.ds(i - 1, step)]
        if diag is not None:
            diag[here] = total
        inv[here] = jnp.where(c_out > 0.0, 1.0 / jnp.where(c_out > 0.0, total, 1.0), 0.0)

    loop(1, n - 1, step, body)


def offdiag(v, ax, ay, az, i, step):
    here, after, before = pl.ds(i, step), pl.ds(i + 1, step), pl.ds(i - 1, step)
    c = v[here]
    total = ax[here] * v[after] + ax[before] * v[before]
    cy, cz = ay[here], az[here]
    total = total + cy * up(c, 1) + down(cy * c, 1)
    return c, total + cz * up(c, 2) + down(cz * c, 2)


def half_sweep(v, b, ax, ay, az, inv, colour, offset, start, stop, step):
    shape = (step,) + tuple(v.shape[1:])
    place = iota(shape, 0) + iota(shape, 1) + iota(shape, 2)

    def body(i):
        here = pl.ds(i, step)
        c, total = offdiag(v, ax, ay, az, i, step)
        mine = ((place + (i + offset)) & 1) == colour
        v[here] = jnp.where(mine, (b[here] + total) * inv[here], c)

    loop(start, stop, step, body)


def first_half(v, b, inv, offset, start, stop, step):
    shape = (step,) + tuple(v.shape[1:])
    place = iota(shape, 0) + iota(shape, 1) + iota(shape, 2)

    def body(i):
        here = pl.ds(i, step)
        mine = ((place + (i + offset)) & 1) == 0
        v[here] = jnp.where(mine, b[here] * inv[here], 0.0)

    loop(start, stop, step, body)


def prep_kernel(m, r, u, f, labels, own, xup, xdn, yup, ydn, rnext):
    spread = jnp.where(iota((BZ // 8, BZ), 1) // 8 == iota((BZ // 8, BZ), 0), 1.0, 0.0).astype(F32)
    for bx in range(BX // 8):
        wide = jnp.dot(labels[bx].astype(F32), spread, preferred_element_type=F32)
        kind = jnp.concatenate(
            [jnp.broadcast_to(wide[by : by + 1], (8, BZ)) for by in range(BY // 8)], axis=0
        )
        factor = jnp.where(kind > 1.5, 0.3, jnp.where(kind > 0.5, 1.0, 0.0)).astype(F32)
        for x in range(8 * bx, 8 * bx + 8):
            own[2, x] = factor * f[x]
            mm, rr = m[x], r[x]
            own[0, x] = mm
            own[1, x] = u[x]
            own[3, x] = rr
            rnext[x] = rr + TIME_STEP * RECOVERY_RATE * (
                -rr - IONIC_GAIN * mm * (mm - IONIC_ONSET - 1.0)
            )
    for q in range(4):
        xup[q] = own[q, BX - H : BX]
        xdn[q] = own[q, 0:H]
        yup[q] = own[q, :, BY - 8 : BY, :]
        ydn[q] = own[q, :, 0:8, :]


def fine_kernel(
    place, own, own_z, xlo, xlo_z, xhi, xhi_z, ylo, ylo_z, yhi, yhi_z, clo, clo_z, chi, chi_z,
    mnext, v, rhs, inner, packed,
    m, r, s, outer, mx, my, mz, ax, ay, az, diag, inv, fold, fold2,
):
    core = place[2]
    has_xl = (place[0] > 0).astype(F32)
    has_xh = (place[0] < place[3] - 1).astype(F32)
    has_yl = (place[1] > 0).astype(F32)
    has_yh = (place[1] < place[4] - 1).astype(F32)
    for buf in (m, v, inner, r):
        buf[0:H, 0:8, :] = jnp.zeros((H, 8, Z0), F32)
    for side in (0, 1):
        lanes = pl.ds(pl.multiple_of((core if side == 0 else 1 - core) * BZ, BZ), BZ)
        o, xl, xh, yl, yh, cl, ch = (
            (own, xlo, xhi, ylo, yhi, clo, chi)
            if side == 0
            else (own_z, xlo_z, xhi_z, ylo_z, yhi_z, clo_z, chi_z)
        )
        for q, buf in enumerate((m, v, inner, r)):
            def body(x, q=q, buf=buf):
                buf[x + H, 8:24, lanes] = o[q, x]
                buf[x + H, 0:8, lanes] = yl[q, x] * has_yl
                buf[x + H, 24:32, lanes] = yh[q, x] * has_yh

            loop(0, BX, 1, body)

            def edge(x, q=q, buf=buf):
                buf[x, 8:24, lanes] = xl[q, x] * has_xl
                buf[x + BX + H, 8:24, lanes] = xh[q, x] * has_xh
                buf[x, 0:8, lanes] = cl[q, x] * (has_xl * has_yl)
                buf[x, 24:32, lanes] = ch[q, x] * (has_xl * has_yh)
                buf[x + BX + H, 0:8, lanes] = cl[q, x + H] * (has_xh * has_yl)
                buf[x + BX + H, 24:32, lanes] = ch[q, x + H] * (has_xh * has_yh)

            loop(0, H, 1, edge)
    row = iota((1, Y0, Z0), 1)
    in_y = jnp.where(row < 8, has_yl, jnp.where(row < 24, 1.0, has_yh))

    def body(x):
        in_x = jnp.where(x < H, has_xl, jnp.where(x < BX + H, 1.0, has_xh))
        here = pl.ds(x, 1)
        outer[here] = jnp.where(inner[here] > 0.0, 1.0, 3.0 * in_x * in_y)
        s[here] = m[here] + v[here]

    loop(0, X0, 1, body)
    faces(inner, outer, ax, ay, az, diag, inv, mx, my, mz, 1)

    def intra(w, i):
        here, after, before = pl.ds(i, 1), pl.ds(i + 1, 1), pl.ds(i - 1, 1)
        c = w[here]
        total = mx[here] * (w[after] - c) + mx[before] * (w[before] - c)
        flow = my[here] * (up(c, 1) - c)
        total = total + flow - down(flow, 1)
        flow = mz[here] * (up(c, 2) - c)
        return total + flow - down(flow, 2)

    def body(x):
        here = pl.ds(x, 1)
        mm = m[here]
        ionic = IONIC_GAIN * mm * (mm - IONIC_ONSET) * (mm - 1.0) + mm * r[here]
        ionic = jnp.where(inner[here] > 0.0, ionic, 0.0)
        r[here] = mm + TIME_STEP * (intra(s, x) - ionic)

    loop(1, X0 - 1, 1, body)
    lanes = pl.ds(pl.multiple_of(core * BZ, BZ), BZ)
    mnext[...] = r[H : BX + H, 8:24, lanes]

    def body(x):
        rhs[pl.ds(x, 1)] = intra(r, x)

    loop(2, X0 - 2, 1, body)
    half_sweep(v, rhs, ax, ay, az, inv, 0, 1, 2, X0 - 2, 1)
    half_sweep(v, rhs, ax, ay, az, inv, 1, 1, 3, X0 - 3, 1)

    def body(p):
        total = None
        for i in (2 * p + H, 2 * p + H + 1):
            c, off = offdiag(v, ax, ay, az, i, 1)
            here = pl.ds(i, 1)
            res = rhs[here] - (diag[here] * c - off)
            total = res if total is None else total + res
        fold[pl.ds(p, 1)] = total[:, 8:24, :]
        fold[pl.ds(p + 8, 1)] = (
            inner[pl.ds(2 * p + H, 1), 8:24, :] + inner[pl.ds(2 * p + H + 1, 1), 8:24, :]
        )

    loop(0, BX // 2, 1, body)
    half = BX // 2 * BY
    pairs = pair_matrix(Z0, Z1, 0.5)
    both = sum_rows(fold2, dot(fold[...].reshape(2 * half, Z0), pairs))
    packed[0] = both[: half // 2].reshape(8, 8, Z1)
    packed[1] = 0.25 * both[half // 2 :].reshape(8, 8, Z1)


def middle_kernel(
    place, low, own, high, v, b, inner, send, outer, ax, ay, az, diag, inv, fold, fold2
):
    core = place[2]
    has_xl = (place[0] > 0).astype(F32)
    has_xh = (place[0] < place[3] - 1).astype(F32)
    has_yl = (place[1] > 0).astype(F32)
    has_yh = (place[1] < place[4] - 1).astype(F32)
    row = iota((1, Y1, Z1), 1)
    in_y = jnp.where(row < 8, has_yl, jnp.where(row < 16, 1.0, has_yh))
    for q, buf in enumerate((b, inner)):
        buf[0:H] = low[q] * (in_y * has_xl)
        buf[H : H + 8] = own[q] * in_y
        buf[H + 8 :] = high[q] * (in_y * has_xh)
    for x in range(X1):
        in_x = has_xl if x < H else (has_xh if x >= H + 8 else 1.0)
        here = slice(x, x + 1)
        outer[here] = jnp.where(inner[here] > 0.0, 1.0, 3.0 * in_x * in_y)
    faces(inner, outer, ax, ay, az, diag, inv, None, None, None, 2)
    v[0:1] = jnp.zeros((1, Y1, Z1), F32)
    v[X1 - 1 :] = jnp.zeros((1, Y1, Z1), F32)
    first_half(v, b, inv, 1, 1, X1 - 1, 2)
    half_sweep(v, b, ax, ay, az, inv, 1, 1, 1, X1 - 1, 2)
    for p in range(4):
        i = 2 * p + H
        c, off = offdiag(v, ax, ay, az, i, 2)
        here = slice(i, i + 2)
        res = (b[here] - (diag[here] * c - off))[:, 8:16, :]
        mean = inner[here][:, 8:16, :]
        fold[8 * p : 8 * p + 8] = res[0] + res[1]
        fold[32 + 8 * p : 40 + 8 * p] = 0.25 * (mean[0] + mean[1])
    both = sum_rows(fold2, dot(fold[...], pair_matrix(Z1, Z2, 0.5)))
    first = core == 0
    piece = jnp.concatenate(
        [
            jnp.where(first, both[0:8], both[8:16]),
            jnp.where(first, both[16:24], both[24:32]),
        ],
        axis=0,
    )

    def body(d):
        send[d] = piece

    loop(0, send.shape[0], 1, body)


def up_kernel(
    place, got, got_z, v1, b1, in1, v0, b0, in0, out,
    b2, in2, out2, ax2, ay2, az2, diag2, inv2, v2,
    b3, in3, out3, ax3, ay3, az3, inv3, v3,
    out1, ax1, ay1, az1, inv1, out0, ax0, ay0, az0, inv0, fold2, fold1, fold0,
    *, nx, ny,
):
    core = place[2]
    has_xl = (place[0] > 0).astype(F32)
    has_xh = (place[0] < nx - 1).astype(F32)
    has_yl = (place[1] > 0).astype(F32)
    has_yh = (place[1] < ny - 1).astype(F32)
    n2, y2 = 4 * nx, 4 * ny
    n3, y3 = 2 * nx, 2 * ny
    for buf in (b2, in2, out2, v2):
        buf[0:PAD] = jnp.zeros((PAD, y2, Z2), F32)
        buf[PAD + n2 :] = jnp.zeros((PAD, y2, Z2), F32)

    def body(gx):
        for side in (0, 1):
            src = got if side == 0 else got_z
            half = core if side == 0 else 1 - core
            for i in (0, 1):
                x = PAD + 4 * gx + 2 * half + i
                for gy in range(ny):
                    b2[x, 4 * gy : 4 * gy + 4, :] = src[gx * ny + gy, 4 * i : 4 * i + 4, :]
                    in2[x, 4 * gy : 4 * gy + 4, :] = src[gx * ny + gy, 8 + 4 * i : 12 + 4 * i, :]

    loop(0, nx, 1, body)

    def body(i):
        here = pl.ds(i, 4)
        out2[here] = jnp.where(in2[here] > 0.0, 1.0, 3.0)

    loop(PAD, PAD + n2, 4, body)
    core2 = slice(PAD - 1, PAD + n2 + 1)
    at = lambda ref: ref.at[pl.ds(PAD - 1, n2 + 2)]
    faces(at(in2), at(out2), at(ax2), at(ay2), at(az2), at(diag2), at(inv2), None, None, None, 4)
    first_half(v2, b2, inv2, 0, PAD, PAD + n2, 4)
    half_sweep(v2, b2, ax2, ay2, az2, inv2, 1, 0, PAD, PAD + n2, 4)

    def body(p):
        i = PAD + 4 * p
        c, off = offdiag(v2, ax2, ay2, az2, i, 4)
        here = pl.ds(i, 4)
        res = b2[here] - (diag2[here] * c - off)
        mean = in2[here]
        for k in (0, 1):
            fold2[0, pl.ds(2 * p + k, 1)] = res[2 * k : 2 * k + 1] + res[2 * k + 1 : 2 * k + 2]
            fold2[1, pl.ds(2 * p + k, 1)] = 0.25 * (
                mean[2 * k : 2 * k + 1] + mean[2 * k + 1 : 2 * k + 2]
            )

    loop(0, nx, 1, body)
    pairs = pair_matrix(Z2, Z2, 0.5)
    rows = n3 * y2
    for q in (0, 1):
        both = sum_rows(fold1, dot(fold2[q].reshape(rows, Z2), pairs))
        (b3, in3)[q][1 : n3 + 1] = both.reshape(n3, y3, Z2)
    for buf in (in3, out3, v3):
        buf[0:1] = jnp.zeros((1, y3, Z2), F32)
        buf[n3 + 1 :] = jnp.zeros((1, y3, Z2), F32)
    lane = iota((n3, y3, Z2), 2)
    out3[1 : n3 + 1] = jnp.where(
        lane < Z2 // 2, jnp.where(in3[1 : n3 + 1] > 0.0, 1.0, 3.0), 0.0
    )
    step3 = 8 if n3 % 8 == 0 else n3
    faces(in3, out3, ax3, ay3, az3, None, inv3, None, None, None, step3)
    first_half(v3, b3, inv3, 1, 1, n3 + 1, step3)
    half_sweep(v3, b3, ax3, ay3, az3, inv3, 1, 1, 1, n3 + 1, step3)

    def sweep(k):
        half_sweep(v3, b3, ax3, ay3, az3, inv3, 0, 1, 1, n3 + 1, step3)
        half_sweep(v3, b3, ax3, ay3, az3, inv3, 1, 1, 1, n3 + 1, step3)

    loop(0, COARSE_SWEEPS - 1, 1, sweep)
    wide = dot(v3[1 : n3 + 1].reshape(n3 * y3, Z2), copy_matrix(Z2, Z2))
    twice_rows(fold1, wide)

    def body(p):
        e = columns(fold1, pl.multiple_of(p * y2, y2), y2, Z2)
        for k in (0, 1):
            v2[PAD + 2 * p + k] = v2[PAD + 2 * p + k] + e

    loop(0, n3, 1, body)
    half_sweep(v2, b2, ax2, ay2, az2, inv2, 0, 0, PAD, PAD + n2, 4)
    half_sweep(v2, b2, ax2, ay2, az2, inv2, 1, 0, PAD, PAD + n2, 4)
    row = iota((1, Y1, Z1), 1)
    in_y = jnp.where(row < 8, has_yl, jnp.where(row < 16, 1.0, has_yh))
    for x in range(X1):
        in_x = has_xl if x < H else (has_xh if x >= H + 8 else 1.0)
        here = slice(x, x + 1)
        out1[here] = jnp.where(in1[here] > 0.0, 1.0, 3.0 * in_x * in_y)
    faces(in1, out1, ax1, ay1, az1, None, inv1, None, None, None, 2)
    shift = lax.rem(4 - 4 * place[1] + 2 * y2, y2)
    part = pltpu.roll(v2[pl.ds(PAD + 4 * place[0] - 2, 8)], shift, 1)[:, 0:16, :]
    wide = dot(part.reshape(128, Z2), copy_matrix(Z2, Z1))
    twice_rows(fold1, wide)
    for x in range(1, X1 - 1):
        k = (x - 1) // 2
        e = columns(fold1, 32 * k, Y1, Z1)
        v1[x] = jnp.where(out1[x] > 0.0, v1[x] + e, 0.0)
    half_sweep(v1, b1, ax1, ay1, az1, inv1, 0, 1, 1, X1 - 1, 2)
    half_sweep(v1, b1, ax1, ay1, az1, inv1, 1, 1, 1, X1 - 1, 2)
    row = iota((1, Y0, Z0), 1)
    in_y = jnp.where(row < 8, has_yl, jnp.where(row < 24, 1.0, has_yh))

    def body(x):
        in_x = jnp.where(x < H, has_xl, jnp.where(x < BX + H, 1.0, has_xh))
        here = pl.ds(x, 1)
        out0[here] = jnp.where(in0[here] > 0.0, 1.0, 3.0 * in_x * in_y)

    loop(2, X0 - 2, 1, body)
    at = lambda ref: ref.at[pl.ds(2, X0 - 4)]
    faces(at(in0), at(out0), at(ax0), at(ay0), at(az0), None, at(inv0), None, None, None, 1)
    part = v1[4:14, 4:20, :]
    wide = dot(part.reshape(160, Z1), copy_matrix(Z1, Z0))
    twice_rows(fold0, wide)

    def body(p):
        e = columns(fold0, pl.multiple_of(p * 32, 32), 32, Z0)
        for k in (0, 1):
            x = 3 + 2 * p + k
            v0[x] = jnp.where(out0[x] > 0.0, v0[x] + e, 0.0)

    loop(0, 10, 1, body)
    half_sweep(v0, b0, ax0, ay0, az0, inv0, 0, 1, H - 1, X0 - H + 1, 1)
    half_sweep(v0, b0, ax0, ay0, az0, inv0, 1, 1, H, X0 - H, 1)
    lanes = pl.ds(pl.multiple_of(core * BZ, BZ), BZ)
    out[...] = v0[H : BX + H, 8:24, lanes]


def shape(*dims):
    return jax.ShapeDtypeStruct(dims, F32)


def scratch(*dims):
    return pltpu.VMEM(dims, F32)


def ring(x, axis, step):
    n = lax.axis_size(axis)
    return lax.ppermute(x, axis, [(i, (i + step) % n) for i in range(n)])


def swap(x):
    return lax.ppermute(x, "gz", [(0, 1), (1, 0)])


def on_device(membrane, recovery, extracellular, fiber_scale, labels):
    nx, ny = lax.axis_size("gx"), lax.axis_size("gy")
    place = jnp.stack(
        [lax.axis_index("gx"), lax.axis_index("gy"), lax.axis_index("gz"), nx, ny]
    ).astype(jnp.int32)
    own, xup, xdn, yup, ydn, rnext = pl.pallas_call(
        prep_kernel,
        out_shape=(
            shape(4, BX, BY, BZ),
            shape(4, H, BY, BZ),
            shape(4, H, BY, BZ),
            shape(4, BX, 8, BZ),
            shape(4, BX, 8, BZ),
            shape(BX, BY, BZ),
        ),
        in_specs=[VMEM] * 5,
        out_specs=(VMEM,) * 6,
        compiler_params=PARAMS,
        name="prep",
    )(membrane, recovery, extracellular, fiber_scale, labels)
    xlo, xhi = ring(xup, "gx", 1), ring(xdn, "gx", -1)
    ylo, yhi = ring(yup, "gy", 1), ring(ydn, "gy", -1)
    clo = ring(jnp.concatenate([xlo[:, :, 8:16], xhi[:, :, 8:16]], axis=1), "gy", 1)
    chi = ring(jnp.concatenate([xlo[:, :, 0:8], xhi[:, :, 0:8]], axis=1), "gy", -1)
    halos = []
    for piece in (own, xlo, xhi, ylo, yhi, clo, chi):
        halos += [piece, swap(piece)]
    fine = (X0, Y0, Z0)
    mnext, v0, b0, in0, packed = pl.pallas_call(
        fine_kernel,
        out_shape=(
            shape(BX, BY, BZ), shape(*fine), shape(*fine), shape(*fine), shape(2, 8, 8, Z1),
        ),
        in_specs=[SMEM] + [VMEM] * 14,
        out_specs=(VMEM,) * 5,
        scratch_shapes=[scratch(*fine)] * 12 + [scratch(16, BY, Z0), scratch(2, 256, 128)],
        compiler_params=PARAMS,
        name="fine",
    )(place, *halos)
    wide = jnp.concatenate([ring(packed, "gy", 1), packed, ring(packed, "gy", -1)], axis=2)
    low, high = ring(wide[:, 8 - H :], "gx", 1), ring(wide[:, :H], "gx", -1)
    mid = (X1, Y1, Z1)
    v1, b1, in1, send = pl.pallas_call(
        middle_kernel,
        out_shape=(shape(*mid), shape(*mid), shape(*mid), shape(nx * ny, 16, Z2)),
        in_specs=[SMEM] + [VMEM] * 3,
        out_specs=(VMEM,) * 4,
        scratch_shapes=[scratch(*mid)] * 6 + [scratch(64, Z1), scratch(1, 64, 128)],
        compiler_params=PARAMS,
        name="middle",
    )(place, low, wide, high)
    got = lax.all_to_all(send, ("gx", "gy"), 0, 0, tiled=True)
    got_z = swap(got)
    grid2 = (4 * nx + 2 * PAD, 4 * ny, Z2)
    grid3 = (2 * nx + 2, 2 * ny, Z2)
    enext = pl.pallas_call(
        lambda *refs: up_kernel(*refs, nx=nx, ny=ny),
        out_shape=shape(BX, BY, BZ),
        in_specs=[SMEM] + [VMEM] * 8,
        out_specs=VMEM,
        scratch_shapes=[scratch(*grid2)] * 9
        + [scratch(*grid3)] * 8
        + [scratch(*mid)] * 5
        + [scratch(*fine)] * 5
        + [
            scratch(2, 2 * nx, 4 * ny, Z2),
            scratch(2, max(8 * nx * ny, 256), 128),
            scratch(4, 320, 128),
        ],
        compiler_params=PARAMS,
        name="up",
    )(place, got, got_z, v1, b1, in1, v0, b0, in0)
    return mnext, rnext, enext


def solution(mesh):
    spec = P("gx", "gy", "gz")
    return jax.shard_map(
        on_device, mesh=mesh, in_specs=(spec,) * 5, out_specs=(spec,) * 3, check_vma=False
    )
```

time: 604 us -> 171 us (0.28)
  the two profiles are of different devices: /device:TPU:131 before, /device:TPU:1 now
where the time goes in v1:
time: 171 us; the launch traced here: 170 us
  Pallas kernels  70.1 us (41%)
  blocking collectives  36.9 us (22%)
  starting transfers between devices  33.2 us (19%)
  waiting for transfers between devices  23.7 us (14%)
  local copies, waits for them, and re-layouts  5.64 us (3%)
    all_to_all x1, blocking collectives, on_device(): got = lax.all_to_all(send, ('gx', 'gy'), 0, 0, tiled=True)  36.9 us
    pallas_call x1, Pallas kernels, on_device(): pl.pallas_call(lambda *refs: up_kernel(*refs, nx=nx, ny=ny), out_shape=sh...  36.2 us
    pallas_call x1, Pallas kernels, on_device(): pl.pallas_call(fine_kernel, out_shape=(shape(BX, BY, BZ), shape(*fine), s...  24.8 us
    ppermute x10, waiting for transfers between devices, ring(): return lax.ppermute(x, axis, [(i, (i + step) % n) for i in range(n)])  20.7 us
    ppermute x10, starting transfers between devices, ring(): return lax.ppermute(x, axis, [(i, (i + step) % n) for i in range(n)])  18.9 us
    ppermute x8, starting transfers between devices, swap(): return lax.ppermute(x, 'gz', [(0, 1), (1, 0)])  14.3 us
    pallas_call x1, Pallas kernels, on_device(): pl.pallas_call(middle_kernel, out_shape=(shape(*mid), shape(*mid), shape(...  6.14 us
    unnamed x28, local copies, waits for them, and re-layouts  4.95 us
  transfers between devices with their start and end apart: 18, of which 8 were waited for; matrix products, arithmetic and copies ran while one was open for 1% of the time, Pallas kernels for 0%

profile of v1, /device:TPU:1, one launch (start us, length us, event | category | flops | bytes accessed | tf_op | source)
XLA Modules:
  0.0 170.3 jit_solution(14227291208311003994)
XLA Ops:
  0.6 3.0 %prep.1 = (f32[4,16,16,256]{3,2,1,0:T(8,128)}, f32[4,5,16,256]{3,2,1,0:T(8,128)}, f32[4,5,16,256]{3,2,1,0:T(8,128)}, f32[4,16,8,256]{3,2,1,0:T(8,128)}, f32[4,16...) custom-call(f32[16,16,256]{2,1,0:T(8,128)} %m.1, f32[16,16,256]{2,1,0:T(8,128)} %r.1, f32[16,16,256]{2,1,0:T(8,128)} %u.1, ...), custom_call_target="tpu_custom_call" | custom-call | tf_op jit(solution)/shard_map/prep/pallas_call | solution.py:478
  3.6 2.1 %collective-permute-start.1 = (f32[4,5,16,256]{3,2,1,0:T(8,128)}, f32[4,5,16,256]{3,2,1,0:T(8,128)S(1)}, u32[]{:S(2)}, u32[]{:S(2)}) collective-permute-start(f32[4,5,16,256]{3,2,1,0:T(8,128)} %get-tuple-element.19), channel_id=1, source_target_pairs={{0,16},{16,32},{32,48},{48,64},{64,80},{80,96},{96,112},{112,128},... | collective-permute-start | bytes 983048 | tf_op jit(solution)/shard_map/ppermute | solution.py:466
  5.7 3.6 %collective-permute-start.3 = (f32[4,5,16,256]{3,2,1,0:T(8,128)}, f32[4,5,16,256]{3,2,1,0:T(8,128)S(1)}, u32[]{:S(2)}, u32[]{:S(2)}) collective-permute-start(f32[4,5,16,256]{3,2,1,0:T(8,128)} %get-tuple-element.20), channel_id=1, source_target_pairs={{0,240},{16,0},{32,16},{48,32},{64,48},{80,64},{96,80},{112,96},{1... | collective-permute-start | bytes 983048 | tf_op jit(solution)/shard_map/ppermute | solution.py:466
  9.4 1.6 collective-permute-start.5
  11.0 3.9 %collective-permute-start.7 = (f32[4,16,8,256]{3,2,1,0:T(8,128)}, f32[4,16,8,256]{3,2,1,0:T(8,128)S(1)}, u32[]{:S(2)}, u32[]{:S(2)}) collective-permute-start(f32[4,16,8,256]{3,2,1,0:T(8,128)} %get-tuple-element.22), channel_id=1, source_target_pairs={{0,14},{2,0},{4,2},{6,4},{8,6},{10,8},{12,10},{14,12},{1,15},{3,1}... | collective-permute-start | bytes 1572872 | tf_op jit(solution)/shard_map/ppermute | solution.py:466
  15.0 1.4 collective-permute-start
  16.3 1.9 %collective-permute-start.2 = (f32[4,5,16,256]{3,2,1,0:T(8,128)S(1)}, f32[4,5,16,256]{3,2,1,0:T(8,128)S(1)}, u32[]{:S(2)}, u32[]{:S(2)}) collective-permute-start(f32[4,5,16,256]{3,2,1,0:T(8,128)S(1)} %collective-permute-done.1.xlo), channel_id=1, source_target_pairs={{0,1},{1,0},{2,3},{3,2},{4,5},{5,4},{6,7},{7,6},{8,9},{9,8},{10,11... | collective-permute-start | bytes 983048 | tf_op jit(solution)/shard_map/ppermute | solution.py:470
  18.4 1.7 %collective-permute-start.9 = (f32[4,10,8,256]{3,2,1,0:T(8,128)S(1)}, f32[4,10,8,256]{3,2,1,0:T(8,128)}, u32[]{:S(2)}, u32[]{:S(2)}) collective-permute-start(f32[4,10,8,256]{3,2,1,0:T(8,128)S(1)} %pad_maximum_fusion), channel_id=1, source_target_pairs={{0,2},{2,4},{4,6},{6,8},{8,10},{10,12},{12,14},{14,0},{1,3},{3,5},... | collective-permute-start | bytes 983048 | tf_op jit(solution)/shard_map/ppermute | solution.py:466
  20.1 6.3 %collective-permute-done.5.ylo = f32[4,16,8,256]{3,2,1,0:T(8,128)S(1)} collective-permute-done((f32[4,16,8,256]{3,2,1,0:T(8,128)}, f32[4,16,8,256]{3,2,1,0:T(8,128)S(1)}, u32[]{:S(2)}, u32[]{:S(2)}) %collective-permute-start.5) | collective-permute-done | bytes 524320 | tf_op jit(solution)/shard_map/ppermute | solution.py:466
  27.6 3.8 %collective-permute-start.4 = (f32[4,5,16,256]{3,2,1,0:T(8,128)S(1)}, f32[4,5,16,256]{3,2,1,0:T(8,128)S(1)}, u32[]{:S(2)}, u32[]{:S(2)}) collective-permute-start(f32[4,5,16,256]{3,2,1,0:T(8,128)S(1)} %collective-permute-done.3.xhi), channel_id=1, source_target_pairs={{0,1},{1,0},{2,3},{3,2},{4,5},{5,4},{6,7},{7,6},{8,9},{9,8},{10,11... | collective-permute-start | bytes 983048 | tf_op jit(solution)/shard_map/ppermute | solution.py:470
  31.5 2.0 %collective-permute-done.9.clo = f32[4,10,8,256]{3,2,1,0:T(8,128)} collective-permute-done((f32[4,10,8,256]{3,2,1,0:T(8,128)S(1)}, f32[4,10,8,256]{3,2,1,0:T(8,128)}, u32[]{:S(2)}, u32[]{:S(2)}) %collective-permute-start.9) | collective-permute-done | bytes 327712 | tf_op jit(solution)/shard_map/ppermute | solution.py:466
  33.5 1.7 collective-permute-start.8
  35.2 1.4 collective-permute-start.10
  40.4 24.8 %fine.1 = (f32[16,16,256]{2,1,0:T(8,128)}, f32[26,32,512]{2,1,0:T(8,128)}, f32[26,32,512]{2,1,0:T(8,128)}, f32[26,32,512]{2,1,0:T(8,128)}, f32[2,8,8,256]{3,2,1,0:T(8,128)}) custom-call(s32[5]{0:T(128)} %stack.15.place.refs_0_, f32[4,16,16,256]{3,2,1,0:T(8,128)} %get-tuple-element.18.own, f32[4,16,16,256]{3,2,1,0:T(8,128)} %copy-done.5, ...), custom_call_target="tpu_custom_call" | custom-call | tf_op jit(solution)/shard_map/fine/pallas_call | solution.py:501
  65.2 2.9 %collective-permute-start.14 = (f32[2,8,8,256]{3,2,1,0:T(8,128)}, f32[2,8,8,256]{3,2,1,0:T(8,128)S(1)}, u32[]{:S(2)}, u32[]{:S(2)}) collective-permute-start(f32[2,8,8,256]{3,2,1,0:T(8,128)} %get-tuple-element.25), channel_id=1, source_target_pairs={{0,14},{2,0},{4,2},{6,4},{8,6},{10,8},{12,10},{14,12},{1,15},{3,1}... | collective-permute-start | bytes 393224 | tf_op jit(solution)/shard_map/ppermute | solution.py:466
  68.1 3.5 %collective-permute-done.13 = f32[2,8,8,256]{3,2,1,0:T(8,128)S(1)} collective-permute-done((f32[2,8,8,256]{3,2,1,0:T(8,128)}, f32[2,8,8,256]{3,2,1,0:T(8,128)S(1)}, u32[]{:S(2)}, u32[]{:S(2)}) %collective-permute-start.13) | collective-permute-done | bytes 131104 | tf_op jit(solution)/shard_map/ppermute | solution.py:466
  72.6 1.3 collective-permute-start.16
  74.4 5.0 %collective-permute-done.16.high = f32[2,5,24,256]{3,2,1,0:T(8,128)S(1)} collective-permute-done((f32[2,5,24,256]{3,2,1,0:T(8,128)S(1)}, f32[2,5,24,256]{3,2,1,0:T(8,128)S(1)}, u32[]{:S(2)}, u32[]{:S(2)}) %collective-permute-start.16) | collective-permute-done | bytes 245792 | tf_op jit(solution)/shard_map/ppermute | solution.py:466
  79.4 3.9 %collective-permute-done.15.low = f32[2,5,24,256]{3,2,1,0:T(8,128)S(1)} collective-permute-done((f32[2,5,24,256]{3,2,1,0:T(8,128)S(1)}, f32[2,5,24,256]{3,2,1,0:T(8,128)S(1)}, u32[]{:S(2)}, u32[]{:S(2)}) %collective-permute-start.15) | collective-permute-done | bytes 245792 | tf_op jit(solution)/shard_map/ppermute | solution.py:466
  83.9 6.1 %middle.1 = (f32[18,24,256]{2,1,0:T(8,128)}, f32[18,24,256]{2,1,0:T(8,128)}, f32[18,24,256]{2,1,0:T(8,128)}, f32[128,16,128]{2,1,0:T(8,128)}) custom-call(s32[5]{0:T(128)} %stack.15.place.refs_0_, f32[2,5,24,256]{3,2,1,0:T(8,128)} %copy-done.12, f32[2,8,24,256]{3,2,1,0:T(8,128)} %copy-done.1, f32[2,5,24,256]{3,2,1,0:T(8,128)} %copy-done.11), custom_call_target="tpu_custom_call" | custom-call | tf_op jit(solution)/shard_map/middle/pallas_call | solution.py:515
  90.1 36.9 %all_to_all.5.refs_1_ = f32[128,16,128]{2,1,0:T(8,128)S(1)} all-to-all(f32[128,16,128]{2,1,0:T(8,128)} %get-tuple-element.26), channel_id=1, replica_groups=mesh['gx'=16,'gy'=8,'gz'=2] {'gx','gy'}, dimensions={0} | all-to-all | bytes 2097152 | tf_op jit(solution)/shard_map/all_to_all | solution.py:524
  126.9 3.9 %collective-permute-start.17 = (f32[128,16,128]{2,1,0:T(8,128)S(1)}, f32[128,16,128]{2,1,0:T(8,128)S(1)}, u32[]{:S(2)}, u32[]{:S(2)}) collective-permute-start(f32[128,16,128]{2,1,0:T(8,128)S(1)} %all_to_all.5.refs_1_), channel_id=1, source_target_pairs={{0,1},{1,0},{2,3},{3,2},{4,5},{5,4},{6,7},{7,6},{8,9},{9,8},{10,11... | collective-permute-start | bytes 3145736 | tf_op jit(solution)/shard_map/ppermute | solution.py:470
  130.9 2.3 %collective-permute-done.17.refs_2_ = f32[128,16,128]{2,1,0:T(8,128)S(1)} collective-permute-done((f32[128,16,128]{2,1,0:T(8,128)S(1)}, f32[128,16,128]{2,1,0:T(8,128)S(1)}, u32[]{:S(2)}, u32[]{:S(2)}) %collective-permute-start.17) | collective-permute-done | bytes 1048608 | tf_op jit(solution)/shard_map/ppermute | solution.py:470
  134.1 36.2 %up.1 = f32[16,16,256]{2,1,0:T(8,128)} custom-call(s32[5]{0:T(128)} %stack.15.place.refs_0_, f32[128,16,128]{2,1,0:T(8,128)} %copy-done, f32[128,16,128]{2,1,0:T(8,128)} %copy-done.4, f32[18,24,256]{2,1,0:T(8,128)} %get-tuple-element.27.refs_3_, f32[18,24,256]{2,1,0:T(8,128)} %get-tuple-element.28.refs_4_, f32[18,24,256]{2,1,0:T(8,128)} %get-tuple-element.29.refs_5_, ...), custom_call_target="tpu_custom_call" | custom-call | tf_op jit(solution)/shard_map/up/pallas_call | solution.py:528
  (52 shorter events, 8.3 us)
Async XLA Ops:
  3.6 12.7 %collective-permute-start.1 = (f32[4,5,16,256]{3,2,1,0:T(8,128)}, f32[4,5,16,256]{3,2,1,0:T(8,128)S(1)}, u32[]{:S(2)}, u32[]{:S(2)}) collective-permute-start(f32[4,5,16,256]{3,2,1,0:T(8,128)} %get-tuple-element.19), channel_id=1, source_target_pairs={{0,16},{16,32},{32,48},{48,64},{64,80},{80,96},{96,112},{112,128},... | collective-permute-start | bytes 983048 | tf_op jit(solution)/shard_map/ppermute | solution.py:466
  5.7 12.5 %collective-permute-start.3 = (f32[4,5,16,256]{3,2,1,0:T(8,128)}, f32[4,5,16,256]{3,2,1,0:T(8,128)S(1)}, u32[]{:S(2)}, u32[]{:S(2)}) collective-permute-start(f32[4,5,16,256]{3,2,1,0:T(8,128)} %get-tuple-element.20), channel_id=1, source_target_pairs={{0,240},{16,0},{32,16},{48,32},{64,48},{80,64},{96,80},{112,96},{1... | collective-permute-start | bytes 983048 | tf_op jit(solution)/shard_map/ppermute | solution.py:466
  9.4 17.0 %collective-permute-start.5 = (f32[4,16,8,256]{3,2,1,0:T(8,128)}, f32[4,16,8,256]{3,2,1,0:T(8,128)S(1)}, u32[]{:S(2)}, u32[]{:S(2)}) collective-permute-start(f32[4,16,8,256]{3,2,1,0:T(8,128)} %get-tuple-element.21), channel_id=1, source_target_pairs={{0,2},{2,4},{4,6},{6,8},{8,10},{10,12},{12,14},{14,0},{1,3},{3,5},... | collective-permute-start | bytes 1572872 | tf_op jit(solution)/shard_map/ppermute | solution.py:466
  11.0 16.5 %collective-permute-start.7 = (f32[4,16,8,256]{3,2,1,0:T(8,128)}, f32[4,16,8,256]{3,2,1,0:T(8,128)S(1)}, u32[]{:S(2)}, u32[]{:S(2)}) collective-permute-start(f32[4,16,8,256]{3,2,1,0:T(8,128)} %get-tuple-element.22), channel_id=1, source_target_pairs={{0,14},{2,0},{4,2},{6,4},{8,6},{10,8},{12,10},{14,12},{1,15},{3,1}... | collective-permute-start | bytes 1572872 | tf_op jit(solution)/shard_map/ppermute | solution.py:466
  15.0 23.7 %collective-permute-start = (f32[4,16,16,256]{3,2,1,0:T(8,128)}, f32[4,16,16,256]{3,2,1,0:T(8,128)S(1)}, u32[]{:S(2)}, u32[]{:S(2)}) collective-permute-start(f32[4,16,16,256]{3,2,1,0:T(8,128)} %get-tuple-element.18.own), channel_id=1, source_target_pairs={{0,1},{1,0},{2,3},{3,2},{4,5},{5,4},{6,7},{7,6},{8,9},{9,8},{10,11... | collective-permute-start | bytes 3145736 | tf_op jit(solution)/shard_map/ppermute | solution.py:470
  16.3 22.4 %copy-start.2 = (f32[4,5,16,256]{3,2,1,0:T(8,128)}, f32[4,5,16,256]{3,2,1,0:T(8,128)S(1)}, u32[]{:S(2)}) copy-start(f32[4,5,16,256]{3,2,1,0:T(8,128)S(1)} %collective-permute-done.1.xlo) | copy-start | bytes 983044
  16.3 15.0 %collective-permute-start.2 = (f32[4,5,16,256]{3,2,1,0:T(8,128)S(1)}, f32[4,5,16,256]{3,2,1,0:T(8,128)S(1)}, u32[]{:S(2)}, u32[]{:S(2)}) collective-permute-start(f32[4,5,16,256]{3,2,1,0:T(8,128)S(1)} %collective-permute-done.1.xlo), channel_id=1, source_target_pairs={{0,1},{1,0},{2,3},{3,2},{4,5},{5,4},{6,7},{7,6},{8,9},{9,8},{10,11... | collective-permute-start | bytes 983048 | tf_op jit(solution)/shard_map/ppermute | solution.py:470
  18.3 20.4 %copy-start.3 = (f32[4,5,16,256]{3,2,1,0:T(8,128)}, f32[4,5,16,256]{3,2,1,0:T(8,128)S(1)}, u32[]{:S(2)}) copy-start(f32[4,5,16,256]{3,2,1,0:T(8,128)S(1)} %collective-permute-done.3.xhi) | copy-start | bytes 983044
  18.4 15.1 %collective-permute-start.9 = (f32[4,10,8,256]{3,2,1,0:T(8,128)S(1)}, f32[4,10,8,256]{3,2,1,0:T(8,128)}, u32[]{:S(2)}, u32[]{:S(2)}) collective-permute-start(f32[4,10,8,256]{3,2,1,0:T(8,128)S(1)} %pad_maximum_fusion), channel_id=1, source_target_pairs={{0,2},{2,4},{4,6},{6,8},{8,10},{10,12},{12,14},{14,0},{1,3},{3,5},... | collective-permute-start | bytes 983048 | tf_op jit(solution)/shard_map/ppermute | solution.py:466
  26.4 12.3 %copy-start.6 = (f32[4,16,8,256]{3,2,1,0:T(8,128)}, f32[4,16,8,256]{3,2,1,0:T(8,128)S(1)}, u32[]{:S(2)}) copy-start(f32[4,16,8,256]{3,2,1,0:T(8,128)S(1)} %collective-permute-done.5.ylo) | copy-start | bytes 1572868
  26.4 8.8 %collective-permute-start.11 = (f32[4,10,8,256]{3,2,1,0:T(8,128)S(1)}, f32[4,10,8,256]{3,2,1,0:T(8,128)}, u32[]{:S(2)}, u32[]{:S(2)}) collective-permute-start(f32[4,10,8,256]{3,2,1,0:T(8,128)S(1)} %pad_maximum_fusion.1), channel_id=1, source_target_pairs={{0,14},{2,0},{4,2},{6,4},{8,6},{10,8},{12,10},{14,12},{1,15},{3,1}... | collective-permute-start | bytes 983048 | tf_op jit(solution)/shard_map/ppermute | solution.py:466
  27.6 11.2 %copy-start.7 = (f32[4,16,8,256]{3,2,1,0:T(8,128)}, f32[4,16,8,256]{3,2,1,0:T(8,128)S(1)}, u32[]{:S(2)}) copy-start(f32[4,16,8,256]{3,2,1,0:T(8,128)S(1)} %collective-permute-done.7.yhi) | copy-start | bytes 1572868
  27.6 9.0 %collective-permute-start.4 = (f32[4,5,16,256]{3,2,1,0:T(8,128)S(1)}, f32[4,5,16,256]{3,2,1,0:T(8,128)S(1)}, u32[]{:S(2)}, u32[]{:S(2)}) collective-permute-start(f32[4,5,16,256]{3,2,1,0:T(8,128)S(1)} %collective-permute-done.3.xhi), channel_id=1, source_target_pairs={{0,1},{1,0},{2,3},{3,2},{4,5},{5,4},{6,7},{7,6},{8,9},{9,8},{10,11... | collective-permute-start | bytes 983048 | tf_op jit(solution)/shard_map/ppermute | solution.py:470
  31.3 7.3 %collective-permute-start.6 = (f32[4,16,8,256]{3,2,1,0:T(8,128)S(1)}, f32[4,16,8,256]{3,2,1,0:T(8,128)S(1)}, u32[]{:S(2)}, u32[]{:S(2)}) collective-permute-start(f32[4,16,8,256]{3,2,1,0:T(8,128)S(1)} %collective-permute-done.5.ylo), channel_id=1, source_target_pairs={{0,1},{1,0},{2,3},{3,2},{4,5},{5,4},{6,7},{7,6},{8,9},{9,8},{10,11... | collective-permute-start | bytes 1572872 | tf_op jit(solution)/shard_map/ppermute | solution.py:470
  33.5 5.2 %collective-permute-start.8 = (f32[4,16,8,256]{3,2,1,0:T(8,128)S(1)}, f32[4,16,8,256]{3,2,1,0:T(8,128)}, u32[]{:S(2)}, u32[]{:S(2)}) collective-permute-start(f32[4,16,8,256]{3,2,1,0:T(8,128)S(1)} %collective-permute-done.7.yhi), channel_id=1, source_target_pairs={{0,1},{1,0},{2,3},{3,2},{4,5},{5,4},{6,7},{7,6},{8,9},{9,8},{10,11... | collective-permute-start | bytes 1572872 | tf_op jit(solution)/shard_map/ppermute | solution.py:470
  35.2 3.0 %collective-permute-start.10 = (f32[4,10,8,256]{3,2,1,0:T(8,128)}, f32[4,10,8,256]{3,2,1,0:T(8,128)}, u32[]{:S(2)}, u32[]{:S(2)}) collective-permute-start(f32[4,10,8,256]{3,2,1,0:T(8,128)} %collective-permute-done.9.clo), channel_id=1, source_target_pairs={{0,1},{1,0},{2,3},{3,2},{4,5},{5,4},{6,7},{7,6},{8,9},{9,8},{10,11... | collective-permute-start | bytes 983048 | tf_op jit(solution)/shard_map/ppermute | solution.py:470
  36.6 2.1 %collective-permute-start.12 = (f32[4,10,8,256]{3,2,1,0:T(8,128)}, f32[4,10,8,256]{3,2,1,0:T(8,128)}, u32[]{:S(2)}, u32[]{:S(2)}) collective-permute-start(f32[4,10,8,256]{3,2,1,0:T(8,128)} %collective-permute-done.11.chi), channel_id=1, source_target_pairs={{0,1},{1,0},{2,3},{3,2},{4,5},{5,4},{6,7},{7,6},{8,9},{9,8},{10,11... | collective-permute-start | bytes 983048 | tf_op jit(solution)/shard_map/ppermute | solution.py:470
  65.2 6.4 %collective-permute-start.13 = (f32[2,8,8,256]{3,2,1,0:T(8,128)}, f32[2,8,8,256]{3,2,1,0:T(8,128)S(1)}, u32[]{:S(2)}, u32[]{:S(2)}) collective-permute-start(f32[2,8,8,256]{3,2,1,0:T(8,128)} %get-tuple-element.25), channel_id=1, source_target_pairs={{0,2},{2,4},{4,6},{6,8},{8,10},{10,12},{12,14},{14,0},{1,3},{3,5},... | collective-permute-start | bytes 393224 | tf_op jit(solution)/shard_map/ppermute | solution.py:466
  65.2 7.4 %collective-permute-start.14 = (f32[2,8,8,256]{3,2,1,0:T(8,128)}, f32[2,8,8,256]{3,2,1,0:T(8,128)S(1)}, u32[]{:S(2)}, u32[]{:S(2)}) collective-permute-start(f32[2,8,8,256]{3,2,1,0:T(8,128)} %get-tuple-element.25), channel_id=1, source_target_pairs={{0,14},{2,0},{4,2},{6,4},{8,6},{10,8},{12,10},{14,12},{1,15},{3,1}... | collective-permute-start | bytes 393224 | tf_op jit(solution)/shard_map/ppermute | solution.py:466
  72.6 10.6 %copy-start.1 = (f32[2,8,24,256]{3,2,1,0:T(8,128)}, f32[2,8,24,256]{3,2,1,0:T(8,128)S(1)}, u32[]{:S(2)}) copy-start(f32[2,8,24,256]{3,2,1,0:T(8,128)S(1)} %constant_dynamic-update-slice_fusion.own) | copy-start | bytes 1179652
  72.6 6.7 %collective-permute-start.16 = (f32[2,5,24,256]{3,2,1,0:T(8,128)S(1)}, f32[2,5,24,256]{3,2,1,0:T(8,128)S(1)}, u32[]{:S(2)}, u32[]{:S(2)}) collective-permute-start(f32[2,5,24,256]{3,2,1,0:T(8,128)S(1)} %get-tuple-element.33), channel_id=1, source_target_pairs={{0,240},{16,0},{32,16},{48,32},{64,48},{80,64},{96,80},{112,96},{1... | collective-permute-start | bytes 737288 | tf_op jit(solution)/shard_map/ppermute | solution.py:466
  73.9 9.3 %collective-permute-start.15 = (f32[2,5,24,256]{3,2,1,0:T(8,128)S(1)}, f32[2,5,24,256]{3,2,1,0:T(8,128)S(1)}, u32[]{:S(2)}, u32[]{:S(2)}) collective-permute-start(f32[2,5,24,256]{3,2,1,0:T(8,128)S(1)} %get-tuple-element.34), channel_id=1, source_target_pairs={{0,16},{16,32},{32,48},{48,64},{64,80},{80,96},{96,112},{112,128},... | collective-permute-start | bytes 737288 | tf_op jit(solution)/shard_map/ppermute | solution.py:466
  126.9 6.2 %copy-start = (f32[128,16,128]{2,1,0:T(8,128)}, f32[128,16,128]{2,1,0:T(8,128)S(1)}, u32[]{:S(2)}) copy-start(f32[128,16,128]{2,1,0:T(8,128)S(1)} %all_to_all.5.refs_1_) | copy-start | bytes 3145732
  126.9 6.2 %collective-permute-start.17 = (f32[128,16,128]{2,1,0:T(8,128)S(1)}, f32[128,16,128]{2,1,0:T(8,128)S(1)}, u32[]{:S(2)}, u32[]{:S(2)}) collective-permute-start(f32[128,16,128]{2,1,0:T(8,128)S(1)} %all_to_all.5.refs_1_), channel_id=1, source_target_pairs={{0,1},{1,0},{2,3},{3,2},{4,5},{5,4},{6,7},{7,6},{8,9},{9,8},{10,11... | collective-permute-start | bytes 3145736 | tf_op jit(solution)/shard_map/ppermute | solution.py:470
  (7 other events, 13.3 us)

commit v2 on v0

v2 whole, which is shorter than its diff:
```python
import jax
import jax.numpy as jnp
from jax import lax
from jax.experimental import pallas as pl
from jax.experimental.pallas import tpu as pltpu
from jax.sharding import PartitionSpec as P

TIME_STEP = 0.05
IONIC_GAIN = 8.0
IONIC_ONSET = 0.15
RECOVERY_RATE = 0.01
COARSE_SWEEPS = 8

F32 = jnp.float32
BX, BY, BZ = 16, 16, 256
H = 3
K0, Y0, Z0 = BX // 2 + 2 * H, 32, 384
K1, Y1, Z1 = BX // 4 + 2 * H, 24, BZ
Z2 = BZ // 2
VMEM = pl.BlockSpec(memory_space=pltpu.VMEM)
HBM = pl.BlockSpec(memory_space=pltpu.HBM)


def params(mib):
    return pltpu.CompilerParams(vmem_limit_bytes=mib * 1024 * 1024)


def iota(shape, dim):
    return lax.broadcasted_iota(jnp.int32, shape, dim)


def first_is_red(shape):
    return ((iota(shape, len(shape) - 2) + iota(shape, len(shape) - 1)) & 1) == 0


def up(x, axis):
    return pltpu.roll(x, x.shape[axis] - 1, axis)


def down(x, axis):
    return pltpu.roll(x, 1, axis)


def pair_matrix(rows, cols, value, shift=0):
    return jnp.where(
        iota((rows, cols), 0) // 2 + shift == iota((rows, cols), 1), value, 0.0
    ).astype(F32)


def copy_matrix(rows, cols, shift=0):
    return jnp.where(
        iota((rows, cols), 1) // 2 + shift == iota((rows, cols), 0), 1.0, 0.0
    ).astype(F32)


def dot(a, b):
    return jnp.dot(a, b, precision=lax.Precision.HIGHEST, preferred_element_type=F32)


def sum_rows(buf, x):
    rows, cols = x.shape
    sums = []
    for c in range(cols // 128):
        buf[c, 0:rows, :] = x[:, 128 * c : 128 * c + 128]
        sums.append(buf[c, pl.ds(0, rows // 2, 2), :] + buf[c, pl.ds(1, rows // 2, 2), :])
    return sums[0] if len(sums) == 1 else jnp.concatenate(sums, axis=1)


def twice_rows(buf, x):
    rows, cols = x.shape
    for c in range(cols // 128):
        for k in (0, 1):
            buf[c, pl.ds(k, rows, 2), :] = x[:, 128 * c : 128 * c + 128]


def columns(buf, start, rows, cols):
    parts = [buf[c, pl.ds(start, rows), :] for c in range(cols // 128)]
    return parts[0] if len(parts) == 1 else jnp.concatenate(parts, axis=1)


def loop(start, stop, step, body):
    def run(index, carry):
        body(start + index * step)
        return carry

    lax.fori_loop(0, (stop - start) // step, run, 0)


def far(other, k, step, red, first):
    before, after = other[pl.ds(k - 1, step)], other[pl.ds(k + 1, step)]
    return jnp.where(first, before, after) if red else jnp.where(first, after, before)


def faces(inner, outer, near, fars, ys, zs, diag, inv, least, start, stop, step):
    rows, lanes = inner[0].shape[1:]
    shape = (step, rows, lanes)
    row, lane = iota(shape, 1), iota(shape, 2)
    first = first_is_red(shape)

    def body(k):
        here = pl.ds(k, step)
        low = jnp.minimum(inner[0][here], inner[1][here])
        if least is not None:
            least[0][here] = low
        halves = [0.5 * outer[c][here] for c in (0, 1)]
        pair = low + halves[0] + halves[1]
        near[here] = pair
        totals = [pair, pair]
        for axis, out, keep, place, size in (
            (1, ys, None if least is None else least[2], row, rows),
            (2, zs, None if least is None else least[3], lane, lanes),
        ):
            full = []
            for c in (0, 1):
                o = 1 - c
                mine = inner[c][here]
                low = jnp.where(place < size - 1, jnp.minimum(mine, up(inner[o][here], axis)), 0.0)
                if keep is not None:
                    keep[c][here] = low
                both = low + halves[c] + jnp.where(place < size - 1, up(halves[o], axis), 0.0)
                full.append(both)
                out[c][here] = jnp.where(place < size - 1, both, 0.0)
            for c in (0, 1):
                below = jnp.where(place > 0, down(full[1 - c], axis), halves[c])
                totals[c] = totals[c] + full[c] + below
        for c in (0, 1):
            o = 1 - c
            low = jnp.minimum(inner[c][here], far(inner[o], k, step, c == 0, first))
            if least is not None:
                least[1][c][here] = low
            both = low + halves[c] + 0.5 * far(outer[o], k, step, c == 0, first)
            fars[c][here] = both
            total = totals[c] + both
            if c == 0 and diag is not None:
                diag[here] = total
            inside = outer[c][here] > 0.0
            inv[c][here] = jnp.where(inside, 1.0 / jnp.where(inside, total, 1.0), 0.0)

    loop(start, stop, step, body)


def gathered(v, c, near, fars, ys, zs, k, step, first):
    here = pl.ds(k, step)
    o = 1 - c
    other = v[o][here]
    total = near[here] * other + fars[c][here] * far(v[o], k, step, c == 0, first)
    total = total + ys[c][here] * up(other, 1) + down(ys[o][here] * other, 1)
    return total + zs[c][here] * up(other, 2) + down(zs[o][here] * other, 2)


def half_sweep(v, b, c, coef, inv, start, stop, step):
    first = first_is_red((step,) + tuple(v[0].shape[1:]))

    def body(k):
        here = pl.ds(k, step)
        v[c][here] = (b[c][here] + gathered(v, c, *coef, k, step, first)) * inv[c][here]

    loop(start, stop, step, body)


def from_zero(v, b, coef, inv, start, stop, step):
    count = v[0].shape[0]
    for c in (0, 1):
        v[c][0:1] = jnp.zeros_like(v[c][0:1])
        v[c][count - 1 :] = jnp.zeros_like(v[c][0:1])

    def body(k):
        here = pl.ds(k, step)
        v[0][here] = b[0][here] * inv[0][here]

    loop(start, stop, step, body)
    half_sweep(v, b, 1, coef, inv, start, stop, step)


def put(bufs, k, rows, lanes, a, b):
    some = a if b is None else b
    a = jnp.zeros_like(some) if a is None else a
    b = jnp.zeros_like(some) if b is None else b
    first = first_is_red(some.shape)
    bufs[0][k, rows, lanes] = jnp.where(first, a, b)
    bufs[1][k, rows, lanes] = jnp.where(first, b, a)


def colours(x):
    n = x.shape[0] // 2
    first = first_is_red(x.shape[1:])
    pairs = [(x[2 * p], x[2 * p + 1]) for p in range(n)]
    return (
        jnp.stack([jnp.where(first, a, b) for a, b in pairs]),
        jnp.stack([jnp.where(first, b, a) for a, b in pairs]),
    )


def where_am_i():
    return lax.axis_index("gx"), lax.axis_index("gy"), lax.axis_index("gz")


def flags():
    gx, gy, _ = where_am_i()
    return (
        (gx > 0).astype(F32),
        (gx < lax.axis_size("gx") - 1).astype(F32),
        (gy > 0).astype(F32),
        (gy < lax.axis_size("gy") - 1).astype(F32),
    )


def fetch(pairs, sems):
    copies = [pltpu.make_async_copy(src, dst, sems.at[i]) for i, (src, dst) in enumerate(pairs)]
    for copy in copies:
        copy.start()
    return copies


def outside(shape, own_rows, k, own, has):
    row = iota(shape, len(shape) - 2)
    in_y = jnp.where(row < 8, has[2], jnp.where(row < 8 + own_rows, 1.0, has[3]))
    return in_y * jnp.where(k < H, has[0], jnp.where(k < H + own, 1.0, has[1]))


def block_of(i):
    rows, lanes = 8 * ((i % 4) // 2), 128 * (i % 2)
    return i // 4, slice(rows, rows + 8), slice(lanes, lanes + 128)


def block_of24(i):
    tile, half = (i % 6) // 2, i % 2
    return i // 6, slice(8 * tile, 8 * tile + 8), slice(128 * half, 128 * half + 128)


def prep_kernel(
    m_in, r_in, u_in, f_in, labels_in, own, xup, xdn, yup, ydn, m, r, u, f, labels, fold, sems
):
    copies = fetch(
        [(labels_in, labels), (m_in, m), (u_in, u), (r_in, r), (f_in, f)], sems
    )
    for copy in copies:
        copy.wait()
    spread = jnp.where(iota((BZ // 8, BZ), 1) // 8 == iota((BZ // 8, BZ), 0), 1.0, 0.0).astype(F32)
    for bx in range(BX // 8):
        wide = jnp.dot(labels[bx].astype(F32), spread, preferred_element_type=F32)
        kind = jnp.concatenate(
            [jnp.broadcast_to(wide[by : by + 1], (8, BZ)) for by in range(BY // 8)], axis=0
        )
        factor = jnp.where(kind > 1.5, 0.3, jnp.where(kind > 0.5, 1.0, 0.0)).astype(F32)
        for x in range(8 * bx, 8 * bx + 8):
            mm, rr, uu = m[x], r[x], u[x]
            inner = factor * f[x]
            own[x] = mm + uu
            own[BX + x] = inner
            ionic = IONIC_GAIN * mm * (mm - IONIC_ONSET) * (mm - 1.0) + mm * rr
            own[2 * BX + x] = mm - jnp.where(kind > 0.5, TIME_STEP * ionic, 0.0)
            own[3 * BX + x] = uu
    sums = jnp.concatenate(
        [own[BX + 2 * p] + own[BX + 2 * p + 1] for p in range(BX // 2)], axis=0
    )
    mean = sum_rows(fold, dot(sums, pair_matrix(BZ, BZ // 2, 0.125)))
    for i in range(8):
        slab, rows, lanes = block_of(i)
        own[4 * BX + slab, rows, lanes] = mean[8 * i : 8 * i + 8]
        slab, rows, lanes = block_of24(i)
        yup[BX + slab, rows, lanes] = mean[8 * i : 8 * i + 8]
        ydn[BX + slab, rows, lanes] = mean[8 * i : 8 * i + 8]
    for i in range(5):
        slab, rows, lanes = block_of(i)
        xup[18 + slab, rows, lanes] = mean[8 * (3 + i) : 8 * (4 + i)]
        xdn[18 + slab, rows, lanes] = mean[8 * i : 8 * i + 8]
    base = 0
    for q, depth in enumerate((5, 5, 4, 4)):
        xup[base : base + depth] = own[BX * (q + 1) - depth : BX * (q + 1)]
        xdn[base : base + depth] = own[BX * q : BX * q + depth]
        base += depth
    row = iota((8, BZ), 0)
    for x in range(BX):
        for q in (0, 1):
            yup[x, 8 * q : 8 * q + 8] = own[BX * q + x, 8:16]
            ydn[x, 8 * q : 8 * q + 8] = own[BX * q + x, 0:8]
        w, v = own[2 * BX + x], own[3 * BX + x]
        yup[x, 16:24] = merge(True, w[8:16], v[8:16])
        ydn[x, 16:24] = merge(False, w[0:8], v[0:8])


def merge(high, a, b):
    row = iota(a.shape, 0)
    return jnp.where(row >= 4, a, pltpu.roll(b, 4, 0)) if high else jnp.where(
        row < 4, a, pltpu.roll(b, 4, 0)
    )


def corner_kernel(xlo, xhi, cup, cdn):
    for high, out in ((True, cup), (False, cdn)):
        rows = slice(8, 16) if high else slice(0, 8)
        for side, src in ((0, xlo), (1, xhi)):
            at = lambda base, depth, d: src[base + (depth - d if side == 0 else d - 1), rows]
            s, n, w, u = (
                lambda d: at(0, 5, d),
                lambda d: at(5, 5, d),
                lambda d: at(10, 4, d),
                lambda d: at(14, 4, d),
            )
            tiles = [
                merge(high, s(1), s(2)),
                merge(high, s(3), s(4)),
                merge(high, n(1), n(2)),
                merge(high, n(3), n(4)),
                merge(high, w(1), w(2)),
                merge(high, u(1), u(2)),
                merge(high, w(3), u(3)),
            ]
            for t, tile in enumerate(tiles):
                out[10 * side + t] = tile

            def coarse(d):
                slab, block_rows, lanes = block_of(5 - d if side == 0 else d - 1)
                return src[18 + slab, block_rows, lanes]

            for d in range(1, 6):
                tile, lanes = 10 * side + 7 + (d - 1) // 2, 128 * ((d - 1) % 2)
                out[tile, :, lanes : lanes + 128] = coarse(d)


def fine_kernel(*refs):
    pieces, refs = refs[:14], refs[14:]
    mnext, rhs1, refs = refs[0], refs[1], refs[2:]
    mean1, refs = refs[0:2], refs[2:]
    v, b, near, fars, ys, zs, inv, refs = (
        refs[0:2], refs[2:4], refs[4], refs[5:7], refs[7:9], refs[9:11], refs[11:13], refs[13:],
    )
    inner, outer, s, w, refs = refs[0:2], refs[2:4], refs[4:6], refs[6:8], refs[8:]
    low_near, low_far, low_y, low_z, diag, fold, fold2 = (
        refs[0], refs[1:3], refs[3:5], refs[5:7], refs[7], refs[8], refs[9],
    )
    mout, sems = refs[10], refs[11]
    core = lax.axis_index("gz")
    has = flags()
    fields = (s, inner, w, v)
    for side in (0, 1):
        own, xlo, xhi, ylo, yhi, clo, chi = pieces[side::2]
        wide = BZ if side == 0 else 128
        src = pl.ds(0 if side == 0 else pl.multiple_of(core * 128, 128), wide)
        dst = pl.ds(pl.multiple_of(core * 128 if side == 0 else (1 - core) * 256, 128), wide)
        mid, low, high = slice(8, 24), slice(0, 8), slice(24, 32)

        def body(p, own=own, ylo=ylo, yhi=yhi, src=src, dst=dst):
            k = p + H
            for q, bufs in enumerate(fields):
                put(bufs, k, mid, dst, own[BX * q + 2 * p, :, src], own[BX * q + 2 * p + 1, :, src])
            for rows, ref, flag in ((low, ylo, has[2]), (high, yhi, has[3])):
                for q in (0, 1):
                    part = slice(8 * q, 8 * q + 8)
                    put(
                        fields[q], k, rows, dst,
                        ref[2 * p, part, src] * flag, ref[2 * p + 1, part, src] * flag,
                    )
                a, c = (ref[2 * p + i, 16:24, src] * flag for i in (0, 1))
                put(w, k, rows, dst, a, c)
                put(v, k, rows, dst, pltpu.roll(a, 4, 0), pltpu.roll(c, 4, 0))

        loop(0, BX // 2, 1, body)
        for x_side, ref, flag in ((0, xlo, has[0]), (1, xhi, has[1])):
            base = 0
            order = (5, 4, 3, 2, 1) if x_side == 0 else (1, 2, 3, 4, 5)
            for q, depth in enumerate((5, 5, 4, 4)):
                slabs = {d: ref[base + i, :, src] * flag for i, d in enumerate(
                    [d for d in order if d <= depth])}
                base += depth
                for j in range(H):
                    near_d, far_d = 2 * j + 1, 2 * j + 2
                    pair = (slabs.get(near_d), slabs.get(far_d))
                    k = H - 1 - j if x_side == 0 else K0 - H + j
                    if x_side == 0:
                        pair = pair[::-1]
                    if pair[0] is None and pair[1] is None:
                        pair = (jnp.zeros((16, wide), F32), None)
                    put(fields[q], k, mid, dst, *pair)
            for rows, cref, yflag in ((low, clo, has[2]), (high, chi, has[3])):
                both = flag * yflag
                tile = [cref[10 * x_side + t, :, src] * both for t in range(7)]
                turned = [pltpu.roll(t, 4, 0) for t in tile]
                zero = jnp.zeros((8, wide), F32)
                by_field = (
                    (tile[0], turned[0], tile[1], turned[1]),
                    (tile[2], turned[2], tile[3], turned[3]),
                    (tile[4], turned[4], tile[6], zero),
                    (tile[5], turned[5], turned[6], zero),
                )
                for q in range(4):
                    slabs = by_field[q] + (zero, zero)
                    for j in range(H):
                        pair = (slabs[2 * j], slabs[2 * j + 1])
                        k = H - 1 - j if x_side == 0 else K0 - H + j
                        put(fields[q], k, rows, dst, *(pair[::-1] if x_side == 0 else pair))
        dst = pl.ds(pl.multiple_of((core if side == 0 else 1 - core) * 128, 128), 128)
        for p in range(4):
            def of_own(i):
                slab, rows, lanes = block_of(i)
                return own[4 * BX + slab, rows, lanes]

            put(mean1, p + H, slice(8, 16), dst, of_own(2 * p), of_own(2 * p + 1))
            for rows, ref, flag in ((slice(0, 8), ylo, has[2]), (slice(16, 24), yhi, has[3])):
                def of_y(i):
                    slab, part, lanes = block_of24(i)
                    return ref[BX + slab, part, lanes] * flag

                put(mean1, p + H, rows, dst, of_y(2 * p), of_y(2 * p + 1))
        for x_side, ref, flag in ((0, xlo, has[0]), (1, xhi, has[1])):
            def of_x(d):
                slab, part, lanes = block_of(5 - d if x_side == 0 else d - 1)
                return ref[18 + slab, part, lanes] * flag

            zero = jnp.zeros((8, 128), F32)
            mids = [of_x(d) for d in (1, 2, 3, 4, 5)] + [zero]
            columns_of = [(slice(8, 16), mids)]
            for rows, cref, yflag in ((slice(0, 8), clo, has[2]), (slice(16, 24), chi, has[3])):
                t = [
                    cref[10 * x_side + 7 + i // 2, :, 128 * (i % 2) : 128 * (i % 2) + 128]
                    * (flag * yflag)
                    for i in range(5)
                ]
                columns_of.append((rows, t + [zero]))
            for rows, slabs in columns_of:
                for j in range(H):
                    pair = (slabs[2 * j], slabs[2 * j + 1])
                    k = H - 1 - j if x_side == 0 else K1 - H + j
                    put(mean1, k, rows, dst, *(pair[::-1] if x_side == 0 else pair))

    def body(k):
        here = pl.ds(k, 1)
        inside = outside((1, Y0, Z0), 16, k, BX // 2, has)
        for c in (0, 1):
            outer[c][here] = jnp.where(inner[c][here] > 0.0, 1.0, 3.0 * inside)

    loop(0, K0, 1, body)
    faces(
        inner, outer, near, fars, ys, zs, diag, inv, (low_near, low_far, low_y, low_z), 1, K0 - 1, 1
    )
    first = first_is_red((1, Y0, Z0))

    def intra(x, k):
        here = pl.ds(k, 1)
        a = [x[0][here], x[1][here]]
        flow = low_near[here] * (a[1] - a[0])
        total = [flow, -flow]
        for c in (0, 1):
            total[c] = total[c] + low_far[c][here] * (far(x[1 - c], k, 1, c == 0, first) - a[c])
        for axis, low in ((1, low_y), (2, low_z)):
            flows = [low[c][here] * (up(a[1 - c], axis) - a[c]) for c in (0, 1)]
            for c in (0, 1):
                total[c] = total[c] + flows[c] - down(flows[1 - c], axis)
        return total

    def body(k):
        here = pl.ds(k, 1)
        drive = intra(s, k)
        for c in (0, 1):
            w[c][here] = w[c][here] + TIME_STEP * drive[c]

    loop(1, K0 - 1, 1, body)
    lanes = pl.ds(pl.multiple_of(core * 128, 128), BZ)
    half_first = first_is_red((BY, BZ))

    def body(p):
        a, c = w[0][p + H, 8:24, lanes], w[1][p + H, 8:24, lanes]
        mout[2 * p] = jnp.where(half_first, a, c)
        mout[2 * p + 1] = jnp.where(half_first, c, a)

    loop(0, BX // 2, 1, body)
    copies = fetch([(mout, mnext)], sems)

    def body(k):
        here = pl.ds(k, 1)
        both = intra(w, k)
        for c in (0, 1):
            b[c][here] = both[c]

    loop(1, K0 - 1, 1, body)
    coef = (near, fars, ys, zs)
    half_sweep(v, b, 0, coef, inv, 1, K0 - 1, 1)
    half_sweep(v, b, 1, coef, inv, 2, K0 - 2, 1)

    def body(p):
        here = pl.ds(p + H, 1)
        res = b[0][here] - (diag[here] * v[0][here] - gathered(v, 0, *coef, p + H, 1, first))
        fold[pl.ds(p, 1)] = res[:, 8:24, :]

    loop(0, BX // 2, 1, body)
    half = BX // 2 * BY
    pairs = pair_matrix(Z0, Z1, 0.5, core * 64)
    coarse = sum_rows(fold2, dot(fold[...].reshape(half, Z0), pairs)).reshape(8, 8, Z1)
    red, black = colours(coarse)
    rhs1[0] = red
    rhs1[1] = black
    copies[0].wait()


def middle_faces_kernel(m_in, r_in, *refs):
    inner, refs = refs[0:2], refs[2:]
    rnext, near, fars, ys, zs, diag, inv, outer = (
        refs[0], refs[1], refs[2:4], refs[4:6], refs[6:8], refs[8], refs[9:11], refs[11:13],
    )
    m, r, sems = refs[13:]
    copies = fetch([(m_in, m), (r_in, r)], sems)
    has = flags()
    for k in range(K1):
        inside = outside((Y1, Z1), 8, k, 4, has)
        for c in (0, 1):
            outer[c][k] = jnp.where(inner[c][k] > 0.0, 1.0, 3.0 * inside)
    for copy in copies:
        copy.wait()
    for x in range(BX):
        mm, rr = m[x], r[x]
        r[x] = rr + TIME_STEP * RECOVERY_RATE * (
            -rr - IONIC_GAIN * mm * (mm - IONIC_ONSET - 1.0)
        )
    copies = fetch([(r, rnext)], sems)
    faces(inner, outer, near, fars, ys, zs, diag, inv, None, 1, K1 - 1, 2)
    copies[0].wait()


def join_kernel(low, own, high, wide, xup, xdn):
    for c in (0, 1):
        for p in range(4):
            for i, ref in enumerate((low, own, high)):
                rows = slice(8 * i, 8 * i + 8)
                wide[c, p, rows] = ref[c, p]
                if p < 2:
                    xdn[c, p, rows] = ref[c, p]
                else:
                    xup[c, p - 2, rows] = ref[c, p]


def spread_kernel(got, send):
    whole = got[...]
    for d in range(send.shape[0]):
        send[d] = whole


def middle_kernel(low, own, high, *refs):
    inner, refs = refs[0:2], refs[2:]
    near, fars, ys, zs, diag, inv, refs = (
        refs[0], refs[1:3], refs[3:5], refs[5:7], refs[7], refs[8:10], refs[10:],
    )
    v, b, send, fold, fold2 = refs[0:2], refs[2:4], refs[4], refs[5], refs[6]
    core = lax.axis_index("gz")
    has = flags()
    for c in (0, 1):
        b[c][0:1] = jnp.zeros((1, Y1, Z1), F32)
        b[c][K1 - 1 :] = jnp.zeros((1, Y1, Z1), F32)
        for k in range(1, K1 - 1):
            src = low[c, k - 1] if k < H else (own[c, k - H] if k < H + 4 else high[c, k - H - 4])
            b[c][k] = src * outside((Y1, Z1), 8, k, 4, has)
    coef = (near, fars, ys, zs)
    from_zero(v, b, coef, inv, 1, K1 - 1, 2)
    first = first_is_red((2, Y1, Z1))
    for p in (0, 2):
        here = slice(p + H, p + H + 2)
        res = b[0][here] - (diag[here] * v[0][here] - gathered(v, 0, *coef, p + H, 2, first))
        res = res[:, 8:16, :]
        fold[8 * p : 8 * p + 16] = res.reshape(16, Z1)
        total = (inner[0][here] + inner[1][here])[:, 8:16, :]
        fold[32 + 8 * p : 48 + 8 * p] = 0.25 * total.reshape(16, Z1)
    both = sum_rows(fold2, dot(fold[...], pair_matrix(Z1, Z2, 0.5)))
    lane = iota((8, Z2), 1)
    out = []
    for q in (0, 1):
        red, black = colours(both[16 * q : 16 * q + 16].reshape(4, 4, Z2))
        red, black = red.reshape(8, Z2), black.reshape(8, Z2)
        lower = jnp.where(lane < 64, red, pltpu.roll(black, 64, 1))
        upper = jnp.where(lane < 64, pltpu.roll(red, 64, 1), black)
        out.append(jnp.where(core == 0, lower, upper))
    piece = jnp.concatenate(out, axis=0)
    for d in range(send.shape[0]):
        send[d] = piece


def up_kernel(got, got_z, *refs, nx, ny):
    level1, refs = refs[:13], refs[13:]
    level0, refs = refs[:13], refs[13:]
    out, refs = refs[0], refs[1:]

    def split(r):
        return r[0:2], r[2:4], (r[4], r[5:7], r[7:9], r[9:11]), r[11:13]

    v1, b1, coef1, inv1 = split(level1)
    v0, b0, coef0, inv0 = split(level0)
    n2, y2 = 2 * nx, 4 * ny
    n3, y3 = nx, 2 * ny
    v2, b2, coef2, inv2 = split(refs[:13])
    in2, out2, diag2, refs = refs[13:15], refs[15:17], refs[17], refs[18:]
    v3, b3, coef3, inv3 = split(refs[:13])
    in3, out3, refs = refs[13:15], refs[15:17], refs[17:]
    parts, fold2, fold1, fold0 = refs[0:2], refs[2], refs[3], refs[4]
    gx_me, gy_me, core = where_am_i()
    lane = iota((2, y2, Z2), 2)

    def body(gx):
        for side in (0, 1):
            src = got if side == 0 else got_z
            for gy in range(ny):
                d = gx * ny + gy
                for q in (0, 1):
                    for p in (0, 1):
                        row = 8 * q + 4 * p
                        parts[side][2 * q + p, 4 * gy : 4 * gy + 4, :] = src[d, row : row + 4, :]
        for q, bufs in ((0, b2), (1, in2)):
            mine, other = parts[0][2 * q : 2 * q + 2], parts[1][2 * q : 2 * q + 2]
            h0 = jnp.where(core == 0, mine, other)
            h1 = jnp.where(core == 0, other, mine)
            here = pl.ds(1 + 2 * gx, 2)
            bufs[0][here] = jnp.where(lane < 64, h0, pltpu.roll(h1, 64, 2))
            bufs[1][here] = jnp.where(lane < 64, pltpu.roll(h0, 64, 2), h1)
            if q == 1:
                for c in (0, 1):
                    out2[c][here] = jnp.where(in2[c][here] > 0.0, 1.0, 3.0)

    loop(0, nx, 1, body)
    for bufs, count in ((in2, n2), (out2, n2), (in3, n3), (out3, n3)):
        for c in (0, 1):
            bufs[c][0:1] = jnp.zeros_like(bufs[c][0:1])
            bufs[c][count + 1 :] = jnp.zeros_like(bufs[c][0:1])
    faces(in2, out2, *coef2, diag2, inv2, None, 1, n2 + 1, 2)
    from_zero(v2, b2, coef2, inv2, 1, n2 + 1, 4)
    first = first_is_red((4, y2, Z2))

    def body(k):
        here, there = pl.ds(k, 4), pl.ds(k - 1, 4)
        res = b2[0][here] - (diag2[here] * v2[0][here] - gathered(v2, 0, *coef2, k, 4, first))
        fold2[0, pl.ds(pl.multiple_of((k - 1) * y2, 4 * y2), 4 * y2), :] = res.reshape(4 * y2, Z2)
        total = 0.25 * (in2[0][here] + in2[1][here])
        fold2[1, pl.ds(pl.multiple_of((k - 1) * y2, 4 * y2), 4 * y2), :] = total.reshape(4 * y2, Z2)

    loop(1, n2 + 1, 4, body)
    pairs = pair_matrix(Z2, Z2, 0.5)
    rows = n2 * y3
    first3 = first_is_red((1, y3, Z2))
    lane3 = iota((1, y3, Z2), 2)
    for q in (0, 1):
        sums = fold2[q, pl.ds(0, rows, 2), :] + fold2[q, pl.ds(1, rows, 2), :]
        fold1[0, 0:rows, :] = dot(sums, pairs)
        bufs = (b3, in3)[q]

        def body(p):
            a = fold1[0, pl.ds(pl.multiple_of(2 * p * y3, y3), y3), :][None]
            c = fold1[0, pl.ds(pl.multiple_of((2 * p + 1) * y3, y3), y3), :][None]
            here = pl.ds(p + 1, 1)
            bufs[0][here] = jnp.where(first3, a, c)
            bufs[1][here] = jnp.where(first3, c, a)
            if q == 1:
                for colour in (0, 1):
                    value = jnp.where(in3[colour][here] > 0.0, 1.0, 3.0)
                    out3[colour][here] = jnp.where(lane3 < Z2 // 2, value, 0.0)

        loop(0, n3, 1, body)
    step3 = 8 if n3 % 8 == 0 else n3
    faces(in3, out3, *coef3, None, inv3, None, 1, n3 + 1, step3)
    from_zero(v3, b3, coef3, inv3, 1, n3 + 1, step3)

    def sweep(i):
        half_sweep(v3, b3, 0, coef3, inv3, 1, n3 + 1, step3)
        half_sweep(v3, b3, 1, coef3, inv3, 1, n3 + 1, step3)

    loop(0, COARSE_SWEEPS - 1, 1, sweep)
    for p in range(n3):
        a, c = v3[0][p + 1 : p + 2], v3[1][p + 1 : p + 2]
        fold2[0, 2 * p * y3 : (2 * p + 1) * y3, :] = jnp.where(first3, a, c)[0]
        fold2[0, (2 * p + 1) * y3 : (2 * p + 2) * y3, :] = jnp.where(first3, c, a)[0]
    twice_rows(fold1, dot(fold2[0, 0:rows, :], copy_matrix(Z2, Z2)))

    def body(k):
        here = pl.ds(k, 4)
        start = pl.multiple_of((k - 1) * y2, 4 * y2)
        e = fold1[0, pl.ds(start, 4 * y2), :].reshape(4, y2, Z2)
        for c in (0, 1):
            v2[c][here] = v2[c][here] + e

    loop(1, n2 + 1, 4, body)
    half_sweep(v2, b2, 0, coef2, inv2, 1, n2 + 1, 4)
    half_sweep(v2, b2, 1, coef2, inv2, 1, n2 + 1, 4)
    shift = lax.rem(4 - 4 * gy_me + 2 * y2, y2)
    first1 = first_is_red((y2, Z2))
    cells = []
    for j in range(4):
        a, c = v2[0][2 * gx_me + j], v2[1][2 * gx_me + j]
        for cell in (jnp.where(first1, a, c), jnp.where(first1, c, a)):
            cells.append(pltpu.roll(cell, shift, 0)[0:16])
    twice_rows(fold1, dot(jnp.concatenate(cells, axis=0), copy_matrix(Z2, Z1)))
    for k in range(1, K1 - 1):
        e = columns(fold1, 32 * (k - 1), Y1, Z1)
        for c in (0, 1):
            v1[c][k] = jnp.where(inv1[c][k] > 0.0, v1[c][k] + e, 0.0)
    half_sweep(v1, b1, 0, coef1, inv1, 1, K1 - 1, 2)
    half_sweep(v1, b1, 1, coef1, inv1, 1, K1 - 1, 2)
    first0 = first_is_red((Y1, Z1))
    cells = []
    for k in range(H - 1, K1 - H + 1):
        a, c = v1[0][k], v1[1][k]
        cells += [jnp.where(first0, a, c), jnp.where(first0, c, a)]
    cells = [cell[4:20] for cell in cells[1:-1]]
    twice_rows(fold0, dot(jnp.concatenate(cells, axis=0), copy_matrix(Z1, Z0, core * 64)))

    def body(p):
        e = columns(fold0, pl.multiple_of(p * 32, 32), 32, Z0)[None]
        here = pl.ds(p + H - 1, 1)
        for c in (0, 1):
            v0[c][here] = jnp.where(inv0[c][here] > 0.0, v0[c][here] + e, 0.0)

    loop(0, BX // 2 + 2, 1, body)
    half_sweep(v0, b0, 0, coef0, inv0, H - 1, K0 - H + 1, 1)
    half_sweep(v0, b0, 1, coef0, inv0, H, K0 - H, 1)
    lanes = pl.ds(pl.multiple_of(core * 128, 128), BZ)
    half_first = first_is_red((BY, BZ))

    def body(p):
        a, c = v0[0][p + H, 8:24, lanes], v0[1][p + H, 8:24, lanes]
        out[2 * p] = jnp.where(half_first, a, c)
        out[2 * p + 1] = jnp.where(half_first, c, a)

    loop(0, BX // 2, 1, body)


def shape(*dims):
    return jax.ShapeDtypeStruct(dims, F32)


def scratch(*dims):
    return pltpu.VMEM(dims, F32)


def ring(x, axis, step):
    n = lax.axis_size(axis)
    return lax.ppermute(x, axis, [(i, (i + step) % n) for i in range(n)])


def swap(x):
    return lax.ppermute(x, "gz", [(0, 1), (1, 0)])


def call(kernel, name, mib, outs, scratches, *args, hbm_in=0, hbm_out=0):
    return pl.pallas_call(
        kernel,
        out_shape=tuple(shape(*o) for o in outs),
        in_specs=[HBM] * hbm_in + [VMEM] * (len(args) - hbm_in),
        out_specs=(HBM,) * hbm_out + (VMEM,) * (len(outs) - hbm_out),
        scratch_shapes=[scratch(*s) if isinstance(s, tuple) else s for s in scratches],
        compiler_params=params(mib),
        name=name,
    )(*args)


def on_device(membrane, recovery, extracellular, fiber_scale, labels):
    nx, ny = lax.axis_size("gx"), lax.axis_size("gy")
    block = (BX, BY, BZ)
    held = [
        pltpu.with_memory_space_constraint(x, pltpu.HBM)
        for x in (membrane, recovery, extracellular, fiber_scale, labels)
    ]
    own, xup, xdn, yup, ydn = call(
        prep_kernel, "prep", 6,
        [(4 * BX + 2, BY, BZ)] + [(20, BY, BZ)] * 2 + [(BX + 2, 24, BZ)] * 2,
        [block] * 4
        + [pltpu.VMEM(labels.shape, jnp.int32), (1, 128, 128), pltpu.SemaphoreType.DMA((5,))],
        *held, hbm_in=5,
    )
    xlo, xhi = ring(xup, "gx", 1), ring(xdn, "gx", -1)
    ylo, yhi = ring(yup, "gy", 1), ring(ydn, "gy", -1)
    cup, cdn = call(corner_kernel, "corner", 4, [(20, 8, BZ)] * 2, [], xlo, xhi)
    clo, chi = ring(cup, "gy", 1), ring(cdn, "gy", -1)
    halos = []
    for piece in (own, xlo, xhi, ylo, yhi, clo, chi):
        halos += [piece, swap(piece)]
    fine = (K0, Y0, Z0)
    mid = (K1, Y1, Z1)
    mnext, rhs1, in1r, in1b, *level0 = call(
        fine_kernel, "fine", 20,
        [block, (2, 4, 8, Z1)] + [mid] * 2 + [fine] * 13,
        [fine] * 16
        + [(8, BY, Z0), (2, 128, 128), block, pltpu.SemaphoreType.DMA((1,))],
        *halos, hbm_out=1,
    )
    rnext, *coef1 = call(
        middle_faces_kernel, "middle_faces", 4, [block] + [mid] * 10,
        [mid] * 2 + [block] * 2 + [pltpu.SemaphoreType.DMA((2,))],
        held[0], held[1], in1r, in1b, hbm_in=2, hbm_out=1,
    )
    part = (2, 2, Y1, Z1)
    wide, xup, xdn = call(
        join_kernel, "join", 4, [(2, 4, Y1, Z1), part, part], [],
        ring(rhs1, "gy", 1), rhs1, ring(rhs1, "gy", -1),
    )
    low, high = ring(xup, "gx", 1), ring(xdn, "gx", -1)
    v1r, v1b, b1r, b1b, send = call(
        middle_kernel, "middle", 4,
        [mid] * 4 + [(ny, 16, Z2)],
        [(64, Z1), (1, 64, 128)],
        low, wide, high, in1r, in1b, *coef1,
    )
    got = lax.all_to_all(send, "gy", 0, 0, tiled=True)
    (send,) = call(spread_kernel, "spread", 4, [(nx, ny, 16, Z2)], [], got)
    got = lax.all_to_all(send, "gx", 0, 0, tiled=True).reshape(nx * ny, 16, Z2)
    grid2, grid3 = (2 * nx + 2, 4 * ny, Z2), (nx + 2, 2 * ny, Z2)
    level1 = [v1r, v1b, b1r, b1b, *coef1[:7], *coef1[8:]]
    (enext,) = call(
        lambda *refs: up_kernel(*refs, nx=nx, ny=ny), "up", 24,
        [block],
        [grid2] * 18 + [grid3] * 17
        + [(4, 4 * ny, Z2)] * 2
        + [(2, 8 * nx * ny, Z2), (2, max(8 * nx * ny, 256), Z2), (3, 320, 128)],
        got, swap(got), *level1, *level0,
    )
    return mnext, rnext, enext


def solution(mesh):
    spec = P("gx", "gy", "gz")
    return jax.shard_map(
        on_device, mesh=mesh, in_specs=(spec,) * 5, out_specs=(spec,) * 3, check_vma=False
    )
```

time: 604 us -> 115 us (0.19)
  the two profiles are of different devices: /device:TPU:131 before, /device:TPU:1 now
where the time goes in v2:
time: 115 us
  Pallas kernels  34.7 us (30%)
  starting transfers between devices  32.9 us (29%)
  blocking collectives  30.2 us (26%)
  waiting for transfers between devices  16.7 us (15%)
    pallas_call x8, Pallas kernels, call(): pl.pallas_call(kernel, out_shape=tuple((shape(*o) for o in outs)), in_spe...  34.7 us
    ppermute x10, starting transfers between devices, ring(): return lax.ppermute(x, axis, [(i, (i + step) % n) for i in range(n)])  19.2 us
    all_to_all x1, blocking collectives, on_device(): got = lax.all_to_all(send, 'gx', 0, 0, tiled=True).reshape(nx * ny, 16, Z2)  17.9 us
    ppermute x8, starting transfers between devices, swap(): return lax.ppermute(x, 'gz', [(0, 1), (1, 0)])  13.8 us
    all_to_all x1, blocking collectives, on_device(): got = lax.all_to_all(send, 'gy', 0, 0, tiled=True)  12.3 us
    ppermute x10, waiting for transfers between devices, ring(): return lax.ppermute(x, axis, [(i, (i + step) % n) for i in range(n)])  12.2 us
    ppermute x8, waiting for transfers between devices, swap(): return lax.ppermute(x, 'gz', [(0, 1), (1, 0)])  4.46 us
  transfers between devices with their start and end apart: 18, of which 9 were waited for; matrix products, arithmetic and copies ran while one was open for 0% of the time, Pallas kernels for 2%

profile of v2, /device:TPU:1, one launch (start us, length us, event | category | flops | bytes accessed | tf_op | source)
XLA Modules:
  0.0 115.2 jit_solution(6529163993881699971)
XLA Ops:
  0.6 1.8 %prep.1 = (f32[66,16,256]{2,1,0:T(8,128)S(1)}, f32[20,16,256]{2,1,0:T(8,128)S(1)}, f32[20,16,256]{2,1,0:T(8,128)S(1)}, f32[18,24,256]{2,1,0:T(8,128)S(1)}, f32[18,24,256]{2,1,0:T(8,128)S(1)}) custom-call(f32[16,16,256]{2,1,0:T(8,128)} %m_in.3, f32[16,16,256]{2,1,0:T(8,128)} %r_in.3, f32[16,16,256]{2,1,0:T(8,128)} %u_in.1, f32[16,16,256]{2,1,0:T(8,128)} %f_in.1, ...), custom_call_target="tpu_custom_call" | custom-call | tf_op jit(solution)/shard_map/prep/pallas_call | solution.py:739
  2.4 3.3 %collective-permute-start = (f32[66,16,256]{2,1,0:T(8,128)S(1)}, f32[66,16,256]{2,1,0:T(8,128)S(1)}, u32[]{:S(2)}, u32[]{:S(2)}) collective-permute-start(f32[66,16,256]{2,1,0:T(8,128)S(1)} %get-tuple-element.46.refs_0_), channel_id=1, source_target_pairs={{0,1},{1,0},{2,3},{3,2},{4,5},{5,4},{6,7},{7,6},{8,9},{9,8},{10,11... | collective-permute-start | bytes 3244040 | tf_op jit(solution)/shard_map/ppermute | solution.py:735
  5.7 1.2 %collective-permute-start.5 = (f32[18,24,256]{2,1,0:T(8,128)S(1)}, f32[18,24,256]{2,1,0:T(8,128)S(1)}, u32[]{:S(2)}, u32[]{:S(2)}) collective-permute-start(f32[18,24,256]{2,1,0:T(8,128)S(1)} %get-tuple-element.49), channel_id=1, source_target_pairs={{0,2},{2,4},{4,6},{6,8},{8,10},{10,12},{12,14},{14,0},{1,3},{3,5},... | collective-permute-start | bytes 1327112 | tf_op jit(solution)/shard_map/ppermute | solution.py:731
  6.9 3.6 %collective-permute-start.3 = (f32[20,16,256]{2,1,0:T(8,128)S(1)}, f32[20,16,256]{2,1,0:T(8,128)S(1)}, u32[]{:S(2)}, u32[]{:S(2)}) collective-permute-start(f32[20,16,256]{2,1,0:T(8,128)S(1)} %get-tuple-element.48), channel_id=1, source_target_pairs={{0,240},{16,0},{32,16},{48,32},{64,48},{80,64},{96,80},{112,96},{1... | collective-permute-start | bytes 983048 | tf_op jit(solution)/shard_map/ppermute | solution.py:731
  10.6 3.9 %collective-permute-start.7 = (f32[18,24,256]{2,1,0:T(8,128)S(1)}, f32[18,24,256]{2,1,0:T(8,128)S(1)}, u32[]{:S(2)}, u32[]{:S(2)}) collective-permute-start(f32[18,24,256]{2,1,0:T(8,128)S(1)} %get-tuple-element.50), channel_id=1, source_target_pairs={{0,14},{2,0},{4,2},{6,4},{8,6},{10,8},{12,10},{14,12},{1,15},{3,1}... | collective-permute-start | bytes 1327112 | tf_op jit(solution)/shard_map/ppermute | solution.py:731
  14.5 3.7 %collective-permute-done.1.xlo.refs_2_ = f32[20,16,256]{2,1,0:T(8,128)S(1)} collective-permute-done((f32[20,16,256]{2,1,0:T(8,128)S(1)}, f32[20,16,256]{2,1,0:T(8,128)S(1)}, u32[]{:S(2)}, u32[]{:S(2)}) %collective-permute-start.1) | collective-permute-done | bytes 327712 | tf_op jit(solution)/shard_map/ppermute | solution.py:731
  18.2 0.9 collective-permute-start.2
  19.3 1.7 %collective-permute-done.5.refs_6_ = f32[18,24,256]{2,1,0:T(8,128)S(1)} collective-permute-done((f32[18,24,256]{2,1,0:T(8,128)S(1)}, f32[18,24,256]{2,1,0:T(8,128)S(1)}, u32[]{:S(2)}, u32[]{:S(2)}) %collective-permute-start.5) | collective-permute-done | bytes 442400 | tf_op jit(solution)/shard_map/ppermute | solution.py:731
  21.0 2.3 %collective-permute-start.11 = (f32[20,8,256]{2,1,0:T(8,128)S(1)}, f32[20,8,256]{2,1,0:T(8,128)S(1)}, u32[]{:S(2)}, u32[]{:S(2)}) collective-permute-start(f32[20,8,256]{2,1,0:T(8,128)S(1)} %get-tuple-element.52), channel_id=1, source_target_pairs={{0,14},{2,0},{4,2},{6,4},{8,6},{10,8},{12,10},{14,12},{1,15},{3,1}... | collective-permute-start | bytes 491528 | tf_op jit(solution)/shard_map/ppermute | solution.py:731
  23.5 2.0 %collective-permute-start.6 = (f32[18,24,256]{2,1,0:T(8,128)S(1)}, f32[18,24,256]{2,1,0:T(8,128)S(1)}, u32[]{:S(2)}, u32[]{:S(2)}) collective-permute-start(f32[18,24,256]{2,1,0:T(8,128)S(1)} %collective-permute-done.5.refs_6_), channel_id=1, source_target_pairs={{0,1},{1,0},{2,3},{3,2},{4,5},{5,4},{6,7},{7,6},{8,9},{9,8},{10,11... | collective-permute-start | bytes 1327112 | tf_op jit(solution)/shard_map/ppermute | solution.py:735
  25.5 2.4 %collective-permute-done.9.refs_10_ = f32[20,8,256]{2,1,0:T(8,128)S(1)} collective-permute-done((f32[20,8,256]{2,1,0:T(8,128)S(1)}, f32[20,8,256]{2,1,0:T(8,128)S(1)}, u32[]{:S(2)}, u32[]{:S(2)}) %collective-permute-start.9) | collective-permute-done | bytes 163872 | tf_op jit(solution)/shard_map/ppermute | solution.py:731
  29.0 1.1 collective-permute-done.10.refs_11_
  30.5 1.0 collective-permute-done.12.refs_13_
  31.5 11.5 %fine.1 = (f32[16,16,256]{2,1,0:T(8,128)}, f32[2,4,8,256]{3,2,1,0:T(8,128)S(1)}, f32[10,24,256]{2,1,0:T(8,128)S(1)}, f32[10,24,256]{2,1,0:T(8,128)S(1)}, f32[14,...) custom-call(f32[66,16,256]{2,1,0:T(8,128)S(1)} %get-tuple-element.46, ...), custom_call_target="tpu_custom_call" | custom-call | tf_op jit(solution)/shard_map/fine/pallas_call | solution.py:739
  43.1 2.8 %collective-permute-start.14 = (f32[2,4,8,256]{3,2,1,0:T(8,128)S(1)}, f32[2,4,8,256]{3,2,1,0:T(8,128)S(1)}, u32[]{:S(2)}, u32[]{:S(2)}) collective-permute-start(f32[2,4,8,256]{3,2,1,0:T(8,128)S(1)} %get-tuple-element.57.own), channel_id=1, source_target_pairs={{0,14},{2,0},{4,2},{6,4},{8,6},{10,8},{12,10},{14,12},{1,15},{3,1}... | collective-permute-start | bytes 196616 | tf_op jit(solution)/shard_map/ppermute | solution.py:731
  45.9 1.3 %collective-permute-done.14.high = f32[2,4,8,256]{3,2,1,0:T(8,128)S(1)} collective-permute-done((f32[2,4,8,256]{3,2,1,0:T(8,128)S(1)}, f32[2,4,8,256]{3,2,1,0:T(8,128)S(1)}, u32[]{:S(2)}, u32[]{:S(2)}) %collective-permute-start.14) | collective-permute-done | bytes 65568 | tf_op jit(solution)/shard_map/ppermute | solution.py:731
  47.2 3.0 %collective-permute-done.13.low = f32[2,4,8,256]{3,2,1,0:T(8,128)S(1)} collective-permute-done((f32[2,4,8,256]{3,2,1,0:T(8,128)S(1)}, f32[2,4,8,256]{3,2,1,0:T(8,128)S(1)}, u32[]{:S(2)}, u32[]{:S(2)}) %collective-permute-start.13) | collective-permute-done | bytes 65568 | tf_op jit(solution)/shard_map/ppermute | solution.py:731
  50.5 4.8 %collective-permute-start.16 = (f32[2,2,24,256]{3,2,1,0:T(8,128)S(1)}, f32[2,2,24,256]{3,2,1,0:T(8,128)S(1)}, u32[]{:S(2)}, u32[]{:S(2)}) collective-permute-start(f32[2,2,24,256]{3,2,1,0:T(8,128)S(1)} %get-tuple-element.60), channel_id=1, source_target_pairs={{0,240},{16,0},{32,16},{48,32},{64,48},{80,64},{96,80},{112,96},{1... | collective-permute-start | bytes 294920 | tf_op jit(solution)/shard_map/ppermute | solution.py:731
  55.3 2.0 %middle_faces.1 = (f32[16,16,256]{2,1,0:T(8,128)}, f32[10,24,256]{2,1,0:T(8,128)S(1)}, f32[10,24,256]{2,1,0:T(8,128)S(1)}, f32[10,24,256]{2,1,0:T(8,128)S(1)}, f...) custom-call(f32[16,16,256]{2,1,0:T(8,128)} %m_in.3, ...), custom_call_target="tpu_custom_call" | custom-call | tf_op jit(solution)/shard_map/middle_faces/pallas_call | solution.py:739
  58.2 12.3 %all_to_all.10.got = f32[8,16,128]{2,1,0:T(8,128)S(1)} all-to-all(f32[8,16,128]{2,1,0:T(8,128)S(1)} %get-tuple-element.71), channel_id=1, replica_groups=mesh['gx'=16,'gy'=8,'gz'=2] {'gy'}, dimensions={0} | all-to-all | bytes 131072 | tf_op jit(solution)/shard_map/all_to_all | solution.py:797
  70.6 17.9 %all_to_all.11 = f32[16,8,16,128]{3,2,1,0:T(8,128)S(1)} all-to-all(f32[16,8,16,128]{3,2,1,0:T(8,128)S(1)} %spread.1), channel_id=1, replica_groups=mesh['gx'=16,'gy'=8,'gz'=2] {'gx'}, dimensions={0} | all-to-all | bytes 2097152 | tf_op jit(solution)/shard_map/all_to_all | solution.py:799
  88.5 6.1 %collective-permute-start.17 = (f32[128,16,128]{2,1,0:T(8,128)S(1)}, f32[128,16,128]{2,1,0:T(8,128)S(1)}, u32[]{:S(2)}, u32[]{:S(2)}) collective-permute-start(f32[128,16,128]{2,1,0:T(8,128)S(1)} %bitcast.1), channel_id=1, source_target_pairs={{0,1},{1,0},{2,3},{3,2},{4,5},{5,4},{6,7},{7,6},{8,9},{9,8},{10,11... | collective-permute-start | bytes 3145736 | tf_op jit(solution)/shard_map/ppermute | solution.py:735
  94.5 2.3 %collective-permute-done.17.refs_1_ = f32[128,16,128]{2,1,0:T(8,128)S(1)} collective-permute-done((f32[128,16,128]{2,1,0:T(8,128)S(1)}, f32[128,16,128]{2,1,0:T(8,128)S(1)}, u32[]{:S(2)}, u32[]{:S(2)}) %collective-permute-start.17) | collective-permute-done | bytes 1048608 | tf_op jit(solution)/shard_map/ppermute | solution.py:735
  96.8 18.3 %up.1 = f32[16,16,256]{2,1,0:T(8,128)} custom-call(f32[128,16,128]{2,1,0:T(8,128)S(1)} %bitcast.2, f32[128,16,128]{2,1,0:T(8,128)S(1)} %collective-permute-done.17.refs_1_, f32[10,24,256]{2,1,0:T(8,128)S(1)} %get-tuple-element.72.refs_2_, f32[10,24,256]{2,1,0:T(8,128)S(1)} %get-tuple-element.73.refs_3_, f32[10,24,256]{2,1,0:T(8,128)S(1)} %get-tuple-element.74.refs_4_, ...), custom_call_target="tpu_custom_call" | custom-call | tf_op jit(solution)/shard_map/up/pallas_call | solution.py:739
  (22 shorter events, 3.0 us)
Async XLA Ops:
  2.4 29.1 %collective-permute-start = (f32[66,16,256]{2,1,0:T(8,128)S(1)}, f32[66,16,256]{2,1,0:T(8,128)S(1)}, u32[]{:S(2)}, u32[]{:S(2)}) collective-permute-start(f32[66,16,256]{2,1,0:T(8,128)S(1)} %get-tuple-element.46.refs_0_), channel_id=1, source_target_pairs={{0,1},{1,0},{2,3},{3,2},{4,5},{5,4},{6,7},{7,6},{8,9},{9,8},{10,11... | collective-permute-start | bytes 3244040 | tf_op jit(solution)/shard_map/ppermute | solution.py:735
  5.7 12.5 %collective-permute-start.1 = (f32[20,16,256]{2,1,0:T(8,128)S(1)}, f32[20,16,256]{2,1,0:T(8,128)S(1)}, u32[]{:S(2)}, u32[]{:S(2)}) collective-permute-start(f32[20,16,256]{2,1,0:T(8,128)S(1)} %get-tuple-element.47), channel_id=1, source_target_pairs={{0,16},{16,32},{32,48},{48,64},{64,80},{80,96},{96,112},{112,128},... | collective-permute-start | bytes 983048 | tf_op jit(solution)/shard_map/ppermute | solution.py:731
  5.7 15.3 %collective-permute-start.5 = (f32[18,24,256]{2,1,0:T(8,128)S(1)}, f32[18,24,256]{2,1,0:T(8,128)S(1)}, u32[]{:S(2)}, u32[]{:S(2)}) collective-permute-start(f32[18,24,256]{2,1,0:T(8,128)S(1)} %get-tuple-element.49), channel_id=1, source_target_pairs={{0,2},{2,4},{4,6},{6,8},{8,10},{10,12},{12,14},{14,0},{1,3},{3,5},... | collective-permute-start | bytes 1327112 | tf_op jit(solution)/shard_map/ppermute | solution.py:731
  6.9 12.2 %collective-permute-start.3 = (f32[20,16,256]{2,1,0:T(8,128)S(1)}, f32[20,16,256]{2,1,0:T(8,128)S(1)}, u32[]{:S(2)}, u32[]{:S(2)}) collective-permute-start(f32[20,16,256]{2,1,0:T(8,128)S(1)} %get-tuple-element.48), channel_id=1, source_target_pairs={{0,240},{16,0},{32,16},{48,32},{64,48},{80,64},{96,80},{112,96},{1... | collective-permute-start | bytes 983048 | tf_op jit(solution)/shard_map/ppermute | solution.py:731
  10.6 12.9 %collective-permute-start.7 = (f32[18,24,256]{2,1,0:T(8,128)S(1)}, f32[18,24,256]{2,1,0:T(8,128)S(1)}, u32[]{:S(2)}, u32[]{:S(2)}) collective-permute-start(f32[18,24,256]{2,1,0:T(8,128)S(1)} %get-tuple-element.50), channel_id=1, source_target_pairs={{0,14},{2,0},{4,2},{6,4},{8,6},{10,8},{12,10},{14,12},{1,15},{3,1}... | collective-permute-start | bytes 1327112 | tf_op jit(solution)/shard_map/ppermute | solution.py:731
  18.2 10.2 %collective-permute-start.2 = (f32[20,16,256]{2,1,0:T(8,128)S(1)}, f32[20,16,256]{2,1,0:T(8,128)S(1)}, u32[]{:S(2)}, u32[]{:S(2)}) collective-permute-start(f32[20,16,256]{2,1,0:T(8,128)S(1)} %collective-permute-done.1.xlo.refs_2_), channel_id=1, source_target_pairs={{0,1},{1,0},{2,3},{3,2},{4,5},{5,4},{6,7},{7,6},{8,9},{9,8},{10,11... | collective-permute-start | bytes 983048 | tf_op jit(solution)/shard_map/ppermute | solution.py:735
  19.2 8.7 %collective-permute-start.9 = (f32[20,8,256]{2,1,0:T(8,128)S(1)}, f32[20,8,256]{2,1,0:T(8,128)S(1)}, u32[]{:S(2)}, u32[]{:S(2)}) collective-permute-start(f32[20,8,256]{2,1,0:T(8,128)S(1)} %get-tuple-element.51), channel_id=1, source_target_pairs={{0,2},{2,4},{4,6},{6,8},{8,10},{10,12},{12,14},{14,0},{1,3},{3,5},... | collective-permute-start | bytes 491528 | tf_op jit(solution)/shard_map/ppermute | solution.py:731
  21.0 7.4 %collective-permute-start.11 = (f32[20,8,256]{2,1,0:T(8,128)S(1)}, f32[20,8,256]{2,1,0:T(8,128)S(1)}, u32[]{:S(2)}, u32[]{:S(2)}) collective-permute-start(f32[20,8,256]{2,1,0:T(8,128)S(1)} %get-tuple-element.52), channel_id=1, source_target_pairs={{0,14},{2,0},{4,2},{6,4},{8,6},{10,8},{12,10},{14,12},{1,15},{3,1}... | collective-permute-start | bytes 491528 | tf_op jit(solution)/shard_map/ppermute | solution.py:731
  23.5 8.0 %collective-permute-start.6 = (f32[18,24,256]{2,1,0:T(8,128)S(1)}, f32[18,24,256]{2,1,0:T(8,128)S(1)}, u32[]{:S(2)}, u32[]{:S(2)}) collective-permute-start(f32[18,24,256]{2,1,0:T(8,128)S(1)} %collective-permute-done.5.refs_6_), channel_id=1, source_target_pairs={{0,1},{1,0},{2,3},{3,2},{4,5},{5,4},{6,7},{7,6},{8,9},{9,8},{10,11... | collective-permute-start | bytes 1327112 | tf_op jit(solution)/shard_map/ppermute | solution.py:735
  27.9 3.6 %collective-permute-start.8 = (f32[18,24,256]{2,1,0:T(8,128)S(1)}, f32[18,24,256]{2,1,0:T(8,128)S(1)}, u32[]{:S(2)}, u32[]{:S(2)}) collective-permute-start(f32[18,24,256]{2,1,0:T(8,128)S(1)} %collective-permute-done.7.refs_8_), channel_id=1, source_target_pairs={{0,1},{1,0},{2,3},{3,2},{4,5},{5,4},{6,7},{7,6},{8,9},{9,8},{10,11... | collective-permute-start | bytes 1327112 | tf_op jit(solution)/shard_map/ppermute | solution.py:735
  28.4 1.7 %collective-permute-start.10 = (f32[20,8,256]{2,1,0:T(8,128)S(1)}, f32[20,8,256]{2,1,0:T(8,128)S(1)}, u32[]{:S(2)}, u32[]{:S(2)}) collective-permute-start(f32[20,8,256]{2,1,0:T(8,128)S(1)} %collective-permute-done.9.refs_10_), channel_id=1, source_target_pairs={{0,1},{1,0},{2,3},{3,2},{4,5},{5,4},{6,7},{7,6},{8,9},{9,8},{10,11... | collective-permute-start | bytes 491528 | tf_op jit(solution)/shard_map/ppermute | solution.py:735
  28.4 3.0 %collective-permute-start.4 = (f32[20,16,256]{2,1,0:T(8,128)S(1)}, f32[20,16,256]{2,1,0:T(8,128)S(1)}, u32[]{:S(2)}, u32[]{:S(2)}) collective-permute-start(f32[20,16,256]{2,1,0:T(8,128)S(1)} %collective-permute-done.3.xhi.refs_4_), channel_id=1, source_target_pairs={{0,1},{1,0},{2,3},{3,2},{4,5},{5,4},{6,7},{7,6},{8,9},{9,8},{10,11... | collective-permute-start | bytes 983048 | tf_op jit(solution)/shard_map/ppermute | solution.py:735
  30.1 1.4 %collective-permute-start.12 = (f32[20,8,256]{2,1,0:T(8,128)S(1)}, f32[20,8,256]{2,1,0:T(8,128)S(1)}, u32[]{:S(2)}, u32[]{:S(2)}) collective-permute-start(f32[20,8,256]{2,1,0:T(8,128)S(1)} %collective-permute-done.11.refs_12_), channel_id=1, source_target_pairs={{0,1},{1,0},{2,3},{3,2},{4,5},{5,4},{6,7},{7,6},{8,9},{9,8},{10,11... | collective-permute-start | bytes 491528 | tf_op jit(solution)/shard_map/ppermute | solution.py:735
  43.1 4.2 %collective-permute-start.14 = (f32[2,4,8,256]{3,2,1,0:T(8,128)S(1)}, f32[2,4,8,256]{3,2,1,0:T(8,128)S(1)}, u32[]{:S(2)}, u32[]{:S(2)}) collective-permute-start(f32[2,4,8,256]{3,2,1,0:T(8,128)S(1)} %get-tuple-element.57.own), channel_id=1, source_target_pairs={{0,14},{2,0},{4,2},{6,4},{8,6},{10,8},{12,10},{14,12},{1,15},{3,1}... | collective-permute-start | bytes 196616 | tf_op jit(solution)/shard_map/ppermute | solution.py:731
  45.9 4.3 %collective-permute-start.13 = (f32[2,4,8,256]{3,2,1,0:T(8,128)S(1)}, f32[2,4,8,256]{3,2,1,0:T(8,128)S(1)}, u32[]{:S(2)}, u32[]{:S(2)}) collective-permute-start(f32[2,4,8,256]{3,2,1,0:T(8,128)S(1)} %get-tuple-element.57.own), channel_id=1, source_target_pairs={{0,2},{2,4},{4,6},{6,8},{8,10},{10,12},{12,14},{14,0},{1,3},{3,5},... | collective-permute-start | bytes 196616 | tf_op jit(solution)/shard_map/ppermute | solution.py:731
  50.2 7.1 %collective-permute-start.15 = (f32[2,2,24,256]{3,2,1,0:T(8,128)S(1)}, f32[2,2,24,256]{3,2,1,0:T(8,128)S(1)}, u32[]{:S(2)}, u32[]{:S(2)}) collective-permute-start(f32[2,2,24,256]{3,2,1,0:T(8,128)S(1)} %get-tuple-element.58), channel_id=1, source_target_pairs={{0,16},{16,32},{32,48},{48,64},{64,80},{80,96},{96,112},{112,128},... | collective-permute-start | bytes 294920 | tf_op jit(solution)/shard_map/ppermute | solution.py:731
  50.5 6.8 %collective-permute-start.16 = (f32[2,2,24,256]{3,2,1,0:T(8,128)S(1)}, f32[2,2,24,256]{3,2,1,0:T(8,128)S(1)}, u32[]{:S(2)}, u32[]{:S(2)}) collective-permute-start(f32[2,2,24,256]{3,2,1,0:T(8,128)S(1)} %get-tuple-element.60), channel_id=1, source_target_pairs={{0,240},{16,0},{32,16},{48,32},{64,48},{80,64},{96,80},{112,96},{1... | collective-permute-start | bytes 294920 | tf_op jit(solution)/shard_map/ppermute | solution.py:731
  88.5 8.3 %collective-permute-start.17 = (f32[128,16,128]{2,1,0:T(8,128)S(1)}, f32[128,16,128]{2,1,0:T(8,128)S(1)}, u32[]{:S(2)}, u32[]{:S(2)}) collective-permute-start(f32[128,16,128]{2,1,0:T(8,128)S(1)} %bitcast.1), channel_id=1, source_target_pairs={{0,1},{1,0},{2,3},{3,2},{4,5},{5,4},{6,7},{7,6},{8,9},{9,8},{10,11... | collective-permute-start | bytes 3145736 | tf_op jit(solution)/shard_map/ppermute | solution.py:735

commit v3 on v2

--- a/solution.py
+++ b/solution.py
@@ -14,6 +14,7 @@
 F32 = jnp.float32
 BX, BY, BZ = 16, 16, 256
 H = 3
+SF, SI, SH, SHB, S1, S2, SU, S22, S3 = 3, 4, 4, 5, 8, 8, 8, 16, 16
 K0, Y0, Z0 = BX // 2 + 2 * H, 32, 384
 K1, Y1, Z1 = BX // 4 + 2 * H, 24, BZ
 Z2 = BZ // 2
@@ -54,7 +55,13 @@
 
 
 def dot(a, b):
-    return jnp.dot(a, b, precision=lax.Precision.HIGHEST, preferred_element_type=F32)
+    b = b.astype(jnp.bfloat16)
+    high = a.astype(jnp.bfloat16)
+    rest = a - high.astype(F32)
+    mid = rest.astype(jnp.bfloat16)
+    low = (rest - mid.astype(F32)).astype(jnp.bfloat16)
+    parts = [jnp.dot(p, b, preferred_element_type=F32) for p in (low, mid, high)]
+    return parts[0] + parts[1] + parts[2]
 
 
 def sum_rows(buf, x):
@@ -79,6 +86,10 @@
 
 
 def loop(start, stop, step, body):
+    if not isinstance(start, int) or stop - start == step:
+        body(start)
+        return
+
     def run(index, carry):
         body(start + index * step)
         return carry
@@ -432,17 +443,17 @@
 
     loop(0, K0, 1, body)
     faces(
-        inner, outer, near, fars, ys, zs, diag, inv, (low_near, low_far, low_y, low_z), 1, K0 - 1, 1
-    )
-    first = first_is_red((1, Y0, Z0))
+        inner, outer, near, fars, ys, zs, diag, inv, (low_near, low_far, low_y, low_z), 1, K0 - 1, SF
+    )
+    first = first_is_red((SI, Y0, Z0))
 
     def intra(x, k):
-        here = pl.ds(k, 1)
+        here = pl.ds(k, SI)
         a = [x[0][here], x[1][here]]
         flow = low_near[here] * (a[1] - a[0])
         total = [flow, -flow]
         for c in (0, 1):
-            total[c] = total[c] + low_far[c][here] * (far(x[1 - c], k, 1, c == 0, first) - a[c])
+            total[c] = total[c] + low_far[c][here] * (far(x[1 - c], k, SI, c == 0, first) - a[c])
         for axis, low in ((1, low_y), (2, low_z)):
             flows = [low[c][here] * (up(a[1 - c], axis) - a[c]) for c in (0, 1)]
             for c in (0, 1):
@@ -450,12 +461,12 @@
         return total
 
     def body(k):
-        here = pl.ds(k, 1)
+        here = pl.ds(k, SI)
         drive = intra(s, k)
         for c in (0, 1):
             w[c][here] = w[c][here] + TIME_STEP * drive[c]
 
-    loop(1, K0 - 1, 1, body)
+    loop(1, K0 - 1, SI, body)
     lanes = pl.ds(pl.multiple_of(core * 128, 128), BZ)
     half_first = first_is_red((BY, BZ))
 
@@ -468,22 +479,23 @@
     copies = fetch([(mout, mnext)], sems)
 
     def body(k):
-        here = pl.ds(k, 1)
+        here = pl.ds(k, SI)
         both = intra(w, k)
         for c in (0, 1):
             b[c][here] = both[c]
 
-    loop(1, K0 - 1, 1, body)
+    loop(1, K0 - 1, SI, body)
     coef = (near, fars, ys, zs)
-    half_sweep(v, b, 0, coef, inv, 1, K0 - 1, 1)
-    half_sweep(v, b, 1, coef, inv, 2, K0 - 2, 1)
+    half_sweep(v, b, 0, coef, inv, 1, K0 - 1, SH)
+    half_sweep(v, b, 1, coef, inv, 2, K0 - 2, SHB)
+    first = first_is_red((SH, Y0, Z0))
 
     def body(p):
-        here = pl.ds(p + H, 1)
-        res = b[0][here] - (diag[here] * v[0][here] - gathered(v, 0, *coef, p + H, 1, first))
-        fold[pl.ds(p, 1)] = res[:, 8:24, :]
-
-    loop(0, BX // 2, 1, body)
+        here = pl.ds(p + H, SH)
+        res = b[0][here] - (diag[here] * v[0][here] - gathered(v, 0, *coef, p + H, SH, first))
+        fold[pl.ds(p, SH)] = res[:, 8:24, :]
+
+    loop(0, BX // 2, SH, body)
     half = BX // 2 * BY
     pairs = pair_matrix(Z0, Z1, 0.5, core * 64)
     coarse = sum_rows(fold2, dot(fold[...].reshape(half, Z0), pairs)).reshape(8, 8, Z1)
@@ -513,7 +525,7 @@
             -rr - IONIC_GAIN * mm * (mm - IONIC_ONSET - 1.0)
         )
     copies = fetch([(r, rnext)], sems)
-    faces(inner, outer, near, fars, ys, zs, diag, inv, None, 1, K1 - 1, 2)
+    faces(inner, outer, near, fars, ys, zs, diag, inv, None, 1, K1 - 1, S1)
     copies[0].wait()
 
 
@@ -535,8 +547,7 @@
         send[d] = whole
 
 
-def middle_kernel(low, own, high, *refs):
-    inner, refs = refs[0:2], refs[2:]
+def middle_kernel(low, own, high, seed, *refs):
     near, fars, ys, zs, diag, inv, refs = (
         refs[0], refs[1:3], refs[3:5], refs[5:7], refs[7], refs[8:10], refs[10:],
     )
@@ -550,32 +561,126 @@
             src = low[c, k - 1] if k < H else (own[c, k - H] if k < H + 4 else high[c, k - H - 4])
             b[c][k] = src * outside((Y1, Z1), 8, k, 4, has)
     coef = (near, fars, ys, zs)
-    from_zero(v, b, coef, inv, 1, K1 - 1, 2)
+    from_zero(v, b, coef, inv, 1, K1 - 1, S1)
     first = first_is_red((2, Y1, Z1))
     for p in (0, 2):
         here = slice(p + H, p + H + 2)
         res = b[0][here] - (diag[here] * v[0][here] - gathered(v, 0, *coef, p + H, 2, first))
-        res = res[:, 8:16, :]
-        fold[8 * p : 8 * p + 16] = res.reshape(16, Z1)
-        total = (inner[0][here] + inner[1][here])[:, 8:16, :]
-        fold[32 + 8 * p : 48 + 8 * p] = 0.25 * total.reshape(16, Z1)
+        fold[8 * p : 8 * p + 16] = res[:, 8:16, :].reshape(16, Z1)
     both = sum_rows(fold2, dot(fold[...], pair_matrix(Z1, Z2, 0.5)))
-    lane = iota((8, Z2), 1)
-    out = []
-    for q in (0, 1):
-        red, black = colours(both[16 * q : 16 * q + 16].reshape(4, 4, Z2))
-        red, black = red.reshape(8, Z2), black.reshape(8, Z2)
-        lower = jnp.where(lane < 64, red, pltpu.roll(black, 64, 1))
-        upper = jnp.where(lane < 64, pltpu.roll(red, 64, 1), black)
-        out.append(jnp.where(core == 0, lower, upper))
-    piece = jnp.concatenate(out, axis=0)
+    red, black = colours(both.reshape(4, 4, Z2))
+    red, black = red.reshape(8, Z2), black.reshape(8, Z2)
+    mine = (iota((8, Z2), 1) < 64) == (core == 0)
+    piece = in_order(jnp.where(mine, red, pltpu.roll(black, 64, 1)))
     for d in range(send.shape[0]):
-        send[d] = piece
+        send[d, 0:8] = piece
+        send[d, 8:16] = seed[...]
+
+
+def in_order(piece):
+    odd = (iota(piece.shape, 0) * 0 + lax.axis_index("gy")) & 1
+    return jnp.where(odd == 1, pltpu.roll(piece, 4, 0), piece)
+
+
+def seed_kernel(own, send, fold):
+    sums = []
+    for p in range(4):
+        total = None
+        for i in (2 * p, 2 * p + 1):
+            slab, rows, lanes = block_of(i)
+            block = own[4 * BX + slab, rows, lanes]
+            total = block if total is None else total + block
+        sums.append(total)
+    both = sum_rows(fold, dot(jnp.concatenate(sums, axis=0), pair_matrix(Z2, Z2, 0.125)))
+    red, black = colours(both.reshape(4, 4, Z2))
+    red, black = red.reshape(8, Z2), black.reshape(8, Z2)
+    core = lax.axis_index("gz")
+    lane = iota((8, Z2), 1) + core * 0
+    lower = jnp.where(lane < 64, red, pltpu.roll(black, 64, 1))
+    upper = jnp.where(lane < 64, black, pltpu.roll(red, 64, 1))
+    send[...] = in_order(jnp.where(core == 0, lower, upper))
+
+
+def unpack(got, got_z, part, bufs, nx, ny):
+    core = lax.axis_index("gz")
+    mine = (iota((8, Z2), 1) < 64) == (core == 0)
+    upper = iota((8, Z2), 0) < 4
+
+    def body(start):
+      for gx in [start + i for i in range(min(SU, nx))]:
+        for t in range(ny // 2):
+            d = gx * ny + 2 * t
+            tiles = []
+            for src in (got, got_z):
+                even, odd = src[d, part : part + 8], src[d + 1, part : part + 8]
+                tiles.append(
+                    (
+                        jnp.where(upper, even, odd),
+                        pltpu.roll(jnp.where(upper, odd, even), 4, 0),
+                    )
+                )
+            for p in (0, 1):
+                a, c = tiles[0][p], tiles[1][p]
+                rows = slice(8 * t, 8 * t + 8)
+                bufs[0][1 + 2 * gx + p, rows, :] = jnp.where(mine, a, c)
+                bufs[1][1 + 2 * gx + p, rows, :] = pltpu.roll(jnp.where(mine, c, a), 64, 1)
+
+    loop(0, nx, min(SU, nx), body)
+
+
+def coarse_kernel(got, got_z, *refs, nx, ny):
+    n2, y2, n3, y3 = 2 * nx, 4 * ny, nx, 2 * ny
+    coef2, refs = (refs[0], refs[1:3], refs[3:5], refs[5:7], refs[7], refs[8:10]), refs[10:]
+    coef3, refs = (refs[0], refs[1:3], refs[3:5], refs[5:7], None, refs[7:9]), refs[9:]
+    in2, out2, in3, out3, fold2, fold1 = (
+        refs[0:2], refs[2:4], refs[4:6], refs[6:8], refs[8], refs[9],
+    )
+    unpack(got, got_z, 8, in2, nx, ny)
+
+    def body(k):
+        here = pl.ds(k, 4)
+        for c in (0, 1):
+            out2[c][here] = jnp.where(in2[c][here] > 0.0, 1.0, 3.0)
+        total = 0.25 * (in2[0][here] + in2[1][here])
+        fold2[pl.ds(pl.multiple_of((k - 1) * y2, 4 * y2), 4 * y2), :] = total.reshape(4 * y2, Z2)
+
+    loop(1, n2 + 1, 4, body)
+    for bufs, count in ((in2, n2), (out2, n2), (in3, n3), (out3, n3)):
+        for c in (0, 1):
+            bufs[c][0:1] = jnp.zeros_like(bufs[c][0:1])
+            bufs[c][count + 1 :] = jnp.zeros_like(bufs[c][0:1])
+    faces(in2, out2, *coef2, None, 1, n2 + 1, min(S2, n2))
+    restrict(fold2, fold1, in3, n3, y3)
+    lane = iota((n3, y3, Z2), 2)
+    for c in (0, 1):
+        value = jnp.where(in3[c][1 : n3 + 1] > 0.0, 1.0, 3.0)
+        out3[c][1 : n3 + 1] = jnp.where(lane < Z2 // 2, value, 0.0)
+    faces(in3, out3, *coef3, None, 1, n3 + 1, min(S3, n3))
+
+
+def restrict(fold2, fold1, bufs, n3, y3):
+    rows = 2 * n3 * y3
+    sums = fold2[pl.ds(0, rows, 2), :] + fold2[pl.ds(1, rows, 2), :]
+    fold1[0, 0:rows, :] = dot(sums, pair_matrix(Z2, Z2, 0.5))
+    first = first_is_red((1, y3, Z2))
+
+    def body(p):
+        a = fold1[0, pl.ds(pl.multiple_of(2 * p * y3, y3), y3), :][None]
+        c = fold1[0, pl.ds(pl.multiple_of((2 * p + 1) * y3, y3), y3), :][None]
+        here = pl.ds(p + 1, 1)
+        bufs[0][here] = jnp.where(first, a, c)
+        bufs[1][here] = jnp.where(first, c, a)
+
+    loop(0, n3, 1, body)
 
 
 def up_kernel(got, got_z, *refs, nx, ny):
     level1, refs = refs[:13], refs[13:]
     level0, refs = refs[:13], refs[13:]
+    coef2, diag2, inv2, refs = (
+        (refs[0], refs[1:3], refs[3:5], refs[5:7]), refs[7], refs[8:10], refs[10:],
+    )
+    coef3, inv3, refs = (refs[0], refs[1:3], refs[3:5], refs[5:7]), refs[7:9], refs[9:]
     out, refs = refs[0], refs[1:]
 
     def split(r):
@@ -585,97 +690,44 @@
     v0, b0, coef0, inv0 = split(level0)
     n2, y2 = 2 * nx, 4 * ny
     n3, y3 = nx, 2 * ny
-    v2, b2, coef2, inv2 = split(refs[:13])
-    in2, out2, diag2, refs = refs[13:15], refs[15:17], refs[17], refs[18:]
-    v3, b3, coef3, inv3 = split(refs[:13])
-    in3, out3, refs = refs[13:15], refs[15:17], refs[17:]
-    parts, fold2, fold1, fold0 = refs[0:2], refs[2], refs[3], refs[4]
+    v2, b2, v3, b3 = refs[0:2], refs[2:4], refs[4:6], refs[6:8]
+    fold2, fold1, fold0 = refs[8], refs[9], refs[10]
     gx_me, gy_me, core = where_am_i()
-    lane = iota((2, y2, Z2), 2)
-
-    def body(gx):
-        for side in (0, 1):
-            src = got if side == 0 else got_z
-            for gy in range(ny):
-                d = gx * ny + gy
-                for q in (0, 1):
-                    for p in (0, 1):
-                        row = 8 * q + 4 * p
-                        parts[side][2 * q + p, 4 * gy : 4 * gy + 4, :] = src[d, row : row + 4, :]
-        for q, bufs in ((0, b2), (1, in2)):
-            mine, other = parts[0][2 * q : 2 * q + 2], parts[1][2 * q : 2 * q + 2]
-            h0 = jnp.where(core == 0, mine, other)
-            h1 = jnp.where(core == 0, other, mine)
-            here = pl.ds(1 + 2 * gx, 2)
-            bufs[0][here] = jnp.where(lane < 64, h0, pltpu.roll(h1, 64, 2))
-            bufs[1][here] = jnp.where(lane < 64, pltpu.roll(h0, 64, 2), h1)
-            if q == 1:
-                for c in (0, 1):
-                    out2[c][here] = jnp.where(in2[c][here] > 0.0, 1.0, 3.0)
-
-    loop(0, nx, 1, body)
-    for bufs, count in ((in2, n2), (out2, n2), (in3, n3), (out3, n3)):
-        for c in (0, 1):
-            bufs[c][0:1] = jnp.zeros_like(bufs[c][0:1])
-            bufs[c][count + 1 :] = jnp.zeros_like(bufs[c][0:1])
-    faces(in2, out2, *coef2, diag2, inv2, None, 1, n2 + 1, 2)
-    from_zero(v2, b2, coef2, inv2, 1, n2 + 1, 4)
-    first = first_is_red((4, y2, Z2))
+    unpack(got, got_z, 0, b2, nx, ny)
+    step2 = min(S22, n2)
+    from_zero(v2, b2, coef2, inv2, 1, n2 + 1, step2)
+    first = first_is_red((step2, y2, Z2))
 
     def body(k):
-        here, there = pl.ds(k, 4), pl.ds(k - 1, 4)
-        res = b2[0][here] - (diag2[here] * v2[0][here] - gathered(v2, 0, *coef2, k, 4, first))
-        fold2[0, pl.ds(pl.multiple_of((k - 1) * y2, 4 * y2), 4 * y2), :] = res.reshape(4 * y2, Z2)
-        total = 0.25 * (in2[0][here] + in2[1][here])
-        fold2[1, pl.ds(pl.multiple_of((k - 1) * y2, 4 * y2), 4 * y2), :] = total.reshape(4 * y2, Z2)
-
-    loop(1, n2 + 1, 4, body)
-    pairs = pair_matrix(Z2, Z2, 0.5)
-    rows = n2 * y3
-    first3 = first_is_red((1, y3, Z2))
-    lane3 = iota((1, y3, Z2), 2)
-    for q in (0, 1):
-        sums = fold2[q, pl.ds(0, rows, 2), :] + fold2[q, pl.ds(1, rows, 2), :]
-        fold1[0, 0:rows, :] = dot(sums, pairs)
-        bufs = (b3, in3)[q]
-
-        def body(p):
-            a = fold1[0, pl.ds(pl.multiple_of(2 * p * y3, y3), y3), :][None]
-            c = fold1[0, pl.ds(pl.multiple_of((2 * p + 1) * y3, y3), y3), :][None]
-            here = pl.ds(p + 1, 1)
-            bufs[0][here] = jnp.where(first3, a, c)
-            bufs[1][here] = jnp.where(first3, c, a)
-            if q == 1:
-                for colour in (0, 1):
-                    value = jnp.where(in3[colour][here] > 0.0, 1.0, 3.0)
-                    out3[colour][here] = jnp.where(lane3 < Z2 // 2, value, 0.0)
-
-        loop(0, n3, 1, body)
-    step3 = 8 if n3 % 8 == 0 else n3
-    faces(in3, out3, *coef3, None, inv3, None, 1, n3 + 1, step3)
-    from_zero(v3, b3, coef3, inv3, 1, n3 + 1, step3)
+        here = pl.ds(k, step2)
+        res = b2[0][here] - (diag2[here] * v2[0][here] - gathered(v2, 0, *coef2, k, step2, first))
+        start = pl.multiple_of((k - 1) * y2, step2 * y2)
+        fold2[pl.ds(start, step2 * y2), :] = res.reshape(step2 * y2, Z2)
+
+    loop(1, n2 + 1, step2, body)
+    restrict(fold2, fold1, b3, n3, y3)
+    from_zero(v3, b3, coef3, inv3, 1, n3 + 1, n3)
 
     def sweep(i):
-        half_sweep(v3, b3, 0, coef3, inv3, 1, n3 + 1, step3)
-        half_sweep(v3, b3, 1, coef3, inv3, 1, n3 + 1, step3)
+        half_sweep(v3, b3, 0, coef3, inv3, 1, n3 + 1, n3)
+        half_sweep(v3, b3, 1, coef3, inv3, 1, n3 + 1, n3)
 
     loop(0, COARSE_SWEEPS - 1, 1, sweep)
-    for p in range(n3):
-        a, c = v3[0][p + 1 : p + 2], v3[1][p + 1 : p + 2]
-        fold2[0, 2 * p * y3 : (2 * p + 1) * y3, :] = jnp.where(first3, a, c)[0]
-        fold2[0, (2 * p + 1) * y3 : (2 * p + 2) * y3, :] = jnp.where(first3, c, a)[0]
-    twice_rows(fold1, dot(fold2[0, 0:rows, :], copy_matrix(Z2, Z2)))
-
-    def body(k):
-        here = pl.ds(k, 4)
-        start = pl.multiple_of((k - 1) * y2, 4 * y2)
-        e = fold1[0, pl.ds(start, 4 * y2), :].reshape(4, y2, Z2)
+    near2 = min(8, n2)
+    base = jnp.clip(2 * gx_me - 2, 0, n2 - near2)
+    first3 = first_is_red((y3, Z2))
+    for p in range(near2 // 2):
+        a, c = v3[0][base // 2 + p + 1], v3[1][base // 2 + p + 1]
+        fold2[2 * p * y3 : (2 * p + 1) * y3, :] = jnp.where(first3, a, c)
+        fold2[(2 * p + 1) * y3 : (2 * p + 2) * y3, :] = jnp.where(first3, c, a)
+    twice_rows(fold1, dot(fold2[0 : near2 * y3, :], copy_matrix(Z2, Z2)))
+    for k in range(0, near2, 4):
+        e = fold1[0, k * y2 : (k + 4) * y2, :].reshape(4, y2, Z2)
+        here = pl.ds(base + 1 + k, 4)
         for c in (0, 1):
             v2[c][here] = v2[c][here] + e
-
-    loop(1, n2 + 1, 4, body)
-    half_sweep(v2, b2, 0, coef2, inv2, 1, n2 + 1, 4)
-    half_sweep(v2, b2, 1, coef2, inv2, 1, n2 + 1, 4)
+    half_sweep(v2, b2, 0, coef2, inv2, base + 1, base + 1 + near2, near2)
+    half_sweep(v2, b2, 1, coef2, inv2, base + 1, base + 1 + near2, near2)
     shift = lax.rem(4 - 4 * gy_me + 2 * y2, y2)
     first1 = first_is_red((y2, Z2))
     cells = []
@@ -688,8 +740,8 @@
         e = columns(fold1, 32 * (k - 1), Y1, Z1)
         for c in (0, 1):
             v1[c][k] = jnp.where(inv1[c][k] > 0.0, v1[c][k] + e, 0.0)
-    half_sweep(v1, b1, 0, coef1, inv1, 1, K1 - 1, 2)
-    half_sweep(v1, b1, 1, coef1, inv1, 1, K1 - 1, 2)
+    half_sweep(v1, b1, 0, coef1, inv1, 1, K1 - 1, S1)
+    half_sweep(v1, b1, 1, coef1, inv1, 1, K1 - 1, S1)
     first0 = first_is_red((Y1, Z1))
     cells = []
     for k in range(H - 1, K1 - H + 1):
@@ -705,8 +757,8 @@
             v0[c][here] = jnp.where(inv0[c][here] > 0.0, v0[c][here] + e, 0.0)
 
     loop(0, BX // 2 + 2, 1, body)
-    half_sweep(v0, b0, 0, coef0, inv0, H - 1, K0 - H + 1, 1)
-    half_sweep(v0, b0, 1, coef0, inv0, H, K0 - H, 1)
+    half_sweep(v0, b0, 0, coef0, inv0, H - 1, K0 - H + 1, SHB)
+    half_sweep(v0, b0, 1, coef0, inv0, H, K0 - H, SH)
     lanes = pl.ds(pl.multiple_of(core * 128, 128), BZ)
     half_first = first_is_red((BY, BZ))
 
@@ -733,6 +785,12 @@
 
 def swap(x):
     return lax.ppermute(x, "gz", [(0, 1), (1, 0)])
+
+
+def gather(send, nx, ny):
+    got = lax.all_to_all(send, "gy", 0, 0, tiled=True)
+    (send,) = call(spread_kernel, "spread", 4, [(nx,) + got.shape], [], got)
+    return lax.all_to_all(send, "gx", 0, 0, tiled=True).reshape((nx * ny,) + got.shape[1:])
 
 
 def call(kernel, name, mib, outs, scratches, *args, hbm_in=0, hbm_out=0):
@@ -768,8 +826,10 @@
     halos = []
     for piece in (own, xlo, xhi, ylo, yhi, clo, chi):
         halos += [piece, swap(piece)]
+    (seed,) = call(seed_kernel, "seed", 4, [(8, Z2)], [(1, 32, 128)], own)
     fine = (K0, Y0, Z0)
     mid = (K1, Y1, Z1)
+    grid2, grid3 = (2 * nx + 2, 4 * ny, Z2), (nx + 2, 2 * ny, Z2)
     mnext, rhs1, in1r, in1b, *level0 = call(
         fine_kernel, "fine", 20,
         [block, (2, 4, 8, Z1)] + [mid] * 2 + [fine] * 13,
@@ -791,21 +851,24 @@
     v1r, v1b, b1r, b1b, send = call(
         middle_kernel, "middle", 4,
         [mid] * 4 + [(ny, 16, Z2)],
-        [(64, Z1), (1, 64, 128)],
-        low, wide, high, in1r, in1b, *coef1,
-    )
-    got = lax.all_to_all(send, "gy", 0, 0, tiled=True)
-    (send,) = call(spread_kernel, "spread", 4, [(nx, ny, 16, Z2)], [], got)
-    got = lax.all_to_all(send, "gx", 0, 0, tiled=True).reshape(nx * ny, 16, Z2)
-    grid2, grid3 = (2 * nx + 2, 4 * ny, Z2), (nx + 2, 2 * ny, Z2)
+        [(32, Z1), (1, 32, 128)],
+        low, wide, high, seed, *coef1,
+    )
+    got = gather(send, nx, ny)
+    got_z = swap(got)
+    coarse = call(
+        lambda *refs: coarse_kernel(*refs, nx=nx, ny=ny), "coarse", 8,
+        [grid2] * 10 + [grid3] * 9,
+        [grid2] * 4 + [grid3] * 4 + [(8 * nx * ny, Z2), (1, 4 * nx * ny, Z2)],
+        got, got_z,
+    )
     level1 = [v1r, v1b, b1r, b1b, *coef1[:7], *coef1[8:]]
     (enext,) = call(
-        lambda *refs: up_kernel(*refs, nx=nx, ny=ny), "up", 24,
+        lambda *refs: up_kernel(*refs, nx=nx, ny=ny), "up", 10,
         [block],
-        [grid2] * 18 + [grid3] * 17
-        + [(4, 4 * ny, Z2)] * 2
-        + [(2, 8 * nx * ny, Z2), (2, max(8 * nx * ny, 256), Z2), (3, 320, 128)],
-        got, swap(got), *level1, *level0,
+        [grid2] * 4 + [grid3] * 4
+        + [(8 * nx * ny, Z2), (2, max(4 * nx * ny, 256), Z2), (3, 320, 128)],
+        got, got_z, *level1, *level0, *coarse,
     )
     return mnext, rnext, enext
 

time: 115 us -> 101 us (0.88)
  Pallas kernels: 34.7 us -> 21.5 us
    pallas_call x8 -> x10, Pallas kernels: 34.7 us -> 21.5 us  [call(): pl.pallas_call(kernel, out_shape=tuple((shape(*o) for o in outs)), in_spe...]
  transfers between devices with their start and end apart: 18 -> 18, of which waited for: 9 -> 9; matrix products, arithmetic and copies ran while one was open for 0% -> 0% of each run, Pallas kernels for 2% -> 3%
where the time goes in v3:
time: 101 us
  starting transfers between devices  32.7 us (32%)
  blocking collectives  29.5 us (29%)
  Pallas kernels  21.5 us (21%)
  waiting for transfers between devices  16.7 us (17%)
    pallas_call x10, Pallas kernels, call(): pl.pallas_call(kernel, out_shape=tuple((shape(*o) for o in outs)), in_spe...  21.5 us
    ppermute x10, starting transfers between devices, ring(): return lax.ppermute(x, axis, [(i, (i + step) % n) for i in range(n)])  19 us
    all_to_all x1, blocking collectives, gather(): lax.all_to_all(send, 'gx', 0, 0, tiled=True)  17.2 us
    ppermute x8, starting transfers between devices, swap(): return lax.ppermute(x, 'gz', [(0, 1), (1, 0)])  13.8 us
    all_to_all x1, blocking collectives, gather(): got = lax.all_to_all(send, 'gy', 0, 0, tiled=True)  12.3 us
    ppermute x10, waiting for transfers between devices, ring(): return lax.ppermute(x, axis, [(i, (i + step) % n) for i in range(n)])  12.2 us
    ppermute x8, waiting for transfers between devices, swap(): return lax.ppermute(x, 'gz', [(0, 1), (1, 0)])  4.46 us
  transfers between devices with their start and end apart: 18, of which 9 were waited for; matrix products, arithmetic and copies ran while one was open for 0% of the time, Pallas kernels for 3%

profile of v3, /device:TPU:1, one launch (start us, length us, event | category | flops | bytes accessed | tf_op | source)
XLA Modules:
  0.0 101.2 jit_solution(11606024679624864249)
XLA Ops:
  0.6 1.7 %prep.1 = (f32[66,16,256]{2,1,0:T(8,128)S(1)}, f32[20,16,256]{2,1,0:T(8,128)S(1)}, f32[20,16,256]{2,1,0:T(8,128)S(1)}, f32[18,24,256]{2,1,0:T(8,128)S(1)}, f32[18,24,256]{2,1,0:T(8,128)S(1)}) custom-call(f32[16,16,256]{2,1,0:T(8,128)} %m_in.3, f32[16,16,256]{2,1,0:T(8,128)} %r_in.3, f32[16,16,256]{2,1,0:T(8,128)} %u_in.1, f32[16,16,256]{2,1,0:T(8,128)} %f_in.1, ...), custom_call_target="tpu_custom_call" | custom-call | tf_op jit(solution)/shard_map/prep/pallas_call | solution.py:797
  2.3 3.3 %collective-permute-start = (f32[66,16,256]{2,1,0:T(8,128)S(1)}, f32[66,16,256]{2,1,0:T(8,128)S(1)}, u32[]{:S(2)}, u32[]{:S(2)}) collective-permute-start(f32[66,16,256]{2,1,0:T(8,128)S(1)} %get-tuple-element.65.refs_0_.own), channel_id=1, source_target_pairs={{0,1},{1,0},{2,3},{3,2},{4,5},{5,4},{6,7},{7,6},{8,9},{9,8},{10,11... | collective-permute-start | bytes 3244040 | tf_op jit(solution)/shard_map/ppermute | solution.py:787
  5.6 1.2 %collective-permute-start.5 = (f32[18,24,256]{2,1,0:T(8,128)S(1)}, f32[18,24,256]{2,1,0:T(8,128)S(1)}, u32[]{:S(2)}, u32[]{:S(2)}) collective-permute-start(f32[18,24,256]{2,1,0:T(8,128)S(1)} %get-tuple-element.68), channel_id=1, source_target_pairs={{0,2},{2,4},{4,6},{6,8},{8,10},{10,12},{12,14},{14,0},{1,3},{3,5},... | collective-permute-start | bytes 1327112 | tf_op jit(solution)/shard_map/ppermute | solution.py:783
  6.9 3.6 %collective-permute-start.3 = (f32[20,16,256]{2,1,0:T(8,128)S(1)}, f32[20,16,256]{2,1,0:T(8,128)S(1)}, u32[]{:S(2)}, u32[]{:S(2)}) collective-permute-start(f32[20,16,256]{2,1,0:T(8,128)S(1)} %get-tuple-element.67), channel_id=1, source_target_pairs={{0,240},{16,0},{32,16},{48,32},{64,48},{80,64},{96,80},{112,96},{1... | collective-permute-start | bytes 983048 | tf_op jit(solution)/shard_map/ppermute | solution.py:783
  10.5 3.9 %collective-permute-start.7 = (f32[18,24,256]{2,1,0:T(8,128)S(1)}, f32[18,24,256]{2,1,0:T(8,128)S(1)}, u32[]{:S(2)}, u32[]{:S(2)}) collective-permute-start(f32[18,24,256]{2,1,0:T(8,128)S(1)} %get-tuple-element.69), channel_id=1, source_target_pairs={{0,14},{2,0},{4,2},{6,4},{8,6},{10,8},{12,10},{14,12},{1,15},{3,1}... | collective-permute-start | bytes 1327112 | tf_op jit(solution)/shard_map/ppermute | solution.py:783
  14.4 3.7 %collective-permute-done.1.xlo.refs_2_ = f32[20,16,256]{2,1,0:T(8,128)S(1)} collective-permute-done((f32[20,16,256]{2,1,0:T(8,128)S(1)}, f32[20,16,256]{2,1,0:T(8,128)S(1)}, u32[]{:S(2)}, u32[]{:S(2)}) %collective-permute-start.1) | collective-permute-done | bytes 327712 | tf_op jit(solution)/shard_map/ppermute | solution.py:783
  19.3 1.7 %collective-permute-done.5.refs_6_ = f32[18,24,256]{2,1,0:T(8,128)S(1)} collective-permute-done((f32[18,24,256]{2,1,0:T(8,128)S(1)}, f32[18,24,256]{2,1,0:T(8,128)S(1)}, u32[]{:S(2)}, u32[]{:S(2)}) %collective-permute-start.5) | collective-permute-done | bytes 442400 | tf_op jit(solution)/shard_map/ppermute | solution.py:783
  21.0 2.3 %collective-permute-start.11 = (f32[20,8,256]{2,1,0:T(8,128)S(1)}, f32[20,8,256]{2,1,0:T(8,128)S(1)}, u32[]{:S(2)}, u32[]{:S(2)}) collective-permute-start(f32[20,8,256]{2,1,0:T(8,128)S(1)} %get-tuple-element.71), channel_id=1, source_target_pairs={{0,14},{2,0},{4,2},{6,4},{8,6},{10,8},{12,10},{14,12},{1,15},{3,1}... | collective-permute-start | bytes 491528 | tf_op jit(solution)/shard_map/ppermute | solution.py:783
  23.4 2.0 %collective-permute-start.6 = (f32[18,24,256]{2,1,0:T(8,128)S(1)}, f32[18,24,256]{2,1,0:T(8,128)S(1)}, u32[]{:S(2)}, u32[]{:S(2)}) collective-permute-start(f32[18,24,256]{2,1,0:T(8,128)S(1)} %collective-permute-done.5.refs_6_), channel_id=1, source_target_pairs={{0,1},{1,0},{2,3},{3,2},{4,5},{5,4},{6,7},{7,6},{8,9},{9,8},{10,11... | collective-permute-start | bytes 1327112 | tf_op jit(solution)/shard_map/ppermute | solution.py:787
  25.4 2.4 %collective-permute-done.9.refs_10_ = f32[20,8,256]{2,1,0:T(8,128)S(1)} collective-permute-done((f32[20,8,256]{2,1,0:T(8,128)S(1)}, f32[20,8,256]{2,1,0:T(8,128)S(1)}, u32[]{:S(2)}, u32[]{:S(2)}) %collective-permute-start.9) | collective-permute-done | bytes 163872 | tf_op jit(solution)/shard_map/ppermute | solution.py:783
  28.9 1.1 %collective-permute-done.10.refs_11_ = f32[20,8,256]{2,1,0:T(8,128)S(1)} collective-permute-done((f32[20,8,256]{2,1,0:T(8,128)S(1)}, f32[20,8,256]{2,1,0:T(8,128)S(1)}, u32[]{:S(2)}, u32[]{:S(2)}) %collective-permute-start.10) | collective-permute-done | bytes 163872 | tf_op jit(solution)/shard_map/ppermute | solution.py:787
  30.4 1.0 %collective-permute-done.12.refs_13_ = f32[20,8,256]{2,1,0:T(8,128)S(1)} collective-permute-done((f32[20,8,256]{2,1,0:T(8,128)S(1)}, f32[20,8,256]{2,1,0:T(8,128)S(1)}, u32[]{:S(2)}, u32[]{:S(2)}) %collective-permute-start.12) | collective-permute-done | bytes 163872 | tf_op jit(solution)/shard_map/ppermute | solution.py:787
  31.4 6.9 %fine.1 = (f32[16,16,256]{2,1,0:T(8,128)}, f32[2,4,8,256]{3,2,1,0:T(8,128)S(1)}, f32[10,24,256]{2,1,0:T(8,128)S(1)}, f32[10,24,256]{2,1,0:T(8,128)S(1)}, f32[14,...) custom-call(f32[66,16,256]{2,1,0:T(8,128)S(1)} %get-tuple-element.65, ...), custom_call_target="tpu_custom_call" | custom-call | tf_op jit(solution)/shard_map/fine/pallas_call | solution.py:797
  38.4 2.8 %collective-permute-start.14 = (f32[2,4,8,256]{3,2,1,0:T(8,128)S(1)}, f32[2,4,8,256]{3,2,1,0:T(8,128)S(1)}, u32[]{:S(2)}, u32[]{:S(2)}) collective-permute-start(f32[2,4,8,256]{3,2,1,0:T(8,128)S(1)} %get-tuple-element.76.own), channel_id=1, source_target_pairs={{0,14},{2,0},{4,2},{6,4},{8,6},{10,8},{12,10},{14,12},{1,15},{3,1}... | collective-permute-start | bytes 196616 | tf_op jit(solution)/shard_map/ppermute | solution.py:783
  41.2 1.3 %collective-permute-done.14.high = f32[2,4,8,256]{3,2,1,0:T(8,128)S(1)} collective-permute-done((f32[2,4,8,256]{3,2,1,0:T(8,128)S(1)}, f32[2,4,8,256]{3,2,1,0:T(8,128)S(1)}, u32[]{:S(2)}, u32[]{:S(2)}) %collective-permute-start.14) | collective-permute-done | bytes 65568 | tf_op jit(solution)/shard_map/ppermute | solution.py:783
  42.5 3.0 %collective-permute-done.13.low = f32[2,4,8,256]{3,2,1,0:T(8,128)S(1)} collective-permute-done((f32[2,4,8,256]{3,2,1,0:T(8,128)S(1)}, f32[2,4,8,256]{3,2,1,0:T(8,128)S(1)}, u32[]{:S(2)}, u32[]{:S(2)}) %collective-permute-start.13) | collective-permute-done | bytes 65568 | tf_op jit(solution)/shard_map/ppermute | solution.py:783
  45.6 4.8 %collective-permute-start.16 = (f32[2,2,24,256]{3,2,1,0:T(8,128)S(1)}, f32[2,2,24,256]{3,2,1,0:T(8,128)S(1)}, u32[]{:S(2)}, u32[]{:S(2)}) collective-permute-start(f32[2,2,24,256]{3,2,1,0:T(8,128)S(1)} %get-tuple-element.79), channel_id=1, source_target_pairs={{0,240},{16,0},{32,16},{48,32},{64,48},{80,64},{96,80},{112,96},{1... | collective-permute-start | bytes 294920 | tf_op jit(solution)/shard_map/ppermute | solution.py:783
  50.6 2.5 %middle_faces.1 = (f32[16,16,256]{2,1,0:T(8,128)}, f32[10,24,256]{2,1,0:T(8,128)S(1)}, f32[10,24,256]{2,1,0:T(8,128)S(1)}, f32[10,24,256]{2,1,0:T(8,128)S(1)}, f...) custom-call(f32[16,16,256]{2,1,0:T(8,128)} %m_in.3, ...), custom_call_target="tpu_custom_call" | custom-call | tf_op jit(solution)/shard_map/middle_faces/pallas_call | solution.py:797
  53.6 12.3 %all_to_all.10.got = f32[8,16,128]{2,1,0:T(8,128)S(1)} all-to-all(f32[8,16,128]{2,1,0:T(8,128)S(1)} %get-tuple-element.90), channel_id=1, replica_groups=mesh['gx'=16,'gy'=8,'gz'=2] {'gy'}, dimensions={0} | all-to-all | bytes 131072 | tf_op jit(solution)/shard_map/all_to_all | solution.py:791
  66.0 17.2 %all_to_all.11 = f32[16,8,16,128]{3,2,1,0:T(8,128)S(1)} all-to-all(f32[16,8,16,128]{3,2,1,0:T(8,128)S(1)} %spread.1), channel_id=1, replica_groups=mesh['gx'=16,'gy'=8,'gz'=2] {'gx'}, dimensions={0} | all-to-all | bytes 2097152 | tf_op jit(solution)/shard_map/all_to_all | solution.py:793
  83.2 6.1 %collective-permute-start.17 = (f32[128,16,128]{2,1,0:T(8,128)S(1)}, f32[128,16,128]{2,1,0:T(8,128)S(1)}, u32[]{:S(2)}, u32[]{:S(2)}) collective-permute-start(f32[128,16,128]{2,1,0:T(8,128)S(1)} %bitcast.1), channel_id=1, source_target_pairs={{0,1},{1,0},{2,3},{3,2},{4,5},{5,4},{6,7},{7,6},{8,9},{9,8},{10,11... | collective-permute-start | bytes 3145736 | tf_op jit(solution)/shard_map/ppermute | solution.py:787
  89.3 2.3 %collective-permute-done.17.refs_1_ = f32[128,16,128]{2,1,0:T(8,128)S(1)} collective-permute-done((f32[128,16,128]{2,1,0:T(8,128)S(1)}, f32[128,16,128]{2,1,0:T(8,128)S(1)}, u32[]{:S(2)}, u32[]{:S(2)}) %collective-permute-start.17) | collective-permute-done | bytes 1048608 | tf_op jit(solution)/shard_map/ppermute | solution.py:787
  91.5 2.7 %coarse.1 = (f32[34,32,128]{2,1,0:T(8,128)S(1)}, f32[34,32,128]{2,1,0:T(8,128)S(1)}, f32[34,32,128]{2,1,0:T(8,128)S(1)}, f32[34,32,128]{2,1,0:T(8,128)S(1)}, f32...) custom-call(f32[128,16,128]{2,1,0:T(8,128)S(1)} %bitcast.2, ...), custom_call_target="tpu_custom_call" | custom-call | tf_op jit(solution)/shard_map/coarse/pallas_call | solution.py:797
  94.3 6.9 %up.1 = f32[16,16,256]{2,1,0:T(8,128)} custom-call(f32[128,16,128]{2,1,0:T(8,128)S(1)} %bitcast.3, f32[128,16,128]{2,1,0:T(8,128)S(1)} %collective-permute-done.17.refs_1_, f32[10,24,256]{2,1,0:T(8,128)S(1)} %get-tuple-element.91.refs_2_, f32[10,24,256]{2,1,0:T(8,128)S(1)} %get-tuple-element.92.refs_3_, f32[10,24,256]{2,1,0:T(8,128)S(1)} %get-tuple-element.93.refs_4_, ...), custom_call_target="tpu_custom_call" | custom-call | tf_op jit(solution)/shard_map/up/pallas_call | solution.py:797
  (24 shorter events, 3.6 us)
Async XLA Ops:
  2.3 29.1 %collective-permute-start = (f32[66,16,256]{2,1,0:T(8,128)S(1)}, f32[66,16,256]{2,1,0:T(8,128)S(1)}, u32[]{:S(2)}, u32[]{:S(2)}) collective-permute-start(f32[66,16,256]{2,1,0:T(8,128)S(1)} %get-tuple-element.65.refs_0_.own), channel_id=1, source_target_pairs={{0,1},{1,0},{2,3},{3,2},{4,5},{5,4},{6,7},{7,6},{8,9},{9,8},{10,11... | collective-permute-start | bytes 3244040 | tf_op jit(solution)/shard_map/ppermute | solution.py:787
  5.6 12.5 %collective-permute-start.1 = (f32[20,16,256]{2,1,0:T(8,128)S(1)}, f32[20,16,256]{2,1,0:T(8,128)S(1)}, u32[]{:S(2)}, u32[]{:S(2)}) collective-permute-start(f32[20,16,256]{2,1,0:T(8,128)S(1)} %get-tuple-element.66), channel_id=1, source_target_pairs={{0,16},{16,32},{32,48},{48,64},{64,80},{80,96},{96,112},{112,128},... | collective-permute-start | bytes 983048 | tf_op jit(solution)/shard_map/ppermute | solution.py:783
  5.6 15.3 %collective-permute-start.5 = (f32[18,24,256]{2,1,0:T(8,128)S(1)}, f32[18,24,256]{2,1,0:T(8,128)S(1)}, u32[]{:S(2)}, u32[]{:S(2)}) collective-permute-start(f32[18,24,256]{2,1,0:T(8,128)S(1)} %get-tuple-element.68), channel_id=1, source_target_pairs={{0,2},{2,4},{4,6},{6,8},{8,10},{10,12},{12,14},{14,0},{1,3},{3,5},... | collective-permute-start | bytes 1327112 | tf_op jit(solution)/shard_map/ppermute | solution.py:783
  6.9 12.2 %collective-permute-start.3 = (f32[20,16,256]{2,1,0:T(8,128)S(1)}, f32[20,16,256]{2,1,0:T(8,128)S(1)}, u32[]{:S(2)}, u32[]{:S(2)}) collective-permute-start(f32[20,16,256]{2,1,0:T(8,128)S(1)} %get-tuple-element.67), channel_id=1, source_target_pairs={{0,240},{16,0},{32,16},{48,32},{64,48},{80,64},{96,80},{112,96},{1... | collective-permute-start | bytes 983048 | tf_op jit(solution)/shard_map/ppermute | solution.py:783
  10.5 12.9 %collective-permute-start.7 = (f32[18,24,256]{2,1,0:T(8,128)S(1)}, f32[18,24,256]{2,1,0:T(8,128)S(1)}, u32[]{:S(2)}, u32[]{:S(2)}) collective-permute-start(f32[18,24,256]{2,1,0:T(8,128)S(1)} %get-tuple-element.69), channel_id=1, source_target_pairs={{0,14},{2,0},{4,2},{6,4},{8,6},{10,8},{12,10},{14,12},{1,15},{3,1}... | collective-permute-start | bytes 1327112 | tf_op jit(solution)/shard_map/ppermute | solution.py:783
  18.1 10.2 %collective-permute-start.2 = (f32[20,16,256]{2,1,0:T(8,128)S(1)}, f32[20,16,256]{2,1,0:T(8,128)S(1)}, u32[]{:S(2)}, u32[]{:S(2)}) collective-permute-start(f32[20,16,256]{2,1,0:T(8,128)S(1)} %collective-permute-done.1.xlo.refs_2_), channel_id=1, source_target_pairs={{0,1},{1,0},{2,3},{3,2},{4,5},{5,4},{6,7},{7,6},{8,9},{9,8},{10,11... | collective-permute-start | bytes 983048 | tf_op jit(solution)/shard_map/ppermute | solution.py:787
  19.1 8.7 %collective-permute-start.9 = (f32[20,8,256]{2,1,0:T(8,128)S(1)}, f32[20,8,256]{2,1,0:T(8,128)S(1)}, u32[]{:S(2)}, u32[]{:S(2)}) collective-permute-start(f32[20,8,256]{2,1,0:T(8,128)S(1)} %get-tuple-element.70), channel_id=1, source_target_pairs={{0,2},{2,4},{4,6},{6,8},{8,10},{10,12},{12,14},{14,0},{1,3},{3,5},... | collective-permute-start | bytes 491528 | tf_op jit(solution)/shard_map/ppermute | solution.py:783
  21.0 7.4 %collective-permute-start.11 = (f32[20,8,256]{2,1,0:T(8,128)S(1)}, f32[20,8,256]{2,1,0:T(8,128)S(1)}, u32[]{:S(2)}, u32[]{:S(2)}) collective-permute-start(f32[20,8,256]{2,1,0:T(8,128)S(1)} %get-tuple-element.71), channel_id=1, source_target_pairs={{0,14},{2,0},{4,2},{6,4},{8,6},{10,8},{12,10},{14,12},{1,15},{3,1}... | collective-permute-start | bytes 491528 | tf_op jit(solution)/shard_map/ppermute | solution.py:783
  23.4 8.0 %collective-permute-start.6 = (f32[18,24,256]{2,1,0:T(8,128)S(1)}, f32[18,24,256]{2,1,0:T(8,128)S(1)}, u32[]{:S(2)}, u32[]{:S(2)}) collective-permute-start(f32[18,24,256]{2,1,0:T(8,128)S(1)} %collective-permute-done.5.refs_6_), channel_id=1, source_target_pairs={{0,1},{1,0},{2,3},{3,2},{4,5},{5,4},{6,7},{7,6},{8,9},{9,8},{10,11... | collective-permute-start | bytes 1327112 | tf_op jit(solution)/shard_map/ppermute | solution.py:787
  27.8 3.6 %collective-permute-start.8 = (f32[18,24,256]{2,1,0:T(8,128)S(1)}, f32[18,24,256]{2,1,0:T(8,128)S(1)}, u32[]{:S(2)}, u32[]{:S(2)}) collective-permute-start(f32[18,24,256]{2,1,0:T(8,128)S(1)} %collective-permute-done.7.refs_8_), channel_id=1, source_target_pairs={{0,1},{1,0},{2,3},{3,2},{4,5},{5,4},{6,7},{7,6},{8,9},{9,8},{10,11... | collective-permute-start | bytes 1327112 | tf_op jit(solution)/shard_map/ppermute | solution.py:787
  28.4 1.7 %collective-permute-start.10 = (f32[20,8,256]{2,1,0:T(8,128)S(1)}, f32[20,8,256]{2,1,0:T(8,128)S(1)}, u32[]{:S(2)}, u32[]{:S(2)}) collective-permute-start(f32[20,8,256]{2,1,0:T(8,128)S(1)} %collective-permute-done.9.refs_10_), channel_id=1, source_target_pairs={{0,1},{1,0},{2,3},{3,2},{4,5},{5,4},{6,7},{7,6},{8,9},{9,8},{10,11... | collective-permute-start | bytes 491528 | tf_op jit(solution)/shard_map/ppermute | solution.py:787
  28.4 3.0 %collective-permute-start.4 = (f32[20,16,256]{2,1,0:T(8,128)S(1)}, f32[20,16,256]{2,1,0:T(8,128)S(1)}, u32[]{:S(2)}, u32[]{:S(2)}) collective-permute-start(f32[20,16,256]{2,1,0:T(8,128)S(1)} %collective-permute-done.3.xhi.refs_4_), channel_id=1, source_target_pairs={{0,1},{1,0},{2,3},{3,2},{4,5},{5,4},{6,7},{7,6},{8,9},{9,8},{10,11... | collective-permute-start | bytes 983048 | tf_op jit(solution)/shard_map/ppermute | solution.py:787
  30.0 1.4 %collective-permute-start.12 = (f32[20,8,256]{2,1,0:T(8,128)S(1)}, f32[20,8,256]{2,1,0:T(8,128)S(1)}, u32[]{:S(2)}, u32[]{:S(2)}) collective-permute-start(f32[20,8,256]{2,1,0:T(8,128)S(1)} %collective-permute-done.11.refs_12_), channel_id=1, source_target_pairs={{0,1},{1,0},{2,3},{3,2},{4,5},{5,4},{6,7},{7,6},{8,9},{9,8},{10,11... | collective-permute-start | bytes 491528 | tf_op jit(solution)/shard_map/ppermute | solution.py:787
  38.4 4.2 %collective-permute-start.14 = (f32[2,4,8,256]{3,2,1,0:T(8,128)S(1)}, f32[2,4,8,256]{3,2,1,0:T(8,128)S(1)}, u32[]{:S(2)}, u32[]{:S(2)}) collective-permute-start(f32[2,4,8,256]{3,2,1,0:T(8,128)S(1)} %get-tuple-element.76.own), channel_id=1, source_target_pairs={{0,14},{2,0},{4,2},{6,4},{8,6},{10,8},{12,10},{14,12},{1,15},{3,1}... | collective-permute-start | bytes 196616 | tf_op jit(solution)/shard_map/ppermute | solution.py:783
  41.2 4.3 %collective-permute-start.13 = (f32[2,4,8,256]{3,2,1,0:T(8,128)S(1)}, f32[2,4,8,256]{3,2,1,0:T(8,128)S(1)}, u32[]{:S(2)}, u32[]{:S(2)}) collective-permute-start(f32[2,4,8,256]{3,2,1,0:T(8,128)S(1)} %get-tuple-element.76.own), channel_id=1, source_target_pairs={{0,2},{2,4},{4,6},{6,8},{8,10},{10,12},{12,14},{14,0},{1,3},{3,5},... | collective-permute-start | bytes 196616 | tf_op jit(solution)/shard_map/ppermute | solution.py:783
  45.6 7.6 %collective-permute-start.15 = (f32[2,2,24,256]{3,2,1,0:T(8,128)S(1)}, f32[2,2,24,256]{3,2,1,0:T(8,128)S(1)}, u32[]{:S(2)}, u32[]{:S(2)}) collective-permute-start(f32[2,2,24,256]{3,2,1,0:T(8,128)S(1)} %get-tuple-element.77), channel_id=1, source_target_pairs={{0,16},{16,32},{32,48},{48,64},{64,80},{80,96},{96,112},{112,128},... | collective-permute-start | bytes 294920 | tf_op jit(solution)/shard_map/ppermute | solution.py:783
  45.6 7.5 %collective-permute-start.16 = (f32[2,2,24,256]{3,2,1,0:T(8,128)S(1)}, f32[2,2,24,256]{3,2,1,0:T(8,128)S(1)}, u32[]{:S(2)}, u32[]{:S(2)}) collective-permute-start(f32[2,2,24,256]{3,2,1,0:T(8,128)S(1)} %get-tuple-element.79), channel_id=1, source_target_pairs={{0,240},{16,0},{32,16},{48,32},{64,48},{80,64},{96,80},{112,96},{1... | collective-permute-start | bytes 294920 | tf_op jit(solution)/shard_map/ppermute | solution.py:783
  83.2 8.3 %collective-permute-start.17 = (f32[128,16,128]{2,1,0:T(8,128)S(1)}, f32[128,16,128]{2,1,0:T(8,128)S(1)}, u32[]{:S(2)}, u32[]{:S(2)}) collective-permute-start(f32[128,16,128]{2,1,0:T(8,128)S(1)} %bitcast.1), channel_id=1, source_target_pairs={{0,1},{1,0},{2,3},{3,2},{4,5},{5,4},{6,7},{7,6},{8,9},{9,8},{10,11... | collective-permute-start | bytes 3145736 | tf_op jit(solution)/shard_map/ppermute | solution.py:787

commit v4 on v3

--- a/solution.py
+++ b/solution.py
@@ -15,6 +15,7 @@
 BX, BY, BZ = 16, 16, 256
 H = 3
 SF, SI, SH, SHB, S1, S2, SU, S22, S3 = 3, 4, 4, 5, 8, 8, 8, 16, 16
+AT_IN, AT_W, AT_U, AT_MEAN = BX, 2 * BX, 3 * BX, 3 * BX + BX // 2
 K0, Y0, Z0 = BX // 2 + 2 * H, 32, 384
 K1, Y1, Z1 = BX // 4 + 2 * H, 24, BZ
 Z2 = BZ // 2
@@ -234,11 +235,6 @@
     return i // 4, slice(rows, rows + 8), slice(lanes, lanes + 128)
 
 
-def block_of24(i):
-    tile, half = (i % 6) // 2, i % 2
-    return i // 6, slice(8 * tile, 8 * tile + 8), slice(128 * half, 128 * half + 128)
-
-
 def prep_kernel(
     m_in, r_in, u_in, f_in, labels_in, own, xup, xdn, yup, ydn, m, r, u, f, labels, fold, sems
 ):
@@ -258,37 +254,49 @@
             mm, rr, uu = m[x], r[x], u[x]
             inner = factor * f[x]
             own[x] = mm + uu
-            own[BX + x] = inner
+            own[AT_IN + x] = inner
             ionic = IONIC_GAIN * mm * (mm - IONIC_ONSET) * (mm - 1.0) + mm * rr
-            own[2 * BX + x] = mm - jnp.where(kind > 0.5, TIME_STEP * ionic, 0.0)
-            own[3 * BX + x] = uu
+            own[AT_W + x] = mm - jnp.where(kind > 0.5, TIME_STEP * ionic, 0.0)
+            if x % 2:
+                first = first_is_red((BY, BZ))
+                own[AT_U + x // 2] = jnp.where(first, uu, u[x - 1])
     sums = jnp.concatenate(
-        [own[BX + 2 * p] + own[BX + 2 * p + 1] for p in range(BX // 2)], axis=0
+        [own[AT_IN + 2 * p] + own[AT_IN + 2 * p + 1] for p in range(BX // 2)], axis=0
     )
     mean = sum_rows(fold, dot(sums, pair_matrix(BZ, BZ // 2, 0.125)))
     for i in range(8):
         slab, rows, lanes = block_of(i)
-        own[4 * BX + slab, rows, lanes] = mean[8 * i : 8 * i + 8]
-        slab, rows, lanes = block_of24(i)
-        yup[BX + slab, rows, lanes] = mean[8 * i : 8 * i + 8]
-        ydn[BX + slab, rows, lanes] = mean[8 * i : 8 * i + 8]
+        for ref, base in ((own, AT_MEAN), (yup, BX), (ydn, BX)):
+            ref[base + slab, rows, lanes] = mean[8 * i : 8 * i + 8]
     for i in range(5):
         slab, rows, lanes = block_of(i)
-        xup[18 + slab, rows, lanes] = mean[8 * (3 + i) : 8 * (4 + i)]
-        xdn[18 + slab, rows, lanes] = mean[8 * i : 8 * i + 8]
+        xup[16 + slab, rows, lanes] = mean[8 * (3 + i) : 8 * (4 + i)]
+        xdn[16 + slab, rows, lanes] = mean[8 * i : 8 * i + 8]
     base = 0
-    for q, depth in enumerate((5, 5, 4, 4)):
-        xup[base : base + depth] = own[BX * (q + 1) - depth : BX * (q + 1)]
-        xdn[base : base + depth] = own[BX * q : BX * q + depth]
+    for start, count, depth in ((0, BX, 5), (AT_IN, BX, 5), (AT_W, BX, 4), (AT_U, BX // 2, 2)):
+        xup[base : base + depth] = own[start + count - depth : start + count]
+        xdn[base : base + depth] = own[start : start + depth]
         base += depth
     row = iota((8, BZ), 0)
-    for x in range(BX):
-        for q in (0, 1):
-            yup[x, 8 * q : 8 * q + 8] = own[BX * q + x, 8:16]
-            ydn[x, 8 * q : 8 * q + 8] = own[BX * q + x, 0:8]
-        w, v = own[2 * BX + x], own[3 * BX + x]
-        yup[x, 16:24] = merge(True, w[8:16], v[8:16])
-        ydn[x, 16:24] = merge(False, w[0:8], v[0:8])
+    turn = lambda x, by: pltpu.roll(x, by % 8, 0)
+    for p in range(BX // 2):
+        for out, rows, keep, by, fourth in (
+            (yup, slice(8, 16), row >= 3, 3, (4, 5, 6)),
+            (ydn, slice(0, 8), row < 5, 5, (2, 3, 4)),
+        ):
+            s = [own[2 * p + i, rows] for i in (0, 1)]
+            n = [own[AT_IN + 2 * p + i, rows] for i in (0, 1)]
+            rest = [own[AT_W + 2 * p, rows], own[AT_W + 2 * p + 1, rows], own[AT_U + p, rows]]
+            at = 0 if out is yup else 5
+            last = jnp.where(
+                row == at,
+                turn(rest[0], fourth[0]),
+                jnp.where(row == at + 1, turn(rest[1], fourth[1]), turn(rest[2], fourth[2])),
+            )
+            out[2 * p, 0:8] = jnp.where(keep, s[0], turn(rest[0], by))
+            out[2 * p, 8:16] = jnp.where(keep, s[1], turn(rest[1], by))
+            out[2 * p + 1, 0:8] = jnp.where(keep, n[0], turn(rest[2], by))
+            out[2 * p + 1, 8:16] = jnp.where(keep, n[1], last)
 
 
 def merge(high, a, b):
@@ -303,27 +311,27 @@
         rows = slice(8, 16) if high else slice(0, 8)
         for side, src in ((0, xlo), (1, xhi)):
             at = lambda base, depth, d: src[base + (depth - d if side == 0 else d - 1), rows]
-            s, n, w, u = (
+            s, n, w = (
                 lambda d: at(0, 5, d),
                 lambda d: at(5, 5, d),
                 lambda d: at(10, 4, d),
-                lambda d: at(14, 4, d),
             )
+            u = lambda d: at(14, 2, d)
             tiles = [
                 merge(high, s(1), s(2)),
                 merge(high, s(3), s(4)),
                 merge(high, n(1), n(2)),
                 merge(high, n(3), n(4)),
                 merge(high, w(1), w(2)),
-                merge(high, u(1), u(2)),
-                merge(high, w(3), u(3)),
+                merge(high, w(3), u(1)),
+                u(2),
             ]
             for t, tile in enumerate(tiles):
                 out[10 * side + t] = tile
 
             def coarse(d):
                 slab, block_rows, lanes = block_of(5 - d if side == 0 else d - 1)
-                return src[18 + slab, block_rows, lanes]
+                return src[16 + slab, block_rows, lanes]
 
             for d in range(1, 6):
                 tile, lanes = 10 * side + 7 + (d - 1) // 2, 128 * ((d - 1) % 2)
@@ -332,7 +340,7 @@
 
 def fine_kernel(*refs):
     pieces, refs = refs[:14], refs[14:]
-    mnext, rhs1, refs = refs[0], refs[1], refs[2:]
+    mnext, rhs1, rup, rdn, refs = refs[0], refs[1], refs[2], refs[3], refs[4:]
     mean1, refs = refs[0:2], refs[2:]
     v, b, near, fars, ys, zs, inv, refs = (
         refs[0:2], refs[2:4], refs[4], refs[5:7], refs[7:9], refs[9:11], refs[11:13], refs[13:],
@@ -344,7 +352,7 @@
     mout, sems = refs[10], refs[11]
     core = lax.axis_index("gz")
     has = flags()
-    fields = (s, inner, w, v)
+    fields = (s, inner, w)
     for side in (0, 1):
         own, xlo, xhi, ylo, yhi, clo, chi = pieces[side::2]
         wide = BZ if side == 0 else 128
@@ -356,22 +364,29 @@
             k = p + H
             for q, bufs in enumerate(fields):
                 put(bufs, k, mid, dst, own[BX * q + 2 * p, :, src], own[BX * q + 2 * p + 1, :, src])
-            for rows, ref, flag in ((low, ylo, has[2]), (high, yhi, has[3])):
-                for q in (0, 1):
-                    part = slice(8 * q, 8 * q + 8)
-                    put(
-                        fields[q], k, rows, dst,
-                        ref[2 * p, part, src] * flag, ref[2 * p + 1, part, src] * flag,
-                    )
-                a, c = (ref[2 * p + i, 16:24, src] * flag for i in (0, 1))
-                put(w, k, rows, dst, a, c)
-                put(v, k, rows, dst, pltpu.roll(a, 4, 0), pltpu.roll(c, 4, 0))
+            v[1][k, mid, dst] = own[AT_U + p, :, src]
+            row = iota((8, wide), 0)
+            turn = lambda x, by: pltpu.roll(x, by, 0)
+            for rows, ref, flag, keep, deep, by, fourth in (
+                (low, ylo, has[2], row >= 3, row >= 5, 5, (4, 3, 2)),
+                (high, yhi, has[3], row < 5, row < 3, 3, (6, 5, 4)),
+            ):
+                t = [
+                    ref[2 * p + i // 2, 8 * (i % 2) : 8 * (i % 2) + 8, src] * flag for i in range(4)
+                ]
+                put(s, k, rows, dst, t[0], t[1])
+                put(inner, k, rows, dst, jnp.where(keep, t[2], 0.0), jnp.where(keep, t[3], 0.0))
+                rest = [
+                    jnp.where(deep, turn(t[i], by), turn(t[3], fourth[i])) for i in (0, 1, 2)
+                ]
+                put(w, k, rows, dst, rest[0], rest[1])
+                v[1][k, rows, dst] = rest[2]
 
         loop(0, BX // 2, 1, body)
         for x_side, ref, flag in ((0, xlo, has[0]), (1, xhi, has[1])):
             base = 0
             order = (5, 4, 3, 2, 1) if x_side == 0 else (1, 2, 3, 4, 5)
-            for q, depth in enumerate((5, 5, 4, 4)):
+            for q, depth in enumerate((5, 5, 4)):
                 slabs = {d: ref[base + i, :, src] * flag for i, d in enumerate(
                     [d for d in order if d <= depth])}
                 base += depth
@@ -384,6 +399,11 @@
                     if pair[0] is None and pair[1] is None:
                         pair = (jnp.zeros((16, wide), F32), None)
                     put(fields[q], k, mid, dst, *pair)
+            black = [ref[14, :, src] * flag, ref[15, :, src] * flag, jnp.zeros((16, wide), F32)]
+            if x_side == 0:
+                black[0], black[1] = black[1], black[0]
+            for j in range(H):
+                v[1][H - 1 - j if x_side == 0 else K0 - H + j, mid, dst] = black[j]
             for rows, cref, yflag in ((low, clo, has[2]), (high, chi, has[3])):
                 both = flag * yflag
                 tile = [cref[10 * x_side + t, :, src] * both for t in range(7)]
@@ -392,10 +412,12 @@
                 by_field = (
                     (tile[0], turned[0], tile[1], turned[1]),
                     (tile[2], turned[2], tile[3], turned[3]),
-                    (tile[4], turned[4], tile[6], zero),
-                    (tile[5], turned[5], turned[6], zero),
+                    (tile[4], turned[4], tile[5], zero),
                 )
-                for q in range(4):
+                black = (turned[5], tile[6], zero)
+                for j in range(H):
+                    v[1][H - 1 - j if x_side == 0 else K0 - H + j, rows, dst] = black[j]
+                for q in range(3):
                     slabs = by_field[q] + (zero, zero)
                     for j in range(H):
                         pair = (slabs[2 * j], slabs[2 * j + 1])
@@ -405,19 +427,19 @@
         for p in range(4):
             def of_own(i):
                 slab, rows, lanes = block_of(i)
-                return own[4 * BX + slab, rows, lanes]
+                return own[AT_MEAN + slab, rows, lanes]
 
             put(mean1, p + H, slice(8, 16), dst, of_own(2 * p), of_own(2 * p + 1))
             for rows, ref, flag in ((slice(0, 8), ylo, has[2]), (slice(16, 24), yhi, has[3])):
                 def of_y(i):
-                    slab, part, lanes = block_of24(i)
+                    slab, part, lanes = block_of(i)
                     return ref[BX + slab, part, lanes] * flag
 
                 put(mean1, p + H, rows, dst, of_y(2 * p), of_y(2 * p + 1))
         for x_side, ref, flag in ((0, xlo, has[0]), (1, xhi, has[1])):
             def of_x(d):
                 slab, part, lanes = block_of(5 - d if x_side == 0 else d - 1)
-                return ref[18 + slab, part, lanes] * flag
+                return ref[16 + slab, part, lanes] * flag
 
             zero = jnp.zeros((8, 128), F32)
             mids = [of_x(d) for d in (1, 2, 3, 4, 5)] + [zero]
@@ -500,8 +522,11 @@
     pairs = pair_matrix(Z0, Z1, 0.5, core * 64)
     coarse = sum_rows(fold2, dot(fold[...].reshape(half, Z0), pairs)).reshape(8, 8, Z1)
     red, black = colours(coarse)
-    rhs1[0] = red
-    rhs1[1] = black
+    for c, pairs in ((0, red), (1, black)):
+        rhs1[c] = pairs
+        for j in (0, 1):
+            rup[c, j] = merge(True, pairs[2 * j], pairs[2 * j + 1])
+            rdn[c, j] = merge(False, pairs[2 * j], pairs[2 * j + 1])
     copies[0].wait()
 
 
@@ -530,15 +555,16 @@
 
 
 def join_kernel(low, own, high, wide, xup, xdn):
+    row = iota((8, Z1), 0)
     for c in (0, 1):
         for p in range(4):
-            for i, ref in enumerate((low, own, high)):
-                rows = slice(8 * i, 8 * i + 8)
-                wide[c, p, rows] = ref[c, p]
-                if p < 2:
-                    xdn[c, p, rows] = ref[c, p]
-                else:
-                    xup[c, p - 2, rows] = ref[c, p]
+            a, b = low[c, p // 2], high[c, p // 2]
+            edge = jnp.where(row >= 4, a, b) if p % 2 == 0 else pltpu.roll(
+                jnp.where(row < 4, a, b), 4, 0
+            )
+            for ref, q in ((wide, p), (xdn, p) if p < 2 else (xup, p - 2)):
+                ref[c, q, 0:8] = edge
+                ref[c, q, 8:16] = own[c, p]
 
 
 def spread_kernel(got, send):
@@ -559,7 +585,9 @@
         b[c][K1 - 1 :] = jnp.zeros((1, Y1, Z1), F32)
         for k in range(1, K1 - 1):
             src = low[c, k - 1] if k < H else (own[c, k - H] if k < H + 4 else high[c, k - H - 4])
-            b[c][k] = src * outside((Y1, Z1), 8, k, 4, has)
+            inside = outside((Y1, Z1), 8, k, 4, has)
+            for rows, part in ((slice(0, 8), src[0:8]), (slice(8, 16), src[8:16]), (slice(16, 24), src[0:8])):
+                b[c][k, rows] = part * inside[rows]
     coef = (near, fars, ys, zs)
     from_zero(v, b, coef, inv, 1, K1 - 1, S1)
     first = first_is_red((2, Y1, Z1))
@@ -588,7 +616,7 @@
         total = None
         for i in (2 * p, 2 * p + 1):
             slab, rows, lanes = block_of(i)
-            block = own[4 * BX + slab, rows, lanes]
+            block = own[AT_MEAN + slab, rows, lanes]
             total = block if total is None else total + block
         sums.append(total)
     both = sum_rows(fold, dot(jnp.concatenate(sums, axis=0), pair_matrix(Z2, Z2, 0.125)))
@@ -724,8 +752,7 @@
     for k in range(0, near2, 4):
         e = fold1[0, k * y2 : (k + 4) * y2, :].reshape(4, y2, Z2)
         here = pl.ds(base + 1 + k, 4)
-        for c in (0, 1):
-            v2[c][here] = v2[c][here] + e
+        v2[1][here] = v2[1][here] + e
     half_sweep(v2, b2, 0, coef2, inv2, base + 1, base + 1 + near2, near2)
     half_sweep(v2, b2, 1, coef2, inv2, base + 1, base + 1 + near2, near2)
     shift = lax.rem(4 - 4 * gy_me + 2 * y2, y2)
@@ -738,8 +765,7 @@
     twice_rows(fold1, dot(jnp.concatenate(cells, axis=0), copy_matrix(Z2, Z1)))
     for k in range(1, K1 - 1):
         e = columns(fold1, 32 * (k - 1), Y1, Z1)
-        for c in (0, 1):
-            v1[c][k] = jnp.where(inv1[c][k] > 0.0, v1[c][k] + e, 0.0)
+        v1[1][k] = jnp.where(inv1[1][k] > 0.0, v1[1][k] + e, 0.0)
     half_sweep(v1, b1, 0, coef1, inv1, 1, K1 - 1, S1)
     half_sweep(v1, b1, 1, coef1, inv1, 1, K1 - 1, S1)
     first0 = first_is_red((Y1, Z1))
@@ -753,8 +779,7 @@
     def body(p):
         e = columns(fold0, pl.multiple_of(p * 32, 32), 32, Z0)[None]
         here = pl.ds(p + H - 1, 1)
-        for c in (0, 1):
-            v0[c][here] = jnp.where(inv0[c][here] > 0.0, v0[c][here] + e, 0.0)
+        v0[1][here] = jnp.where(inv0[1][here] > 0.0, v0[1][here] + e, 0.0)
 
     loop(0, BX // 2 + 2, 1, body)
     half_sweep(v0, b0, 0, coef0, inv0, H - 1, K0 - H + 1, SHB)
@@ -814,7 +839,7 @@
     ]
     own, xup, xdn, yup, ydn = call(
         prep_kernel, "prep", 6,
-        [(4 * BX + 2, BY, BZ)] + [(20, BY, BZ)] * 2 + [(BX + 2, 24, BZ)] * 2,
+        [(AT_MEAN + 2, BY, BZ)] + [(18, BY, BZ)] * 4,
         [block] * 4
         + [pltpu.VMEM(labels.shape, jnp.int32), (1, 128, 128), pltpu.SemaphoreType.DMA((5,))],
         *held, hbm_in=5,
@@ -822,7 +847,7 @@
     xlo, xhi = ring(xup, "gx", 1), ring(xdn, "gx", -1)
     ylo, yhi = ring(yup, "gy", 1), ring(ydn, "gy", -1)
     cup, cdn = call(corner_kernel, "corner", 4, [(20, 8, BZ)] * 2, [], xlo, xhi)
-    clo, chi = ring(cup, "gy", 1), ring(cdn, "gy", -1)
+    clo, chi = lax.optimization_barrier((ring(cup, "gy", 1), ring(cdn, "gy", -1)))
     halos = []
     for piece in (own, xlo, xhi, ylo, yhi, clo, chi):
         halos += [piece, swap(piece)]
@@ -830,9 +855,9 @@
     fine = (K0, Y0, Z0)
     mid = (K1, Y1, Z1)
     grid2, grid3 = (2 * nx + 2, 4 * ny, Z2), (nx + 2, 2 * ny, Z2)
-    mnext, rhs1, in1r, in1b, *level0 = call(
+    mnext, rhs1, rup, rdn, in1r, in1b, *level0 = call(
         fine_kernel, "fine", 20,
-        [block, (2, 4, 8, Z1)] + [mid] * 2 + [fine] * 13,
+        [block, (2, 4, 8, Z1), (2, 2, 8, Z1), (2, 2, 8, Z1)] + [mid] * 2 + [fine] * 13,
         [fine] * 16
         + [(8, BY, Z0), (2, 128, 128), block, pltpu.SemaphoreType.DMA((1,))],
         *halos, hbm_out=1,
@@ -842,10 +867,10 @@
         [mid] * 2 + [block] * 2 + [pltpu.SemaphoreType.DMA((2,))],
         held[0], held[1], in1r, in1b, hbm_in=2, hbm_out=1,
     )
-    part = (2, 2, Y1, Z1)
+    part = (2, 2, 16, Z1)
     wide, xup, xdn = call(
-        join_kernel, "join", 4, [(2, 4, Y1, Z1), part, part], [],
-        ring(rhs1, "gy", 1), rhs1, ring(rhs1, "gy", -1),
+        join_kernel, "join", 4, [(2, 4, 16, Z1), part, part], [],
+        ring(rup, "gy", 1), rhs1, ring(rdn, "gy", -1),
     )
     low, high = ring(xup, "gx", 1), ring(xdn, "gx", -1)
     v1r, v1b, b1r, b1b, send = call(

time: 101 us -> 96.6 us (0.956)
  waiting for transfers between devices: 16.7 us -> 11.5 us
    ppermute x10, waiting for transfers between devices: 12.2 us -> 8.01 us  [ring(): return lax.ppermute(x, axis, [(i, (i + step) % n) for i in range(n)])]
    ppermute x8, starting transfers between devices: 13.8 us -> 14.9 us  [swap(): return lax.ppermute(x, 'gz', [(0, 1), (1, 0)])]
    ppermute x8, waiting for transfers between devices: 4.46 us -> 3.45 us  [swap(): return lax.ppermute(x, 'gz', [(0, 1), (1, 0)])]
  transfers between devices with their start and end apart: 18 -> 18, of which waited for: 9 -> 8; matrix products, arithmetic and copies ran while one was open for 0% -> 0% of each run, Pallas kernels for 3% -> 3%
where the time goes in v4:
time: 96.6 us; the launch traced here: 96.4 us
  starting transfers between devices  33 us (34%)
  blocking collectives  29.8 us (31%)
  Pallas kernels  21.4 us (22%)
  waiting for transfers between devices  11.5 us (12%)
    pallas_call x10, Pallas kernels, call(): pl.pallas_call(kernel, out_shape=tuple((shape(*o) for o in outs)), in_spe...  21.4 us
    ppermute x10, starting transfers between devices, ring(): return lax.ppermute(x, axis, [(i, (i + step) % n) for i in range(n)])  18.1 us
    all_to_all x1, blocking collectives, gather(): lax.all_to_all(send, 'gx', 0, 0, tiled=True)  16.8 us
    ppermute x8, starting transfers between devices, swap(): return lax.ppermute(x, 'gz', [(0, 1), (1, 0)])  14.9 us
    all_to_all x1, blocking collectives, gather(): got = lax.all_to_all(send, 'gy', 0, 0, tiled=True)  12.9 us
    ppermute x10, waiting for transfers between devices, ring(): return lax.ppermute(x, axis, [(i, (i + step) % n) for i in range(n)])  8.01 us
    ppermute x8, waiting for transfers between devices, swap(): return lax.ppermute(x, 'gz', [(0, 1), (1, 0)])  3.45 us
  transfers between devices with their start and end apart: 18, of which 8 were waited for; matrix products, arithmetic and copies ran while one was open for 0% of the time, Pallas kernels for 3%

profile of v4, /device:TPU:1, one launch (start us, length us, event | category | flops | bytes accessed | tf_op | source)
XLA Modules:
  0.0 96.4 jit_solution(12700427057811733624)
XLA Ops:
  0.6 1.7 %prep.1 = (f32[58,16,256]{2,1,0:T(8,128)S(1)}, f32[18,16,256]{2,1,0:T(8,128)S(1)}, f32[18,16,256]{2,1,0:T(8,128)S(1)}, f32[18,16,256]{2,1,0:T(8,128)S(1)}, f32[18,16,256]{2,1,0:T(8,128)S(1)}) custom-call(f32[16,16,256]{2,1,0:T(8,128)} %m_in.3, f32[16,16,256]{2,1,0:T(8,128)} %r_in.3, f32[16,16,256]{2,1,0:T(8,128)} %u_in.1, f32[16,16,256]{2,1,0:T(8,128)} %f_in.1, ...), custom_call_target="tpu_custom_call" | custom-call | tf_op jit(solution)/shard_map/prep/pallas_call | solution.py:822
  2.4 3.3 %collective-permute-start = (f32[58,16,256]{2,1,0:T(8,128)S(1)}, f32[58,16,256]{2,1,0:T(8,128)S(1)}, u32[]{:S(2)}, u32[]{:S(2)}) collective-permute-start(f32[58,16,256]{2,1,0:T(8,128)S(1)} %get-tuple-element.69.refs_0_.own), channel_id=1, source_target_pairs={{0,1},{1,0},{2,3},{3,2},{4,5},{5,4},{6,7},{7,6},{8,9},{9,8},{10,11... | collective-permute-start | bytes 2850824 | tf_op jit(solution)/shard_map/ppermute | solution.py:812
  5.6 4.8 %collective-permute-start.3 = (f32[18,16,256]{2,1,0:T(8,128)S(1)}, f32[18,16,256]{2,1,0:T(8,128)S(1)}, u32[]{:S(2)}, u32[]{:S(2)}) collective-permute-start(f32[18,16,256]{2,1,0:T(8,128)S(1)} %get-tuple-element.71), channel_id=1, source_target_pairs={{0,240},{16,0},{32,16},{48,32},{64,48},{80,64},{96,80},{112,96},{1... | collective-permute-start | bytes 884744 | tf_op jit(solution)/shard_map/ppermute | solution.py:808
  10.5 3.9 %collective-permute-start.7 = (f32[18,16,256]{2,1,0:T(8,128)S(1)}, f32[18,16,256]{2,1,0:T(8,128)S(1)}, u32[]{:S(2)}, u32[]{:S(2)}) collective-permute-start(f32[18,16,256]{2,1,0:T(8,128)S(1)} %get-tuple-element.73), channel_id=1, source_target_pairs={{0,14},{2,0},{4,2},{6,4},{8,6},{10,8},{12,10},{14,12},{1,15},{3,1}... | collective-permute-start | bytes 884744 | tf_op jit(solution)/shard_map/ppermute | solution.py:808
  14.4 3.0 %collective-permute-done.1.xlo.refs_2_ = f32[18,16,256]{2,1,0:T(8,128)S(1)} collective-permute-done((f32[18,16,256]{2,1,0:T(8,128)S(1)}, f32[18,16,256]{2,1,0:T(8,128)S(1)}, u32[]{:S(2)}, u32[]{:S(2)}) %collective-permute-start.1) | collective-permute-done | bytes 294944 | tf_op jit(solution)/shard_map/ppermute | solution.py:808
  17.8 1.1 %collective-permute-start.2 = (f32[18,16,256]{2,1,0:T(8,128)S(1)}, f32[18,16,256]{2,1,0:T(8,128)S(1)}, u32[]{:S(2)}, u32[]{:S(2)}) collective-permute-start(f32[18,16,256]{2,1,0:T(8,128)S(1)} %collective-permute-done.1.xlo.refs_2_), channel_id=1, source_target_pairs={{0,1},{1,0},{2,3},{3,2},{4,5},{5,4},{6,7},{7,6},{8,9},{9,8},{10,11... | collective-permute-start | bytes 884744 | tf_op jit(solution)/shard_map/ppermute | solution.py:812
  18.9 2.5 %collective-permute-done.5.refs_6_ = f32[18,16,256]{2,1,0:T(8,128)S(1)} collective-permute-done((f32[18,16,256]{2,1,0:T(8,128)S(1)}, f32[18,16,256]{2,1,0:T(8,128)S(1)}, u32[]{:S(2)}, u32[]{:S(2)}) %collective-permute-start.5) | collective-permute-done | bytes 294944 | tf_op jit(solution)/shard_map/ppermute | solution.py:808
  21.3 1.3 %collective-permute-start.10 = (f32[20,8,256]{2,1,0:T(8,128)S(1)}, f32[20,8,256]{2,1,0:T(8,128)S(1)}, u32[]{:S(2)}, u32[]{:S(2)}) collective-permute-start(f32[20,8,256]{2,1,0:T(8,128)S(1)} %get-tuple-element.75), channel_id=1, source_target_pairs={{0,14},{2,0},{4,2},{6,4},{8,6},{10,8},{12,10},{14,12},{1,15},{3,1}... | collective-permute-start | bytes 491528 | tf_op jit(solution)/shard_map/ppermute | solution.py:808
  22.6 1.5 %collective-permute-start.4 = (f32[18,16,256]{2,1,0:T(8,128)S(1)}, f32[18,16,256]{2,1,0:T(8,128)S(1)}, u32[]{:S(2)}, u32[]{:S(2)}) collective-permute-start(f32[18,16,256]{2,1,0:T(8,128)S(1)} %collective-permute-done.3.xhi.refs_4_), channel_id=1, source_target_pairs={{0,1},{1,0},{2,3},{3,2},{4,5},{5,4},{6,7},{7,6},{8,9},{9,8},{10,11... | collective-permute-start | bytes 884744 | tf_op jit(solution)/shard_map/ppermute | solution.py:812
  24.2 1.3 %collective-permute-done.9.refs_10_ = f32[20,8,256]{2,1,0:T(8,128)S(1)} collective-permute-done((f32[20,8,256]{2,1,0:T(8,128)S(1)}, f32[20,8,256]{2,1,0:T(8,128)S(1)}, u32[]{:S(2)}, u32[]{:S(2)}) %collective-permute-start.9) | collective-permute-done | bytes 163872 | tf_op jit(solution)/shard_map/ppermute | solution.py:808
  25.5 1.4 %collective-permute-start.6 = (f32[18,16,256]{2,1,0:T(8,128)S(1)}, f32[18,16,256]{2,1,0:T(8,128)S(1)}, u32[]{:S(2)}, u32[]{:S(2)}) collective-permute-start(f32[18,16,256]{2,1,0:T(8,128)S(1)} %collective-permute-done.5.refs_6_), channel_id=1, source_target_pairs={{0,1},{1,0},{2,3},{3,2},{4,5},{5,4},{6,7},{7,6},{8,9},{9,8},{10,11... | collective-permute-start | bytes 884744 | tf_op jit(solution)/shard_map/ppermute | solution.py:812
  26.9 1.1 %collective-permute-start.8 = (f32[18,16,256]{2,1,0:T(8,128)S(1)}, f32[18,16,256]{2,1,0:T(8,128)S(1)}, u32[]{:S(2)}, u32[]{:S(2)}) collective-permute-start(f32[18,16,256]{2,1,0:T(8,128)S(1)} %collective-permute-done.7.refs_8_), channel_id=1, source_target_pairs={{0,1},{1,0},{2,3},{3,2},{4,5},{5,4},{6,7},{7,6},{8,9},{9,8},{10,11... | collective-permute-start | bytes 884744 | tf_op jit(solution)/shard_map/ppermute | solution.py:812
  28.5 0.7 collective-permute-done.8.refs_9_
  29.6 6.9 %fine.1 = (f32[16,16,256]{2,1,0:T(8,128)}, f32[2,4,8,256]{3,2,1,0:T(8,128)S(1)}, f32[2,2,8,256]{3,2,1,0:T(8,128)S(1)}, f32[2,2,8,256]{3,2,1,0:T(8,128)S(1)}, f32...) custom-call(f32[58,16,256]{2,1,0:T(8,128)S(1)} %get-tuple-element.69, ...), custom_call_target="tpu_custom_call" | custom-call | tf_op jit(solution)/shard_map/fine/pallas_call | solution.py:822
  36.6 2.8 %collective-permute-start.14 = (f32[2,2,8,256]{3,2,1,0:T(8,128)S(1)}, f32[2,2,8,256]{3,2,1,0:T(8,128)S(1)}, u32[]{:S(2)}, u32[]{:S(2)}) collective-permute-start(f32[2,2,8,256]{3,2,1,0:T(8,128)S(1)} %get-tuple-element.84), channel_id=1, source_target_pairs={{0,14},{2,0},{4,2},{6,4},{8,6},{10,8},{12,10},{14,12},{1,15},{3,1}... | collective-permute-start | bytes 98312 | tf_op jit(solution)/shard_map/ppermute | solution.py:808
  39.3 1.2 %collective-permute-done.13.low = f32[2,2,8,256]{3,2,1,0:T(8,128)S(1)} collective-permute-done((f32[2,2,8,256]{3,2,1,0:T(8,128)S(1)}, f32[2,2,8,256]{3,2,1,0:T(8,128)S(1)}, u32[]{:S(2)}, u32[]{:S(2)}) %collective-permute-start.13) | collective-permute-done | bytes 32800 | tf_op jit(solution)/shard_map/ppermute | solution.py:808
  40.7 4.8 %collective-permute-start.16 = (f32[2,2,16,256]{3,2,1,0:T(8,128)S(1)}, f32[2,2,16,256]{3,2,1,0:T(8,128)S(1)}, u32[]{:S(2)}, u32[]{:S(2)}) collective-permute-start(f32[2,2,16,256]{3,2,1,0:T(8,128)S(1)} %get-tuple-element.87), channel_id=1, source_target_pairs={{0,240},{16,0},{32,16},{48,32},{64,48},{80,64},{96,80},{112,96},{1... | collective-permute-start | bytes 196616 | tf_op jit(solution)/shard_map/ppermute | solution.py:808
  45.6 2.5 %middle_faces.1 = (f32[16,16,256]{2,1,0:T(8,128)}, f32[10,24,256]{2,1,0:T(8,128)S(1)}, f32[10,24,256]{2,1,0:T(8,128)S(1)}, f32[10,24,256]{2,1,0:T(8,128)S(1)}, f...) custom-call(f32[16,16,256]{2,1,0:T(8,128)} %m_in.3, ...), custom_call_target="tpu_custom_call" | custom-call | tf_op jit(solution)/shard_map/middle_faces/pallas_call | solution.py:822
  48.6 12.9 %all_to_all.10.got = f32[8,16,128]{2,1,0:T(8,128)S(1)} all-to-all(f32[8,16,128]{2,1,0:T(8,128)S(1)} %get-tuple-element.98), channel_id=1, replica_groups=mesh['gx'=16,'gy'=8,'gz'=2] {'gy'}, dimensions={0} | all-to-all | bytes 131072 | tf_op jit(solution)/shard_map/all_to_all | solution.py:816
  61.6 16.8 %all_to_all.11 = f32[16,8,16,128]{3,2,1,0:T(8,128)S(1)} all-to-all(f32[16,8,16,128]{3,2,1,0:T(8,128)S(1)} %spread.1), channel_id=1, replica_groups=mesh['gx'=16,'gy'=8,'gz'=2] {'gx'}, dimensions={0} | all-to-all | bytes 2097152 | tf_op jit(solution)/shard_map/all_to_all | solution.py:818
  78.5 6.1 %collective-permute-start.17 = (f32[128,16,128]{2,1,0:T(8,128)S(1)}, f32[128,16,128]{2,1,0:T(8,128)S(1)}, u32[]{:S(2)}, u32[]{:S(2)}) collective-permute-start(f32[128,16,128]{2,1,0:T(8,128)S(1)} %bitcast.1), channel_id=1, source_target_pairs={{0,1},{1,0},{2,3},{3,2},{4,5},{5,4},{6,7},{7,6},{8,9},{9,8},{10,11... | collective-permute-start | bytes 3145736 | tf_op jit(solution)/shard_map/ppermute | solution.py:812
  84.6 2.3 %collective-permute-done.17.refs_1_ = f32[128,16,128]{2,1,0:T(8,128)S(1)} collective-permute-done((f32[128,16,128]{2,1,0:T(8,128)S(1)}, f32[128,16,128]{2,1,0:T(8,128)S(1)}, u32[]{:S(2)}, u32[]{:S(2)}) %collective-permute-start.17) | collective-permute-done | bytes 1048608 | tf_op jit(solution)/shard_map/ppermute | solution.py:812
  86.9 2.7 %coarse.1 = (f32[34,32,128]{2,1,0:T(8,128)S(1)}, f32[34,32,128]{2,1,0:T(8,128)S(1)}, f32[34,32,128]{2,1,0:T(8,128)S(1)}, f32[34,32,128]{2,1,0:T(8,128)S(1)}, f32...) custom-call(f32[128,16,128]{2,1,0:T(8,128)S(1)} %bitcast.2, ...), custom_call_target="tpu_custom_call" | custom-call | tf_op jit(solution)/shard_map/coarse/pallas_call | solution.py:822
  89.6 6.8 %up.1 = f32[16,16,256]{2,1,0:T(8,128)} custom-call(f32[128,16,128]{2,1,0:T(8,128)S(1)} %bitcast.3, f32[128,16,128]{2,1,0:T(8,128)S(1)} %collective-permute-done.17.refs_1_, f32[10,24,256]{2,1,0:T(8,128)S(1)} %get-tuple-element.99.refs_2_, f32[10,24,256]{2,1,0:T(8,128)S(1)} %get-tuple-element.100.refs_3_, f32[10,24,256]{2,1,0:T(8,128)S(1)} %get-tuple-element.101.refs_4_, ...), custom_call_target="tpu_custom_call" | custom-call | tf_op jit(solution)/shard_map/up/pallas_call | solution.py:822
  (24 shorter events, 2.3 us)
Async XLA Ops:
  2.4 27.3 %collective-permute-start = (f32[58,16,256]{2,1,0:T(8,128)S(1)}, f32[58,16,256]{2,1,0:T(8,128)S(1)}, u32[]{:S(2)}, u32[]{:S(2)}) collective-permute-start(f32[58,16,256]{2,1,0:T(8,128)S(1)} %get-tuple-element.69.refs_0_.own), channel_id=1, source_target_pairs={{0,1},{1,0},{2,3},{3,2},{4,5},{5,4},{6,7},{7,6},{8,9},{9,8},{10,11... | collective-permute-start | bytes 2850824 | tf_op jit(solution)/shard_map/ppermute | solution.py:812
  5.6 11.8 %collective-permute-start.1 = (f32[18,16,256]{2,1,0:T(8,128)S(1)}, f32[18,16,256]{2,1,0:T(8,128)S(1)}, u32[]{:S(2)}, u32[]{:S(2)}) collective-permute-start(f32[18,16,256]{2,1,0:T(8,128)S(1)} %get-tuple-element.70), channel_id=1, source_target_pairs={{0,16},{16,32},{32,48},{48,64},{64,80},{80,96},{96,112},{112,128},... | collective-permute-start | bytes 884744 | tf_op jit(solution)/shard_map/ppermute | solution.py:808
  5.6 11.8 %collective-permute-start.3 = (f32[18,16,256]{2,1,0:T(8,128)S(1)}, f32[18,16,256]{2,1,0:T(8,128)S(1)}, u32[]{:S(2)}, u32[]{:S(2)}) collective-permute-start(f32[18,16,256]{2,1,0:T(8,128)S(1)} %get-tuple-element.71), channel_id=1, source_target_pairs={{0,240},{16,0},{32,16},{48,32},{64,48},{80,64},{96,80},{112,96},{1... | collective-permute-start | bytes 884744 | tf_op jit(solution)/shard_map/ppermute | solution.py:808
  10.4 10.9 %collective-permute-start.5 = (f32[18,16,256]{2,1,0:T(8,128)S(1)}, f32[18,16,256]{2,1,0:T(8,128)S(1)}, u32[]{:S(2)}, u32[]{:S(2)}) collective-permute-start(f32[18,16,256]{2,1,0:T(8,128)S(1)} %get-tuple-element.72), channel_id=1, source_target_pairs={{0,2},{2,4},{4,6},{6,8},{8,10},{10,12},{12,14},{14,0},{1,3},{3,5},... | collective-permute-start | bytes 884744 | tf_op jit(solution)/shard_map/ppermute | solution.py:808
  10.5 12.1 %collective-permute-start.7 = (f32[18,16,256]{2,1,0:T(8,128)S(1)}, f32[18,16,256]{2,1,0:T(8,128)S(1)}, u32[]{:S(2)}, u32[]{:S(2)}) collective-permute-start(f32[18,16,256]{2,1,0:T(8,128)S(1)} %get-tuple-element.73), channel_id=1, source_target_pairs={{0,14},{2,0},{4,2},{6,4},{8,6},{10,8},{12,10},{14,12},{1,15},{3,1}... | collective-permute-start | bytes 884744 | tf_op jit(solution)/shard_map/ppermute | solution.py:808
  17.5 8.0 %collective-permute-start.9 = (f32[20,8,256]{2,1,0:T(8,128)S(1)}, f32[20,8,256]{2,1,0:T(8,128)S(1)}, u32[]{:S(2)}, u32[]{:S(2)}) collective-permute-start(f32[20,8,256]{2,1,0:T(8,128)S(1)} %get-tuple-element.74), channel_id=1, source_target_pairs={{0,2},{2,4},{4,6},{6,8},{8,10},{10,12},{12,14},{14,0},{1,3},{3,5},... | collective-permute-start | bytes 491528 | tf_op jit(solution)/shard_map/ppermute | solution.py:808
  17.8 10.2 %collective-permute-start.2 = (f32[18,16,256]{2,1,0:T(8,128)S(1)}, f32[18,16,256]{2,1,0:T(8,128)S(1)}, u32[]{:S(2)}, u32[]{:S(2)}) collective-permute-start(f32[18,16,256]{2,1,0:T(8,128)S(1)} %collective-permute-done.1.xlo.refs_2_), channel_id=1, source_target_pairs={{0,1},{1,0},{2,3},{3,2},{4,5},{5,4},{6,7},{7,6},{8,9},{9,8},{10,11... | collective-permute-start | bytes 884744 | tf_op jit(solution)/shard_map/ppermute | solution.py:812
  21.3 5.5 %collective-permute-start.10 = (f32[20,8,256]{2,1,0:T(8,128)S(1)}, f32[20,8,256]{2,1,0:T(8,128)S(1)}, u32[]{:S(2)}, u32[]{:S(2)}) collective-permute-start(f32[20,8,256]{2,1,0:T(8,128)S(1)} %get-tuple-element.75), channel_id=1, source_target_pairs={{0,14},{2,0},{4,2},{6,4},{8,6},{10,8},{12,10},{14,12},{1,15},{3,1}... | collective-permute-start | bytes 491528 | tf_op jit(solution)/shard_map/ppermute | solution.py:808
  22.6 5.3 %collective-permute-start.4 = (f32[18,16,256]{2,1,0:T(8,128)S(1)}, f32[18,16,256]{2,1,0:T(8,128)S(1)}, u32[]{:S(2)}, u32[]{:S(2)}) collective-permute-start(f32[18,16,256]{2,1,0:T(8,128)S(1)} %collective-permute-done.3.xhi.refs_4_), channel_id=1, source_target_pairs={{0,1},{1,0},{2,3},{3,2},{4,5},{5,4},{6,7},{7,6},{8,9},{9,8},{10,11... | collective-permute-start | bytes 884744 | tf_op jit(solution)/shard_map/ppermute | solution.py:812
  25.5 3.0 %collective-permute-start.6 = (f32[18,16,256]{2,1,0:T(8,128)S(1)}, f32[18,16,256]{2,1,0:T(8,128)S(1)}, u32[]{:S(2)}, u32[]{:S(2)}) collective-permute-start(f32[18,16,256]{2,1,0:T(8,128)S(1)} %collective-permute-done.5.refs_6_), channel_id=1, source_target_pairs={{0,1},{1,0},{2,3},{3,2},{4,5},{5,4},{6,7},{7,6},{8,9},{9,8},{10,11... | collective-permute-start | bytes 884744 | tf_op jit(solution)/shard_map/ppermute | solution.py:812
  26.9 2.3 %collective-permute-start.8 = (f32[18,16,256]{2,1,0:T(8,128)S(1)}, f32[18,16,256]{2,1,0:T(8,128)S(1)}, u32[]{:S(2)}, u32[]{:S(2)}) collective-permute-start(f32[18,16,256]{2,1,0:T(8,128)S(1)} %collective-permute-done.7.refs_8_), channel_id=1, source_target_pairs={{0,1},{1,0},{2,3},{3,2},{4,5},{5,4},{6,7},{7,6},{8,9},{9,8},{10,11... | collective-permute-start | bytes 884744 | tf_op jit(solution)/shard_map/ppermute | solution.py:812
  27.9 1.4 %collective-permute-start.11 = (f32[20,8,256]{2,1,0:T(8,128)S(1)}, f32[20,8,256]{2,1,0:T(8,128)S(1)}, u32[]{:S(2)}, u32[]{:S(2)}) collective-permute-start(f32[20,8,256]{2,1,0:T(8,128)S(1)} %collective-permute-done.9.refs_10_), channel_id=1, source_target_pairs={{0,1},{1,0},{2,3},{3,2},{4,5},{5,4},{6,7},{7,6},{8,9},{9,8},{10,11... | collective-permute-start | bytes 491528 | tf_op jit(solution)/shard_map/ppermute | solution.py:812
  28.0 1.7 %collective-permute-start.12 = (f32[20,8,256]{2,1,0:T(8,128)S(1)}, f32[20,8,256]{2,1,0:T(8,128)S(1)}, u32[]{:S(2)}, u32[]{:S(2)}) collective-permute-start(f32[20,8,256]{2,1,0:T(8,128)S(1)} %collective-permute-done.10.refs_12_), channel_id=1, source_target_pairs={{0,1},{1,0},{2,3},{3,2},{4,5},{5,4},{6,7},{7,6},{8,9},{9,8},{10,11... | collective-permute-start | bytes 491528 | tf_op jit(solution)/shard_map/ppermute | solution.py:812
  36.5 4.1 %collective-permute-start.13 = (f32[2,2,8,256]{3,2,1,0:T(8,128)S(1)}, f32[2,2,8,256]{3,2,1,0:T(8,128)S(1)}, u32[]{:S(2)}, u32[]{:S(2)}) collective-permute-start(f32[2,2,8,256]{3,2,1,0:T(8,128)S(1)} %get-tuple-element.82), channel_id=1, source_target_pairs={{0,2},{2,4},{4,6},{6,8},{8,10},{10,12},{12,14},{14,0},{1,3},{3,5},... | collective-permute-start | bytes 98312 | tf_op jit(solution)/shard_map/ppermute | solution.py:808
  36.6 4.0 %collective-permute-start.14 = (f32[2,2,8,256]{3,2,1,0:T(8,128)S(1)}, f32[2,2,8,256]{3,2,1,0:T(8,128)S(1)}, u32[]{:S(2)}, u32[]{:S(2)}) collective-permute-start(f32[2,2,8,256]{3,2,1,0:T(8,128)S(1)} %get-tuple-element.84), channel_id=1, source_target_pairs={{0,14},{2,0},{4,2},{6,4},{8,6},{10,8},{12,10},{14,12},{1,15},{3,1}... | collective-permute-start | bytes 98312 | tf_op jit(solution)/shard_map/ppermute | solution.py:808
  40.6 7.6 %collective-permute-start.15 = (f32[2,2,16,256]{3,2,1,0:T(8,128)S(1)}, f32[2,2,16,256]{3,2,1,0:T(8,128)S(1)}, u32[]{:S(2)}, u32[]{:S(2)}) collective-permute-start(f32[2,2,16,256]{3,2,1,0:T(8,128)S(1)} %get-tuple-element.85), channel_id=1, source_target_pairs={{0,16},{16,32},{32,48},{48,64},{64,80},{80,96},{96,112},{112,128},... | collective-permute-start | bytes 196616 | tf_op jit(solution)/shard_map/ppermute | solution.py:808
  40.7 7.5 %collective-permute-start.16 = (f32[2,2,16,256]{3,2,1,0:T(8,128)S(1)}, f32[2,2,16,256]{3,2,1,0:T(8,128)S(1)}, u32[]{:S(2)}, u32[]{:S(2)}) collective-permute-start(f32[2,2,16,256]{3,2,1,0:T(8,128)S(1)} %get-tuple-element.87), channel_id=1, source_target_pairs={{0,240},{16,0},{32,16},{48,32},{64,48},{80,64},{96,80},{112,96},{1... | collective-permute-start | bytes 196616 | tf_op jit(solution)/shard_map/ppermute | solution.py:808
  78.5 8.4 %collective-permute-start.17 = (f32[128,16,128]{2,1,0:T(8,128)S(1)}, f32[128,16,128]{2,1,0:T(8,128)S(1)}, u32[]{:S(2)}, u32[]{:S(2)}) collective-permute-start(f32[128,16,128]{2,1,0:T(8,128)S(1)} %bitcast.1), channel_id=1, source_target_pairs={{0,1},{1,0},{2,3},{3,2},{4,5},{5,4},{6,7},{7,6},{8,9},{9,8},{10,11... | collective-permute-start | bytes 3145736 | tf_op jit(solution)/shard_map/ppermute | solution.py:812

commit v5 on v4

--- a/solution.py
+++ b/solution.py
@@ -309,6 +309,7 @@
 def corner_kernel(xlo, xhi, cup, cdn):
     for high, out in ((True, cup), (False, cdn)):
         rows = slice(8, 16) if high else slice(0, 8)
+        edge = iota((8, BZ), 0) == (7 if high else 0)
         for side, src in ((0, xlo), (1, xhi)):
             at = lambda base, depth, d: src[base + (depth - d if side == 0 else d - 1), rows]
             s, n, w = (
@@ -323,19 +324,24 @@
                 merge(high, n(1), n(2)),
                 merge(high, n(3), n(4)),
                 merge(high, w(1), w(2)),
-                merge(high, w(3), u(1)),
-                u(2),
+                merge(high, jnp.where(edge, w(3), pltpu.roll(u(2), 7 if high else 1, 0)), u(1)),
             ]
             for t, tile in enumerate(tiles):
-                out[10 * side + t] = tile
+                out[8 * side + t] = tile
 
             def coarse(d):
                 slab, block_rows, lanes = block_of(5 - d if side == 0 else d - 1)
                 return src[16 + slab, block_rows, lanes]
 
-            for d in range(1, 6):
-                tile, lanes = 10 * side + 7 + (d - 1) // 2, 128 * ((d - 1) % 2)
-                out[tile, :, lanes : lanes + 128] = coarse(d)
+            halves = (
+                coarse(1),
+                merge(high, coarse(2), coarse(3)),
+                merge(high, coarse(4), coarse(5)),
+            )
+            for i, half in enumerate(halves):
+                lanes = 128 * (i % 2)
+                out[8 * side + 6 + i // 2, :, lanes : lanes + 128] = half
+            out[8 * side + 7, :, 128:256] = halves[2]
 
 
 def fine_kernel(*refs):
@@ -406,7 +412,7 @@
                 v[1][H - 1 - j if x_side == 0 else K0 - H + j, mid, dst] = black[j]
             for rows, cref, yflag in ((low, clo, has[2]), (high, chi, has[3])):
                 both = flag * yflag
-                tile = [cref[10 * x_side + t, :, src] * both for t in range(7)]
+                tile = [cref[8 * x_side + t, :, src] * both for t in range(6)]
                 turned = [pltpu.roll(t, 4, 0) for t in tile]
                 zero = jnp.zeros((8, wide), F32)
                 by_field = (
@@ -414,7 +420,8 @@
                     (tile[2], turned[2], tile[3], turned[3]),
                     (tile[4], turned[4], tile[5], zero),
                 )
-                black = (turned[5], tile[6], zero)
+                last = pltpu.roll(tile[5], 1 if cref is clo else 7, 0)
+                black = (turned[5], last, zero)
                 for j in range(H):
                     v[1][H - 1 - j if x_side == 0 else K0 - H + j, rows, dst] = black[j]
                 for q in range(3):
@@ -445,11 +452,12 @@
             mids = [of_x(d) for d in (1, 2, 3, 4, 5)] + [zero]
             columns_of = [(slice(8, 16), mids)]
             for rows, cref, yflag in ((slice(0, 8), clo, has[2]), (slice(16, 24), chi, has[3])):
-                t = [
-                    cref[10 * x_side + 7 + i // 2, :, 128 * (i % 2) : 128 * (i % 2) + 128]
+                h = [
+                    cref[8 * x_side + 6 + i // 2, :, 128 * (i % 2) : 128 * (i % 2) + 128]
                     * (flag * yflag)
-                    for i in range(5)
+                    for i in range(3)
                 ]
+                t = [h[0], h[1], pltpu.roll(h[1], 4, 0), h[2], pltpu.roll(h[2], 4, 0)]
                 columns_of.append((rows, t + [zero]))
             for rows, slabs in columns_of:
                 for j in range(H):
@@ -846,7 +854,7 @@
     )
     xlo, xhi = ring(xup, "gx", 1), ring(xdn, "gx", -1)
     ylo, yhi = ring(yup, "gy", 1), ring(ydn, "gy", -1)
-    cup, cdn = call(corner_kernel, "corner", 4, [(20, 8, BZ)] * 2, [], xlo, xhi)
+    cup, cdn = call(corner_kernel, "corner", 4, [(16, 8, BZ)] * 2, [], xlo, xhi)
     clo, chi = lax.optimization_barrier((ring(cup, "gy", 1), ring(cdn, "gy", -1)))
     halos = []
     for piece in (own, xlo, xhi, ylo, yhi, clo, chi):

time: 96.6 us -> 96.3 us (level)
    ppermute x8, starting transfers between devices: 14.9 us -> 11.9 us  [swap(): return lax.ppermute(x, 'gz', [(0, 1), (1, 0)])]
    ppermute x10, starting transfers between devices: 18.1 us -> 21.1 us  [ring(): return lax.ppermute(x, axis, [(i, (i + step) % n) for i in range(n)])]
    ppermute x10, waiting for transfers between devices: 8.01 us -> 7.03 us  [ring(): return lax.ppermute(x, axis, [(i, (i + step) % n) for i in range(n)])]
  transfers between devices with their start and end apart: 18 -> 18, of which waited for: 8 -> 9; matrix products, arithmetic and copies ran while one was open for 0% -> 0% of each run, Pallas kernels for 3% -> 3%
where the time goes in v5:
time: 96.3 us; the launch traced here: 96.1 us
  starting transfers between devices  33 us (34%)
  blocking collectives  29.8 us (31%)
  Pallas kernels  21.4 us (22%)
  waiting for transfers between devices  11.2 us (12%)
    pallas_call x10, Pallas kernels, call(): pl.pallas_call(kernel, out_shape=tuple((shape(*o) for o in outs)), in_spe...  21.4 us
    ppermute x10, starting transfers between devices, ring(): return lax.ppermute(x, axis, [(i, (i + step) % n) for i in range(n)])  21.1 us
    all_to_all x1, blocking collectives, gather(): lax.all_to_all(send, 'gx', 0, 0, tiled=True)  16.8 us
    all_to_all x1, blocking collectives, gather(): got = lax.all_to_all(send, 'gy', 0, 0, tiled=True)  13 us
    ppermute x8, starting transfers between devices, swap(): return lax.ppermute(x, 'gz', [(0, 1), (1, 0)])  11.9 us
    ppermute x10, waiting for transfers between devices, ring(): return lax.ppermute(x, axis, [(i, (i + step) % n) for i in range(n)])  7.03 us
    ppermute x8, waiting for transfers between devices, swap(): return lax.ppermute(x, 'gz', [(0, 1), (1, 0)])  4.17 us
  transfers between devices with their start and end apart: 18, of which 9 were waited for; matrix products, arithmetic and copies ran while one was open for 0% of the time, Pallas kernels for 3%

profile of v5, /device:TPU:1, one launch (start us, length us, event | category | flops | bytes accessed | tf_op | source)
XLA Modules:
  0.0 96.1 jit_solution(13034595414376604952)
XLA Ops:
  0.6 1.7 %prep.1 = (f32[58,16,256]{2,1,0:T(8,128)S(1)}, f32[18,16,256]{2,1,0:T(8,128)S(1)}, f32[18,16,256]{2,1,0:T(8,128)S(1)}, f32[18,16,256]{2,1,0:T(8,128)S(1)}, f32[18,16,256]{2,1,0:T(8,128)S(1)}) custom-call(f32[16,16,256]{2,1,0:T(8,128)} %m_in.3, f32[16,16,256]{2,1,0:T(8,128)} %r_in.3, f32[16,16,256]{2,1,0:T(8,128)} %u_in.1, f32[16,16,256]{2,1,0:T(8,128)} %f_in.1, ...), custom_call_target="tpu_custom_call" | custom-call | tf_op jit(solution)/shard_map/prep/pallas_call | solution.py:830
  2.4 3.3 %collective-permute-start = (f32[58,16,256]{2,1,0:T(8,128)S(1)}, f32[58,16,256]{2,1,0:T(8,128)S(1)}, u32[]{:S(2)}, u32[]{:S(2)}) collective-permute-start(f32[58,16,256]{2,1,0:T(8,128)S(1)} %get-tuple-element.69.refs_0_.own), channel_id=1, source_target_pairs={{0,1},{1,0},{2,3},{3,2},{4,5},{5,4},{6,7},{7,6},{8,9},{9,8},{10,11... | collective-permute-start | bytes 2850824 | tf_op jit(solution)/shard_map/ppermute | solution.py:820
  5.6 4.8 %collective-permute-start.3 = (f32[18,16,256]{2,1,0:T(8,128)S(1)}, f32[18,16,256]{2,1,0:T(8,128)S(1)}, u32[]{:S(2)}, u32[]{:S(2)}) collective-permute-start(f32[18,16,256]{2,1,0:T(8,128)S(1)} %get-tuple-element.71), channel_id=1, source_target_pairs={{0,240},{16,0},{32,16},{48,32},{64,48},{80,64},{96,80},{112,96},{1... | collective-permute-start | bytes 884744 | tf_op jit(solution)/shard_map/ppermute | solution.py:816
  10.5 3.9 %collective-permute-start.7 = (f32[18,16,256]{2,1,0:T(8,128)S(1)}, f32[18,16,256]{2,1,0:T(8,128)S(1)}, u32[]{:S(2)}, u32[]{:S(2)}) collective-permute-start(f32[18,16,256]{2,1,0:T(8,128)S(1)} %get-tuple-element.73), channel_id=1, source_target_pairs={{0,14},{2,0},{4,2},{6,4},{8,6},{10,8},{12,10},{14,12},{1,15},{3,1}... | collective-permute-start | bytes 884744 | tf_op jit(solution)/shard_map/ppermute | solution.py:816
  14.4 3.0 %collective-permute-done.1.xlo.refs_2_ = f32[18,16,256]{2,1,0:T(8,128)S(1)} collective-permute-done((f32[18,16,256]{2,1,0:T(8,128)S(1)}, f32[18,16,256]{2,1,0:T(8,128)S(1)}, u32[]{:S(2)}, u32[]{:S(2)}) %collective-permute-start.1) | collective-permute-done | bytes 294944 | tf_op jit(solution)/shard_map/ppermute | solution.py:816
  17.8 4.0 %collective-permute-start.10 = (f32[16,8,256]{2,1,0:T(8,128)S(1)}, f32[16,8,256]{2,1,0:T(8,128)S(1)}, u32[]{:S(2)}, u32[]{:S(2)}) collective-permute-start(f32[16,8,256]{2,1,0:T(8,128)S(1)} %get-tuple-element.75), channel_id=1, source_target_pairs={{0,14},{2,0},{4,2},{6,4},{8,6},{10,8},{12,10},{14,12},{1,15},{3,1}... | collective-permute-start | bytes 393224 | tf_op jit(solution)/shard_map/ppermute | solution.py:816
  21.8 3.0 %collective-permute-done.9.refs_10_ = f32[16,8,256]{2,1,0:T(8,128)S(1)} collective-permute-done((f32[16,8,256]{2,1,0:T(8,128)S(1)}, f32[16,8,256]{2,1,0:T(8,128)S(1)}, u32[]{:S(2)}, u32[]{:S(2)}) %collective-permute-start.9) | collective-permute-done | bytes 131104 | tf_op jit(solution)/shard_map/ppermute | solution.py:816
  24.8 1.4 %collective-permute-start.11 = (f32[16,8,256]{2,1,0:T(8,128)S(1)}, f32[16,8,256]{2,1,0:T(8,128)S(1)}, u32[]{:S(2)}, u32[]{:S(2)}) collective-permute-start(f32[16,8,256]{2,1,0:T(8,128)S(1)} %collective-permute-done.9.refs_10_), channel_id=1, source_target_pairs={{0,1},{1,0},{2,3},{3,2},{4,5},{5,4},{6,7},{7,6},{8,9},{9,8},{10,11... | collective-permute-start | bytes 393224 | tf_op jit(solution)/shard_map/ppermute | solution.py:820
  26.2 0.5 collective-permute-start.2
  27.9 0.4 collective-permute-done.4.refs_5_
  28.4 0.4 collective-permute-done.6.refs_7_
  28.8 0.4 collective-permute-done.8.refs_9_
  29.2 6.9 %fine.1 = (f32[16,16,256]{2,1,0:T(8,128)}, f32[2,4,8,256]{3,2,1,0:T(8,128)S(1)}, f32[2,2,8,256]{3,2,1,0:T(8,128)S(1)}, f32[2,2,8,256]{3,2,1,0:T(8,128)S(1)}, f32...) custom-call(f32[58,16,256]{2,1,0:T(8,128)S(1)} %get-tuple-element.69, ...), custom_call_target="tpu_custom_call" | custom-call | tf_op jit(solution)/shard_map/fine/pallas_call | solution.py:830
  36.2 3.0 %collective-permute-start.14 = (f32[2,2,8,256]{3,2,1,0:T(8,128)S(1)}, f32[2,2,8,256]{3,2,1,0:T(8,128)S(1)}, u32[]{:S(2)}, u32[]{:S(2)}) collective-permute-start(f32[2,2,8,256]{3,2,1,0:T(8,128)S(1)} %get-tuple-element.84), channel_id=1, source_target_pairs={{0,14},{2,0},{4,2},{6,4},{8,6},{10,8},{12,10},{14,12},{1,15},{3,1}... | collective-permute-start | bytes 98312 | tf_op jit(solution)/shard_map/ppermute | solution.py:816
  39.2 1.0 %collective-permute-done.13.low = f32[2,2,8,256]{3,2,1,0:T(8,128)S(1)} collective-permute-done((f32[2,2,8,256]{3,2,1,0:T(8,128)S(1)}, f32[2,2,8,256]{3,2,1,0:T(8,128)S(1)}, u32[]{:S(2)}, u32[]{:S(2)}) %collective-permute-start.13) | collective-permute-done | bytes 32800 | tf_op jit(solution)/shard_map/ppermute | solution.py:816
  40.3 4.8 %collective-permute-start.16 = (f32[2,2,16,256]{3,2,1,0:T(8,128)S(1)}, f32[2,2,16,256]{3,2,1,0:T(8,128)S(1)}, u32[]{:S(2)}, u32[]{:S(2)}) collective-permute-start(f32[2,2,16,256]{3,2,1,0:T(8,128)S(1)} %get-tuple-element.87), channel_id=1, source_target_pairs={{0,240},{16,0},{32,16},{48,32},{64,48},{80,64},{96,80},{112,96},{1... | collective-permute-start | bytes 196616 | tf_op jit(solution)/shard_map/ppermute | solution.py:816
  45.3 2.5 %middle_faces.1 = (f32[16,16,256]{2,1,0:T(8,128)}, f32[10,24,256]{2,1,0:T(8,128)S(1)}, f32[10,24,256]{2,1,0:T(8,128)S(1)}, f32[10,24,256]{2,1,0:T(8,128)S(1)}, f...) custom-call(f32[16,16,256]{2,1,0:T(8,128)} %m_in.3, ...), custom_call_target="tpu_custom_call" | custom-call | tf_op jit(solution)/shard_map/middle_faces/pallas_call | solution.py:830
  47.9 0.4 middle.1
  48.3 13.0 %all_to_all.10.got = f32[8,16,128]{2,1,0:T(8,128)S(1)} all-to-all(f32[8,16,128]{2,1,0:T(8,128)S(1)} %get-tuple-element.98), channel_id=1, replica_groups=mesh['gx'=16,'gy'=8,'gz'=2] {'gy'}, dimensions={0} | all-to-all | bytes 131072 | tf_op jit(solution)/shard_map/all_to_all | solution.py:824
  61.4 16.8 %all_to_all.11 = f32[16,8,16,128]{3,2,1,0:T(8,128)S(1)} all-to-all(f32[16,8,16,128]{3,2,1,0:T(8,128)S(1)} %spread.1), channel_id=1, replica_groups=mesh['gx'=16,'gy'=8,'gz'=2] {'gx'}, dimensions={0} | all-to-all | bytes 2097152 | tf_op jit(solution)/shard_map/all_to_all | solution.py:826
  78.2 6.1 %collective-permute-start.17 = (f32[128,16,128]{2,1,0:T(8,128)S(1)}, f32[128,16,128]{2,1,0:T(8,128)S(1)}, u32[]{:S(2)}, u32[]{:S(2)}) collective-permute-start(f32[128,16,128]{2,1,0:T(8,128)S(1)} %bitcast.1), channel_id=1, source_target_pairs={{0,1},{1,0},{2,3},{3,2},{4,5},{5,4},{6,7},{7,6},{8,9},{9,8},{10,11... | collective-permute-start | bytes 3145736 | tf_op jit(solution)/shard_map/ppermute | solution.py:820
  84.3 2.3 %collective-permute-done.17.refs_1_ = f32[128,16,128]{2,1,0:T(8,128)S(1)} collective-permute-done((f32[128,16,128]{2,1,0:T(8,128)S(1)}, f32[128,16,128]{2,1,0:T(8,128)S(1)}, u32[]{:S(2)}, u32[]{:S(2)}) %collective-permute-start.17) | collective-permute-done | bytes 1048608 | tf_op jit(solution)/shard_map/ppermute | solution.py:820
  86.6 2.7 %coarse.1 = (f32[34,32,128]{2,1,0:T(8,128)S(1)}, f32[34,32,128]{2,1,0:T(8,128)S(1)}, f32[34,32,128]{2,1,0:T(8,128)S(1)}, f32[34,32,128]{2,1,0:T(8,128)S(1)}, f32...) custom-call(f32[128,16,128]{2,1,0:T(8,128)S(1)} %bitcast.2, ...), custom_call_target="tpu_custom_call" | custom-call | tf_op jit(solution)/shard_map/coarse/pallas_call | solution.py:830
  89.3 6.8 %up.1 = f32[16,16,256]{2,1,0:T(8,128)} custom-call(f32[128,16,128]{2,1,0:T(8,128)S(1)} %bitcast.3, f32[128,16,128]{2,1,0:T(8,128)S(1)} %collective-permute-done.17.refs_1_, f32[10,24,256]{2,1,0:T(8,128)S(1)} %get-tuple-element.99.refs_2_, f32[10,24,256]{2,1,0:T(8,128)S(1)} %get-tuple-element.100.refs_3_, f32[10,24,256]{2,1,0:T(8,128)S(1)} %get-tuple-element.101.refs_4_, ...), custom_call_target="tpu_custom_call" | custom-call | tf_op jit(solution)/shard_map/up/pallas_call | solution.py:830
  (24 shorter events, 2.2 us)
Async XLA Ops:
  2.4 26.9 %collective-permute-start = (f32[58,16,256]{2,1,0:T(8,128)S(1)}, f32[58,16,256]{2,1,0:T(8,128)S(1)}, u32[]{:S(2)}, u32[]{:S(2)}) collective-permute-start(f32[58,16,256]{2,1,0:T(8,128)S(1)} %get-tuple-element.69.refs_0_.own), channel_id=1, source_target_pairs={{0,1},{1,0},{2,3},{3,2},{4,5},{5,4},{6,7},{7,6},{8,9},{9,8},{10,11... | collective-permute-start | bytes 2850824 | tf_op jit(solution)/shard_map/ppermute | solution.py:820
  5.6 11.8 %collective-permute-start.1 = (f32[18,16,256]{2,1,0:T(8,128)S(1)}, f32[18,16,256]{2,1,0:T(8,128)S(1)}, u32[]{:S(2)}, u32[]{:S(2)}) collective-permute-start(f32[18,16,256]{2,1,0:T(8,128)S(1)} %get-tuple-element.70), channel_id=1, source_target_pairs={{0,16},{16,32},{32,48},{48,64},{64,80},{80,96},{96,112},{112,128},... | collective-permute-start | bytes 884744 | tf_op jit(solution)/shard_map/ppermute | solution.py:816
  5.6 11.8 %collective-permute-start.3 = (f32[18,16,256]{2,1,0:T(8,128)S(1)}, f32[18,16,256]{2,1,0:T(8,128)S(1)}, u32[]{:S(2)}, u32[]{:S(2)}) collective-permute-start(f32[18,16,256]{2,1,0:T(8,128)S(1)} %get-tuple-element.71), channel_id=1, source_target_pairs={{0,240},{16,0},{32,16},{48,32},{64,48},{80,64},{96,80},{112,96},{1... | collective-permute-start | bytes 884744 | tf_op jit(solution)/shard_map/ppermute | solution.py:816
  10.4 15.8 %collective-permute-start.5 = (f32[18,16,256]{2,1,0:T(8,128)S(1)}, f32[18,16,256]{2,1,0:T(8,128)S(1)}, u32[]{:S(2)}, u32[]{:S(2)}) collective-permute-start(f32[18,16,256]{2,1,0:T(8,128)S(1)} %get-tuple-element.72), channel_id=1, source_target_pairs={{0,2},{2,4},{4,6},{6,8},{8,10},{10,12},{12,14},{14,0},{1,3},{3,5},... | collective-permute-start | bytes 884744 | tf_op jit(solution)/shard_map/ppermute | solution.py:816
  10.5 16.2 %collective-permute-start.7 = (f32[18,16,256]{2,1,0:T(8,128)S(1)}, f32[18,16,256]{2,1,0:T(8,128)S(1)}, u32[]{:S(2)}, u32[]{:S(2)}) collective-permute-start(f32[18,16,256]{2,1,0:T(8,128)S(1)} %get-tuple-element.73), channel_id=1, source_target_pairs={{0,14},{2,0},{4,2},{6,4},{8,6},{10,8},{12,10},{14,12},{1,15},{3,1}... | collective-permute-start | bytes 884744 | tf_op jit(solution)/shard_map/ppermute | solution.py:816
  17.5 7.3 %collective-permute-start.9 = (f32[16,8,256]{2,1,0:T(8,128)S(1)}, f32[16,8,256]{2,1,0:T(8,128)S(1)}, u32[]{:S(2)}, u32[]{:S(2)}) collective-permute-start(f32[16,8,256]{2,1,0:T(8,128)S(1)} %get-tuple-element.74), channel_id=1, source_target_pairs={{0,2},{2,4},{4,6},{6,8},{8,10},{10,12},{12,14},{14,0},{1,3},{3,5},... | collective-permute-start | bytes 393224 | tf_op jit(solution)/shard_map/ppermute | solution.py:816
  17.8 7.0 %collective-permute-start.10 = (f32[16,8,256]{2,1,0:T(8,128)S(1)}, f32[16,8,256]{2,1,0:T(8,128)S(1)}, u32[]{:S(2)}, u32[]{:S(2)}) collective-permute-start(f32[16,8,256]{2,1,0:T(8,128)S(1)} %get-tuple-element.75), channel_id=1, source_target_pairs={{0,14},{2,0},{4,2},{6,4},{8,6},{10,8},{12,10},{14,12},{1,15},{3,1}... | collective-permute-start | bytes 393224 | tf_op jit(solution)/shard_map/ppermute | solution.py:816
  24.8 2.4 %collective-permute-start.11 = (f32[16,8,256]{2,1,0:T(8,128)S(1)}, f32[16,8,256]{2,1,0:T(8,128)S(1)}, u32[]{:S(2)}, u32[]{:S(2)}) collective-permute-start(f32[16,8,256]{2,1,0:T(8,128)S(1)} %collective-permute-done.9.refs_10_), channel_id=1, source_target_pairs={{0,1},{1,0},{2,3},{3,2},{4,5},{5,4},{6,7},{7,6},{8,9},{9,8},{10,11... | collective-permute-start | bytes 393224 | tf_op jit(solution)/shard_map/ppermute | solution.py:820
  26.2 1.4 %collective-permute-start.12 = (f32[16,8,256]{2,1,0:T(8,128)S(1)}, f32[16,8,256]{2,1,0:T(8,128)S(1)}, u32[]{:S(2)}, u32[]{:S(2)}) collective-permute-start(f32[16,8,256]{2,1,0:T(8,128)S(1)} %collective-permute-done.10.refs_12_), channel_id=1, source_target_pairs={{0,1},{1,0},{2,3},{3,2},{4,5},{5,4},{6,7},{7,6},{8,9},{9,8},{10,11... | collective-permute-start | bytes 393224 | tf_op jit(solution)/shard_map/ppermute | solution.py:820
  26.2 1.8 %collective-permute-start.2 = (f32[18,16,256]{2,1,0:T(8,128)S(1)}, f32[18,16,256]{2,1,0:T(8,128)S(1)}, u32[]{:S(2)}, u32[]{:S(2)}) collective-permute-start(f32[18,16,256]{2,1,0:T(8,128)S(1)} %collective-permute-done.1.xlo.refs_2_), channel_id=1, source_target_pairs={{0,1},{1,0},{2,3},{3,2},{4,5},{5,4},{6,7},{7,6},{8,9},{9,8},{10,11... | collective-permute-start | bytes 884744 | tf_op jit(solution)/shard_map/ppermute | solution.py:820
  26.7 1.7 %collective-permute-start.4 = (f32[18,16,256]{2,1,0:T(8,128)S(1)}, f32[18,16,256]{2,1,0:T(8,128)S(1)}, u32[]{:S(2)}, u32[]{:S(2)}) collective-permute-start(f32[18,16,256]{2,1,0:T(8,128)S(1)} %collective-permute-done.3.xhi.refs_4_), channel_id=1, source_target_pairs={{0,1},{1,0},{2,3},{3,2},{4,5},{5,4},{6,7},{7,6},{8,9},{9,8},{10,11... | collective-permute-start | bytes 884744 | tf_op jit(solution)/shard_map/ppermute | solution.py:820
  27.2 1.6 %collective-permute-start.6 = (f32[18,16,256]{2,1,0:T(8,128)S(1)}, f32[18,16,256]{2,1,0:T(8,128)S(1)}, u32[]{:S(2)}, u32[]{:S(2)}) collective-permute-start(f32[18,16,256]{2,1,0:T(8,128)S(1)} %collective-permute-done.5.refs_6_), channel_id=1, source_target_pairs={{0,1},{1,0},{2,3},{3,2},{4,5},{5,4},{6,7},{7,6},{8,9},{9,8},{10,11... | collective-permute-start | bytes 884744 | tf_op jit(solution)/shard_map/ppermute | solution.py:820
  27.5 1.7 %collective-permute-start.8 = (f32[18,16,256]{2,1,0:T(8,128)S(1)}, f32[18,16,256]{2,1,0:T(8,128)S(1)}, u32[]{:S(2)}, u32[]{:S(2)}) collective-permute-start(f32[18,16,256]{2,1,0:T(8,128)S(1)} %collective-permute-done.7.refs_8_), channel_id=1, source_target_pairs={{0,1},{1,0},{2,3},{3,2},{4,5},{5,4},{6,7},{7,6},{8,9},{9,8},{10,11... | collective-permute-start | bytes 884744 | tf_op jit(solution)/shard_map/ppermute | solution.py:820
  36.1 4.1 %collective-permute-start.13 = (f32[2,2,8,256]{3,2,1,0:T(8,128)S(1)}, f32[2,2,8,256]{3,2,1,0:T(8,128)S(1)}, u32[]{:S(2)}, u32[]{:S(2)}) collective-permute-start(f32[2,2,8,256]{3,2,1,0:T(8,128)S(1)} %get-tuple-element.82), channel_id=1, source_target_pairs={{0,2},{2,4},{4,6},{6,8},{8,10},{10,12},{12,14},{14,0},{1,3},{3,5},... | collective-permute-start | bytes 98312 | tf_op jit(solution)/shard_map/ppermute | solution.py:816
  36.2 4.0 %collective-permute-start.14 = (f32[2,2,8,256]{3,2,1,0:T(8,128)S(1)}, f32[2,2,8,256]{3,2,1,0:T(8,128)S(1)}, u32[]{:S(2)}, u32[]{:S(2)}) collective-permute-start(f32[2,2,8,256]{3,2,1,0:T(8,128)S(1)} %get-tuple-element.84), channel_id=1, source_target_pairs={{0,14},{2,0},{4,2},{6,4},{8,6},{10,8},{12,10},{14,12},{1,15},{3,1}... | collective-permute-start | bytes 98312 | tf_op jit(solution)/shard_map/ppermute | solution.py:816
  40.2 7.6 %collective-permute-start.15 = (f32[2,2,16,256]{3,2,1,0:T(8,128)S(1)}, f32[2,2,16,256]{3,2,1,0:T(8,128)S(1)}, u32[]{:S(2)}, u32[]{:S(2)}) collective-permute-start(f32[2,2,16,256]{3,2,1,0:T(8,128)S(1)} %get-tuple-element.85), channel_id=1, source_target_pairs={{0,16},{16,32},{32,48},{48,64},{64,80},{80,96},{96,112},{112,128},... | collective-permute-start | bytes 196616 | tf_op jit(solution)/shard_map/ppermute | solution.py:816
  40.3 7.5 %collective-permute-start.16 = (f32[2,2,16,256]{3,2,1,0:T(8,128)S(1)}, f32[2,2,16,256]{3,2,1,0:T(8,128)S(1)}, u32[]{:S(2)}, u32[]{:S(2)}) collective-permute-start(f32[2,2,16,256]{3,2,1,0:T(8,128)S(1)} %get-tuple-element.87), channel_id=1, source_target_pairs={{0,240},{16,0},{32,16},{48,32},{64,48},{80,64},{96,80},{112,96},{1... | collective-permute-start | bytes 196616 | tf_op jit(solution)/shard_map/ppermute | solution.py:816
  78.2 8.4 %collective-permute-start.17 = (f32[128,16,128]{2,1,0:T(8,128)S(1)}, f32[128,16,128]{2,1,0:T(8,128)S(1)}, u32[]{:S(2)}, u32[]{:S(2)}) collective-permute-start(f32[128,16,128]{2,1,0:T(8,128)S(1)} %bitcast.1), channel_id=1, source_target_pairs={{0,1},{1,0},{2,3},{3,2},{4,5},{5,4},{6,7},{7,6},{8,9},{9,8},{10,11... | collective-permute-start | bytes 3145736 | tf_op jit(solution)/shard_map/ppermute | solution.py:820

commit v6 on v5

--- a/solution.py
+++ b/solution.py
@@ -727,7 +727,7 @@
     n2, y2 = 2 * nx, 4 * ny
     n3, y3 = nx, 2 * ny
     v2, b2, v3, b3 = refs[0:2], refs[2:4], refs[4:6], refs[6:8]
-    fold2, fold1, fold0 = refs[8], refs[9], refs[10]
+    fold2, fold1, fold0, result, sems = refs[8:]
     gx_me, gy_me, core = where_am_i()
     unpack(got, got_z, 0, b2, nx, ny)
     step2 = min(S22, n2)
@@ -791,16 +791,21 @@
 
     loop(0, BX // 2 + 2, 1, body)
     half_sweep(v0, b0, 0, coef0, inv0, H - 1, K0 - H + 1, SHB)
-    half_sweep(v0, b0, 1, coef0, inv0, H, K0 - H, SH)
     lanes = pl.ds(pl.multiple_of(core * 128, 128), BZ)
     half_first = first_is_red((BY, BZ))
 
-    def body(p):
-        a, c = v0[0][p + H, 8:24, lanes], v0[1][p + H, 8:24, lanes]
-        out[2 * p] = jnp.where(half_first, a, c)
-        out[2 * p + 1] = jnp.where(half_first, c, a)
-
-    loop(0, BX // 2, 1, body)
+    copies = []
+    for i, start in enumerate(range(0, BX // 2, SH)):
+        half_sweep(v0, b0, 1, coef0, inv0, H + start, H + start + SH, SH)
+        for p in range(start, start + SH):
+            a, c = v0[0][p + H, 8:24, lanes], v0[1][p + H, 8:24, lanes]
+            result[2 * p] = jnp.where(half_first, a, c)
+            result[2 * p + 1] = jnp.where(half_first, c, a)
+        part = pl.ds(2 * start, 2 * SH)
+        copies.append(pltpu.make_async_copy(result.at[part], out.at[part], sems.at[i]))
+        copies[-1].start()
+    for copy in copies:
+        copy.wait()
 
 
 def shape(*dims):
@@ -900,8 +905,9 @@
         lambda *refs: up_kernel(*refs, nx=nx, ny=ny), "up", 10,
         [block],
         [grid2] * 4 + [grid3] * 4
-        + [(8 * nx * ny, Z2), (2, max(4 * nx * ny, 256), Z2), (3, 320, 128)],
-        got, got_z, *level1, *level0, *coarse,
+        + [(8 * nx * ny, Z2), (2, max(4 * nx * ny, 256), Z2), (3, 320, 128)]
+        + [block, pltpu.SemaphoreType.DMA((2,))],
+        got, got_z, *level1, *level0, *coarse, hbm_out=1,
     )
     return mnext, rnext, enext
 

time: 96.3 us -> 96.4 us (level)
  no operation moved by 1% of the time
where the time goes in v6:
time: 96.4 us; the launch traced here: 96.2 us
  starting transfers between devices  33 us (34%)
  blocking collectives  29.8 us (31%)
  Pallas kernels  21.3 us (22%)
  waiting for transfers between devices  11.2 us (12%)
    pallas_call x10, Pallas kernels, call(): pl.pallas_call(kernel, out_shape=tuple((shape(*o) for o in outs)), in_spe...  21.3 us
    ppermute x10, starting transfers between devices, ring(): return lax.ppermute(x, axis, [(i, (i + step) % n) for i in range(n)])  21.1 us
    all_to_all x1, blocking collectives, gather(): lax.all_to_all(send, 'gx', 0, 0, tiled=True)  16.8 us
    all_to_all x1, blocking collectives, gather(): got = lax.all_to_all(send, 'gy', 0, 0, tiled=True)  13 us
    ppermute x8, starting transfers between devices, swap(): return lax.ppermute(x, 'gz', [(0, 1), (1, 0)])  11.9 us
    ppermute x10, waiting for transfers between devices, ring(): return lax.ppermute(x, axis, [(i, (i + step) % n) for i in range(n)])  7.03 us
    ppermute x8, waiting for transfers between devices, swap(): return lax.ppermute(x, 'gz', [(0, 1), (1, 0)])  4.17 us
  transfers between devices with their start and end apart: 18, of which 9 were waited for; matrix products, arithmetic and copies ran while one was open for 0% of the time, Pallas kernels for 3%

profile of v6, /device:TPU:1, one launch (start us, length us, event | category | flops | bytes accessed | tf_op | source)
XLA Modules:
  0.0 96.2 jit_solution(8582621383183385218)
XLA Ops:
  0.6 1.7 %prep.1 = (f32[58,16,256]{2,1,0:T(8,128)S(1)}, f32[18,16,256]{2,1,0:T(8,128)S(1)}, f32[18,16,256]{2,1,0:T(8,128)S(1)}, f32[18,16,256]{2,1,0:T(8,128)S(1)}, f32[18,16,256]{2,1,0:T(8,128)S(1)}) custom-call(f32[16,16,256]{2,1,0:T(8,128)} %m_in.3, f32[16,16,256]{2,1,0:T(8,128)} %r_in.3, f32[16,16,256]{2,1,0:T(8,128)} %u_in.1, f32[16,16,256]{2,1,0:T(8,128)} %f_in.1, ...), custom_call_target="tpu_custom_call" | custom-call | tf_op jit(solution)/shard_map/prep/pallas_call | solution.py:835
  2.4 3.3 %collective-permute-start = (f32[58,16,256]{2,1,0:T(8,128)S(1)}, f32[58,16,256]{2,1,0:T(8,128)S(1)}, u32[]{:S(2)}, u32[]{:S(2)}) collective-permute-start(f32[58,16,256]{2,1,0:T(8,128)S(1)} %get-tuple-element.69.refs_0_.own), channel_id=1, source_target_pairs={{0,1},{1,0},{2,3},{3,2},{4,5},{5,4},{6,7},{7,6},{8,9},{9,8},{10,11... | collective-permute-start | bytes 2850824 | tf_op jit(solution)/shard_map/ppermute | solution.py:825
  5.6 4.8 %collective-permute-start.3 = (f32[18,16,256]{2,1,0:T(8,128)S(1)}, f32[18,16,256]{2,1,0:T(8,128)S(1)}, u32[]{:S(2)}, u32[]{:S(2)}) collective-permute-start(f32[18,16,256]{2,1,0:T(8,128)S(1)} %get-tuple-element.71), channel_id=1, source_target_pairs={{0,240},{16,0},{32,16},{48,32},{64,48},{80,64},{96,80},{112,96},{1... | collective-permute-start | bytes 884744 | tf_op jit(solution)/shard_map/ppermute | solution.py:821
  10.5 3.9 %collective-permute-start.7 = (f32[18,16,256]{2,1,0:T(8,128)S(1)}, f32[18,16,256]{2,1,0:T(8,128)S(1)}, u32[]{:S(2)}, u32[]{:S(2)}) collective-permute-start(f32[18,16,256]{2,1,0:T(8,128)S(1)} %get-tuple-element.73), channel_id=1, source_target_pairs={{0,14},{2,0},{4,2},{6,4},{8,6},{10,8},{12,10},{14,12},{1,15},{3,1}... | collective-permute-start | bytes 884744 | tf_op jit(solution)/shard_map/ppermute | solution.py:821
  14.4 3.0 %collective-permute-done.1.xlo.refs_2_ = f32[18,16,256]{2,1,0:T(8,128)S(1)} collective-permute-done((f32[18,16,256]{2,1,0:T(8,128)S(1)}, f32[18,16,256]{2,1,0:T(8,128)S(1)}, u32[]{:S(2)}, u32[]{:S(2)}) %collective-permute-start.1) | collective-permute-done | bytes 294944 | tf_op jit(solution)/shard_map/ppermute | solution.py:821
  17.8 4.0 %collective-permute-start.10 = (f32[16,8,256]{2,1,0:T(8,128)S(1)}, f32[16,8,256]{2,1,0:T(8,128)S(1)}, u32[]{:S(2)}, u32[]{:S(2)}) collective-permute-start(f32[16,8,256]{2,1,0:T(8,128)S(1)} %get-tuple-element.75), channel_id=1, source_target_pairs={{0,14},{2,0},{4,2},{6,4},{8,6},{10,8},{12,10},{14,12},{1,15},{3,1}... | collective-permute-start | bytes 393224 | tf_op jit(solution)/shard_map/ppermute | solution.py:821
  21.8 3.0 %collective-permute-done.9.refs_10_ = f32[16,8,256]{2,1,0:T(8,128)S(1)} collective-permute-done((f32[16,8,256]{2,1,0:T(8,128)S(1)}, f32[16,8,256]{2,1,0:T(8,128)S(1)}, u32[]{:S(2)}, u32[]{:S(2)}) %collective-permute-start.9) | collective-permute-done | bytes 131104 | tf_op jit(solution)/shard_map/ppermute | solution.py:821
  24.8 1.4 %collective-permute-start.11 = (f32[16,8,256]{2,1,0:T(8,128)S(1)}, f32[16,8,256]{2,1,0:T(8,128)S(1)}, u32[]{:S(2)}, u32[]{:S(2)}) collective-permute-start(f32[16,8,256]{2,1,0:T(8,128)S(1)} %collective-permute-done.9.refs_10_), channel_id=1, source_target_pairs={{0,1},{1,0},{2,3},{3,2},{4,5},{5,4},{6,7},{7,6},{8,9},{9,8},{10,11... | collective-permute-start | bytes 393224 | tf_op jit(solution)/shard_map/ppermute | solution.py:825
  26.2 0.5 collective-permute-start.2
  27.9 0.4 collective-permute-done.4.refs_5_
  28.4 0.4 collective-permute-done.6.refs_7_
  28.8 0.4 collective-permute-done.8.refs_9_
  29.2 6.9 %fine.1 = (f32[16,16,256]{2,1,0:T(8,128)}, f32[2,4,8,256]{3,2,1,0:T(8,128)S(1)}, f32[2,2,8,256]{3,2,1,0:T(8,128)S(1)}, f32[2,2,8,256]{3,2,1,0:T(8,128)S(1)}, f32...) custom-call(f32[58,16,256]{2,1,0:T(8,128)S(1)} %get-tuple-element.69, ...), custom_call_target="tpu_custom_call" | custom-call | tf_op jit(solution)/shard_map/fine/pallas_call | solution.py:835
  36.2 3.0 %collective-permute-start.14 = (f32[2,2,8,256]{3,2,1,0:T(8,128)S(1)}, f32[2,2,8,256]{3,2,1,0:T(8,128)S(1)}, u32[]{:S(2)}, u32[]{:S(2)}) collective-permute-start(f32[2,2,8,256]{3,2,1,0:T(8,128)S(1)} %get-tuple-element.84), channel_id=1, source_target_pairs={{0,14},{2,0},{4,2},{6,4},{8,6},{10,8},{12,10},{14,12},{1,15},{3,1}... | collective-permute-start | bytes 98312 | tf_op jit(solution)/shard_map/ppermute | solution.py:821
  39.2 1.0 %collective-permute-done.13.low = f32[2,2,8,256]{3,2,1,0:T(8,128)S(1)} collective-permute-done((f32[2,2,8,256]{3,2,1,0:T(8,128)S(1)}, f32[2,2,8,256]{3,2,1,0:T(8,128)S(1)}, u32[]{:S(2)}, u32[]{:S(2)}) %collective-permute-start.13) | collective-permute-done | bytes 32800 | tf_op jit(solution)/shard_map/ppermute | solution.py:821
  40.3 4.8 %collective-permute-start.16 = (f32[2,2,16,256]{3,2,1,0:T(8,128)S(1)}, f32[2,2,16,256]{3,2,1,0:T(8,128)S(1)}, u32[]{:S(2)}, u32[]{:S(2)}) collective-permute-start(f32[2,2,16,256]{3,2,1,0:T(8,128)S(1)} %get-tuple-element.87), channel_id=1, source_target_pairs={{0,240},{16,0},{32,16},{48,32},{64,48},{80,64},{96,80},{112,96},{1... | collective-permute-start | bytes 196616 | tf_op jit(solution)/shard_map/ppermute | solution.py:821
  45.3 2.5 %middle_faces.1 = (f32[16,16,256]{2,1,0:T(8,128)}, f32[10,24,256]{2,1,0:T(8,128)S(1)}, f32[10,24,256]{2,1,0:T(8,128)S(1)}, f32[10,24,256]{2,1,0:T(8,128)S(1)}, f...) custom-call(f32[16,16,256]{2,1,0:T(8,128)} %m_in.3, ...), custom_call_target="tpu_custom_call" | custom-call | tf_op jit(solution)/shard_map/middle_faces/pallas_call | solution.py:835
  47.9 0.4 middle.1
  48.3 13.0 %all_to_all.10.got = f32[8,16,128]{2,1,0:T(8,128)S(1)} all-to-all(f32[8,16,128]{2,1,0:T(8,128)S(1)} %get-tuple-element.98), channel_id=1, replica_groups=mesh['gx'=16,'gy'=8,'gz'=2] {'gy'}, dimensions={0} | all-to-all | bytes 131072 | tf_op jit(solution)/shard_map/all_to_all | solution.py:829
  61.4 16.8 %all_to_all.11 = f32[16,8,16,128]{3,2,1,0:T(8,128)S(1)} all-to-all(f32[16,8,16,128]{3,2,1,0:T(8,128)S(1)} %spread.1), channel_id=1, replica_groups=mesh['gx'=16,'gy'=8,'gz'=2] {'gx'}, dimensions={0} | all-to-all | bytes 2097152 | tf_op jit(solution)/shard_map/all_to_all | solution.py:831
  78.2 6.1 %collective-permute-start.17 = (f32[128,16,128]{2,1,0:T(8,128)S(1)}, f32[128,16,128]{2,1,0:T(8,128)S(1)}, u32[]{:S(2)}, u32[]{:S(2)}) collective-permute-start(f32[128,16,128]{2,1,0:T(8,128)S(1)} %bitcast.1), channel_id=1, source_target_pairs={{0,1},{1,0},{2,3},{3,2},{4,5},{5,4},{6,7},{7,6},{8,9},{9,8},{10,11... | collective-permute-start | bytes 3145736 | tf_op jit(solution)/shard_map/ppermute | solution.py:825
  84.3 2.3 %collective-permute-done.17.refs_1_ = f32[128,16,128]{2,1,0:T(8,128)S(1)} collective-permute-done((f32[128,16,128]{2,1,0:T(8,128)S(1)}, f32[128,16,128]{2,1,0:T(8,128)S(1)}, u32[]{:S(2)}, u32[]{:S(2)}) %collective-permute-start.17) | collective-permute-done | bytes 1048608 | tf_op jit(solution)/shard_map/ppermute | solution.py:825
  86.6 2.7 %coarse.1 = (f32[34,32,128]{2,1,0:T(8,128)S(1)}, f32[34,32,128]{2,1,0:T(8,128)S(1)}, f32[34,32,128]{2,1,0:T(8,128)S(1)}, f32[34,32,128]{2,1,0:T(8,128)S(1)}, f32...) custom-call(f32[128,16,128]{2,1,0:T(8,128)S(1)} %bitcast.2, ...), custom_call_target="tpu_custom_call" | custom-call | tf_op jit(solution)/shard_map/coarse/pallas_call | solution.py:835
  89.3 6.8 %up.1 = f32[16,16,256]{2,1,0:T(8,128)} custom-call(f32[128,16,128]{2,1,0:T(8,128)S(1)} %bitcast.3, f32[128,16,128]{2,1,0:T(8,128)S(1)} %collective-permute-done.17.refs_1_, f32[10,24,256]{2,1,0:T(8,128)S(1)} %get-tuple-element.99.refs_2_, f32[10,24,256]{2,1,0:T(8,128)S(1)} %get-tuple-element.100.refs_3_, f32[10,24,256]{2,1,0:T(8,128)S(1)} %get-tuple-element.101.refs_4_, ...), custom_call_target="tpu_custom_call" | custom-call | tf_op jit(solution)/shard_map/up/pallas_call | solution.py:835
  (24 shorter events, 2.2 us)
Async XLA Ops:
  2.4 26.9 %collective-permute-start = (f32[58,16,256]{2,1,0:T(8,128)S(1)}, f32[58,16,256]{2,1,0:T(8,128)S(1)}, u32[]{:S(2)}, u32[]{:S(2)}) collective-permute-start(f32[58,16,256]{2,1,0:T(8,128)S(1)} %get-tuple-element.69.refs_0_.own), channel_id=1, source_target_pairs={{0,1},{1,0},{2,3},{3,2},{4,5},{5,4},{6,7},{7,6},{8,9},{9,8},{10,11... | collective-permute-start | bytes 2850824 | tf_op jit(solution)/shard_map/ppermute | solution.py:825
  5.6 11.8 %collective-permute-start.1 = (f32[18,16,256]{2,1,0:T(8,128)S(1)}, f32[18,16,256]{2,1,0:T(8,128)S(1)}, u32[]{:S(2)}, u32[]{:S(2)}) collective-permute-start(f32[18,16,256]{2,1,0:T(8,128)S(1)} %get-tuple-element.70), channel_id=1, source_target_pairs={{0,16},{16,32},{32,48},{48,64},{64,80},{80,96},{96,112},{112,128},... | collective-permute-start | bytes 884744 | tf_op jit(solution)/shard_map/ppermute | solution.py:821
  5.6 11.8 %collective-permute-start.3 = (f32[18,16,256]{2,1,0:T(8,128)S(1)}, f32[18,16,256]{2,1,0:T(8,128)S(1)}, u32[]{:S(2)}, u32[]{:S(2)}) collective-permute-start(f32[18,16,256]{2,1,0:T(8,128)S(1)} %get-tuple-element.71), channel_id=1, source_target_pairs={{0,240},{16,0},{32,16},{48,32},{64,48},{80,64},{96,80},{112,96},{1... | collective-permute-start | bytes 884744 | tf_op jit(solution)/shard_map/ppermute | solution.py:821
  10.4 15.8 %collective-permute-start.5 = (f32[18,16,256]{2,1,0:T(8,128)S(1)}, f32[18,16,256]{2,1,0:T(8,128)S(1)}, u32[]{:S(2)}, u32[]{:S(2)}) collective-permute-start(f32[18,16,256]{2,1,0:T(8,128)S(1)} %get-tuple-element.72), channel_id=1, source_target_pairs={{0,2},{2,4},{4,6},{6,8},{8,10},{10,12},{12,14},{14,0},{1,3},{3,5},... | collective-permute-start | bytes 884744 | tf_op jit(solution)/shard_map/ppermute | solution.py:821
  10.5 16.2 %collective-permute-start.7 = (f32[18,16,256]{2,1,0:T(8,128)S(1)}, f32[18,16,256]{2,1,0:T(8,128)S(1)}, u32[]{:S(2)}, u32[]{:S(2)}) collective-permute-start(f32[18,16,256]{2,1,0:T(8,128)S(1)} %get-tuple-element.73), channel_id=1, source_target_pairs={{0,14},{2,0},{4,2},{6,4},{8,6},{10,8},{12,10},{14,12},{1,15},{3,1}... | collective-permute-start | bytes 884744 | tf_op jit(solution)/shard_map/ppermute | solution.py:821
  17.5 7.3 %collective-permute-start.9 = (f32[16,8,256]{2,1,0:T(8,128)S(1)}, f32[16,8,256]{2,1,0:T(8,128)S(1)}, u32[]{:S(2)}, u32[]{:S(2)}) collective-permute-start(f32[16,8,256]{2,1,0:T(8,128)S(1)} %get-tuple-element.74), channel_id=1, source_target_pairs={{0,2},{2,4},{4,6},{6,8},{8,10},{10,12},{12,14},{14,0},{1,3},{3,5},... | collective-permute-start | bytes 393224 | tf_op jit(solution)/shard_map/ppermute | solution.py:821
  17.8 7.0 %collective-permute-start.10 = (f32[16,8,256]{2,1,0:T(8,128)S(1)}, f32[16,8,256]{2,1,0:T(8,128)S(1)}, u32[]{:S(2)}, u32[]{:S(2)}) collective-permute-start(f32[16,8,256]{2,1,0:T(8,128)S(1)} %get-tuple-element.75), channel_id=1, source_target_pairs={{0,14},{2,0},{4,2},{6,4},{8,6},{10,8},{12,10},{14,12},{1,15},{3,1}... | collective-permute-start | bytes 393224 | tf_op jit(solution)/shard_map/ppermute | solution.py:821
  24.8 2.4 %collective-permute-start.11 = (f32[16,8,256]{2,1,0:T(8,128)S(1)}, f32[16,8,256]{2,1,0:T(8,128)S(1)}, u32[]{:S(2)}, u32[]{:S(2)}) collective-permute-start(f32[16,8,256]{2,1,0:T(8,128)S(1)} %collective-permute-done.9.refs_10_), channel_id=1, source_target_pairs={{0,1},{1,0},{2,3},{3,2},{4,5},{5,4},{6,7},{7,6},{8,9},{9,8},{10,11... | collective-permute-start | bytes 393224 | tf_op jit(solution)/shard_map/ppermute | solution.py:825
  26.2 1.4 %collective-permute-start.12 = (f32[16,8,256]{2,1,0:T(8,128)S(1)}, f32[16,8,256]{2,1,0:T(8,128)S(1)}, u32[]{:S(2)}, u32[]{:S(2)}) collective-permute-start(f32[16,8,256]{2,1,0:T(8,128)S(1)} %collective-permute-done.10.refs_12_), channel_id=1, source_target_pairs={{0,1},{1,0},{2,3},{3,2},{4,5},{5,4},{6,7},{7,6},{8,9},{9,8},{10,11... | collective-permute-start | bytes 393224 | tf_op jit(solution)/shard_map/ppermute | solution.py:825
  26.2 1.8 %collective-permute-start.2 = (f32[18,16,256]{2,1,0:T(8,128)S(1)}, f32[18,16,256]{2,1,0:T(8,128)S(1)}, u32[]{:S(2)}, u32[]{:S(2)}) collective-permute-start(f32[18,16,256]{2,1,0:T(8,128)S(1)} %collective-permute-done.1.xlo.refs_2_), channel_id=1, source_target_pairs={{0,1},{1,0},{2,3},{3,2},{4,5},{5,4},{6,7},{7,6},{8,9},{9,8},{10,11... | collective-permute-start | bytes 884744 | tf_op jit(solution)/shard_map/ppermute | solution.py:825
  26.7 1.7 %collective-permute-start.4 = (f32[18,16,256]{2,1,0:T(8,128)S(1)}, f32[18,16,256]{2,1,0:T(8,128)S(1)}, u32[]{:S(2)}, u32[]{:S(2)}) collective-permute-start(f32[18,16,256]{2,1,0:T(8,128)S(1)} %collective-permute-done.3.xhi.refs_4_), channel_id=1, source_target_pairs={{0,1},{1,0},{2,3},{3,2},{4,5},{5,4},{6,7},{7,6},{8,9},{9,8},{10,11... | collective-permute-start | bytes 884744 | tf_op jit(solution)/shard_map/ppermute | solution.py:825
  27.2 1.6 %collective-permute-start.6 = (f32[18,16,256]{2,1,0:T(8,128)S(1)}, f32[18,16,256]{2,1,0:T(8,128)S(1)}, u32[]{:S(2)}, u32[]{:S(2)}) collective-permute-start(f32[18,16,256]{2,1,0:T(8,128)S(1)} %collective-permute-done.5.refs_6_), channel_id=1, source_target_pairs={{0,1},{1,0},{2,3},{3,2},{4,5},{5,4},{6,7},{7,6},{8,9},{9,8},{10,11... | collective-permute-start | bytes 884744 | tf_op jit(solution)/shard_map/ppermute | solution.py:825
  27.5 1.7 %collective-permute-start.8 = (f32[18,16,256]{2,1,0:T(8,128)S(1)}, f32[18,16,256]{2,1,0:T(8,128)S(1)}, u32[]{:S(2)}, u32[]{:S(2)}) collective-permute-start(f32[18,16,256]{2,1,0:T(8,128)S(1)} %collective-permute-done.7.refs_8_), channel_id=1, source_target_pairs={{0,1},{1,0},{2,3},{3,2},{4,5},{5,4},{6,7},{7,6},{8,9},{9,8},{10,11... | collective-permute-start | bytes 884744 | tf_op jit(solution)/shard_map/ppermute | solution.py:825
  36.1 4.1 %collective-permute-start.13 = (f32[2,2,8,256]{3,2,1,0:T(8,128)S(1)}, f32[2,2,8,256]{3,2,1,0:T(8,128)S(1)}, u32[]{:S(2)}, u32[]{:S(2)}) collective-permute-start(f32[2,2,8,256]{3,2,1,0:T(8,128)S(1)} %get-tuple-element.82), channel_id=1, source_target_pairs={{0,2},{2,4},{4,6},{6,8},{8,10},{10,12},{12,14},{14,0},{1,3},{3,5},... | collective-permute-start | bytes 98312 | tf_op jit(solution)/shard_map/ppermute | solution.py:821
  36.2 4.0 %collective-permute-start.14 = (f32[2,2,8,256]{3,2,1,0:T(8,128)S(1)}, f32[2,2,8,256]{3,2,1,0:T(8,128)S(1)}, u32[]{:S(2)}, u32[]{:S(2)}) collective-permute-start(f32[2,2,8,256]{3,2,1,0:T(8,128)S(1)} %get-tuple-element.84), channel_id=1, source_target_pairs={{0,14},{2,0},{4,2},{6,4},{8,6},{10,8},{12,10},{14,12},{1,15},{3,1}... | collective-permute-start | bytes 98312 | tf_op jit(solution)/shard_map/ppermute | solution.py:821
  40.2 7.6 %collective-permute-start.15 = (f32[2,2,16,256]{3,2,1,0:T(8,128)S(1)}, f32[2,2,16,256]{3,2,1,0:T(8,128)S(1)}, u32[]{:S(2)}, u32[]{:S(2)}) collective-permute-start(f32[2,2,16,256]{3,2,1,0:T(8,128)S(1)} %get-tuple-element.85), channel_id=1, source_target_pairs={{0,16},{16,32},{32,48},{48,64},{64,80},{80,96},{96,112},{112,128},... | collective-permute-start | bytes 196616 | tf_op jit(solution)/shard_map/ppermute | solution.py:821
  40.3 7.5 %collective-permute-start.16 = (f32[2,2,16,256]{3,2,1,0:T(8,128)S(1)}, f32[2,2,16,256]{3,2,1,0:T(8,128)S(1)}, u32[]{:S(2)}, u32[]{:S(2)}) collective-permute-start(f32[2,2,16,256]{3,2,1,0:T(8,128)S(1)} %get-tuple-element.87), channel_id=1, source_target_pairs={{0,240},{16,0},{32,16},{48,32},{64,48},{80,64},{96,80},{112,96},{1... | collective-permute-start | bytes 196616 | tf_op jit(solution)/shard_map/ppermute | solution.py:821
  78.2 8.4 %collective-permute-start.17 = (f32[128,16,128]{2,1,0:T(8,128)S(1)}, f32[128,16,128]{2,1,0:T(8,128)S(1)}, u32[]{:S(2)}, u32[]{:S(2)}) collective-permute-start(f32[128,16,128]{2,1,0:T(8,128)S(1)} %bitcast.1), channel_id=1, source_target_pairs={{0,1},{1,0},{2,3},{3,2},{4,5},{5,4},{6,7},{7,6},{8,9},{9,8},{10,11... | collective-permute-start | bytes 3145736 | tf_op jit(solution)/shard_map/ppermute | solution.py:825
